TPU v7x, 512 devices: a 8x2x16 block of a 8x8x16 slice. The times are simulated.
512 devices in a mesh: group: 2 (over y), plane: 16 (over z), planey: 8 (over x), ens: 2 (over core).
Axes of the slice: x: 8, y: 2, z: 16, core: 2. Of those that a mesh axis runs over, the one named last changes fastest.
The devices are a block of a 8x8x16 slice.
Arguments:
- u_prior: float32 [8, 2, 10, 256, 1024], P(('group', 'ens'), None, None, 'plane', 'planey'), parts along dimension 0, may hold values from -6 to 6
- friction_rows: int32 [8], P(('group', 'ens')), parts along dimension 0, may hold values from 0 to 15
- friction_table: float32 [32, 256, 1024], P('group', 'plane', 'planey'), parts along dimension 0, may hold values from 0.3 to 3
- bed_fixed: int32 [256, 1024], P('plane', 'planey'), may hold values from -536870912 to 536870911
- ice_mask: int32 [256, 1024], P('plane', 'planey'), may hold values 0 or 1
Outputs:
- mean_velocity: float32 [4, 10, 256, 1024], P('group', None, 'plane', 'planey'), parts along dimension 0
There are 2 independent parts, one for each index of `group`. A program takes and returns all parts, laid end to end along the dimension named above; an argument that names none is the same for every part. Nothing has to cross between parts.
Inputs may be any that keep to these rules, and one draw needn't show every extreme that they name: `friction_rows`: each sample names one row of the friction table.
All inputs are finite; a program needn't handle non-finite values. No bound on the sum of `ice_mask` on one device may be relied on, other than what follows from the above.
Results may differ from a plain program's by a relative error of at most 0.0003.
Values sent between devices are 32-bit elements; how exact they have to be, the bound alone decides.
No kernel may reach another device: no remote copies, remote signals or barrier semaphores. Data moves between devices by JAX's collectives and lax.ppermute only.
A program may use at most 64 MiB of HBM per device.

v0:
```python
import jax
import jax.numpy as jnp
from jax import lax
from jax.sharding import PartitionSpec as P

bed_unit = 2.0 ** (-29)
factor_u = (2.0, 1.0, 0.5)
factor_v = (2.0, 0.5, 1.0)


def extended_2(cells, sides, width):
    for axis, dim in sides:
        count = lax.axis_size(axis)
        ends = count - 1
        head = lax.slice_in_dim(cells, 0, width, axis=dim)
        tail = lax.slice_in_dim(cells, cells.shape[dim] - width, cells.shape[dim], axis=dim)
        cells = jnp.concatenate(
            [
                lax.ppermute(tail, axis, [(i, (i + 1) % count) for i in range(ends)]),
                cells,
                lax.ppermute(head, axis, [((i + 1) % count, i) for i in range(ends)]),
            ],
            axis=dim,
        )
    return cells


def one_axis_at_a_time(value, axes):
    for axis in axes:
        value = lax.psum(value, axis)
    return value


def total_of_pieces(value, axis):
    blocks = lax.all_gather(value, axis)
    return blocks.sum(axis=0)


def coefficient(offset):
    nonzero = len([entry for entry in offset if entry != 0])
    weight_u = 0.25 ** (nonzero - 1)
    weight_v = weight_u
    for dimension in range(3):
        if offset[dimension] != 0:
            weight_u = weight_u * factor_u[dimension]
            weight_v = weight_v * factor_v[dimension]
    return jnp.array([weight_u, weight_v], jnp.float32).reshape(2, 1, 1, 1)


def neighbour_sum(padded):
    layers = padded.shape[-3] - 2
    span_x = padded.shape[-2] - 2
    span_y = padded.shape[-1] - 2
    summed = None
    for step_z in (-1, 0, 1):
        for step_x in (-1, 0, 1):
            for step_y in (-1, 0, 1):
                if step_z == 0 and step_x == 0 and (step_y == 0):
                    continue
                window = padded[
                    ...,
                    1 + step_z : 1 + step_z + layers,
                    1 + step_x : 1 + step_x + span_x,
                    1 + step_y : 1 + step_y + span_y,
                ]
                addend = coefficient((step_z, step_x, step_y)) * window
                summed = addend if summed is None else summed + addend
    return summed


def strain_roots(extended):
    padded = jnp.pad(extended, [(0, 0)] * (extended.ndim - 3) + [(1, 1), (0, 0), (0, 0)])
    along_x = (padded[..., 1:-1, 2:, 1:-1] - padded[..., 1:-1, :-2, 1:-1]) * 0.5
    along_y = (padded[..., 1:-1, 1:-1, 2:] - padded[..., 1:-1, 1:-1, :-2]) * 0.5
    along_z = (padded[..., 2:, 1:-1, 1:-1] - padded[..., :-2, 1:-1, 1:-1]) * 0.5
    stretch_x = along_x[..., 0, :, :, :]
    stretch_y = along_y[..., 1, :, :, :]
    shear_one = along_y[..., 0, :, :, :]
    shear_two = along_x[..., 1, :, :, :]
    vertical_u = along_z[..., 0, :, :, :]
    vertical_v = along_z[..., 1, :, :, :]
    shear = shear_one + shear_two
    strain = (
        stretch_x * stretch_x
        + stretch_y * stretch_y
        + stretch_x * stretch_y
        + 0.25 * shear * shear
        + 0.25 * (vertical_u * vertical_u + vertical_v * vertical_v)
    )
    return jnp.power(strain + 0.1, -1.0 / 6.0)[..., None, :, :, :]


def pad_layers(field):
    return jnp.pad(field, ((0, 0), (0, 0), (1, 1), (0, 0), (0, 0)))


def inner(left, right):
    return jnp.sum(left * right, axis=(1, 2, 3, 4))


def spread(values):
    return values.reshape(-1, 1, 1, 1, 1)


def trimmed(field, margin):
    return field[..., margin:-margin, margin:-margin]


def apply_local(roots_wide, across_part, diag_part, field_wide):
    product = roots_wide * field_wide
    nearby = neighbour_sum(pad_layers(product))
    centre = trimmed(field_wide, 1)
    return trimmed(roots_wide, 1) * (across_part * centre - nearby) + diag_part * centre


def body(u_prior, friction_rows, friction_table, bed_fixed, ice_mask):
    members = u_prior.shape[0]
    layers = u_prior.shape[2]
    rows_x = u_prior.shape[3]
    rows_y = u_prior.shape[4]
    total_x = rows_x * lax.axis_size("plane")
    cover = ice_mask.astype(jnp.float32)
    bed_block = (bed_fixed.astype(jnp.float32) * bed_unit).reshape(1, 1, 1, rows_x, rows_y)
    levels = jnp.arange(friction_table.shape[0], dtype=jnp.int32)
    chosen = (friction_rows[:, None] == levels[None, :]).astype(jnp.float32)
    friction = jnp.sum(chosen[:, :, None, None] * friction_table[None], axis=1)
    bottom = (
        (jnp.arange(layers, dtype=jnp.int32) == 0).astype(jnp.float32).reshape(1, 1, layers, 1, 1)
    )
    mask_block = cover.reshape(1, 1, 1, rows_x, rows_y)
    friction_block = friction.reshape(members, 1, 1, rows_x, rows_y)
    prior_wide, bed_wide, mask_wide, friction_wide = (
        extended_2(u_prior, (("plane", 3), ("planey", 4)), 4),
        extended_2(bed_block, (("plane", 3), ("planey", 4)), 4),
        extended_2(mask_block, (("plane", 3), ("planey", 4)), 4),
        extended_2(friction_block, (("plane", 3), ("planey", 4)), 4),
    )
    roots_three = trimmed(mask_wide, 1) * strain_roots(prior_wide)
    across_two = neighbour_sum(pad_layers(roots_three))
    bed_three = trimmed(bed_wide, 1)
    slope_x = (bed_three[..., 2:, 1:-1] - bed_three[..., :-2, 1:-1]) * 0.5
    slope_y = (bed_three[..., 1:-1, 2:] - bed_three[..., 1:-1, :-2]) * 0.5
    mask_two = trimmed(mask_wide, 2)
    position = (
        lax.axis_index("plane") * rows_x - 2 + jnp.arange(rows_x + 4, dtype=jnp.int32)
    ).astype(jnp.float32)
    thickness = 1.0 + 2.0 * position[:, None] / (total_x - 1)
    force_two = jnp.concatenate(
        [-(mask_two * thickness * slope_x), -(mask_two * thickness * slope_y)], axis=1
    )
    diag_two = mask_two * trimmed(friction_wide, 2) * bottom + (1.0 - mask_two)
    start_three = trimmed(prior_wide, 1) * trimmed(mask_wide, 1)
    residual_two = force_two - apply_local(roots_three, across_two, diag_two, start_three)
    image_one = apply_local(
        trimmed(roots_three, 1), trimmed(across_two, 1), trimmed(diag_two, 1), residual_two
    )
    second_image = apply_local(
        trimmed(roots_three, 2), trimmed(across_two, 2), trimmed(diag_two, 2), image_one
    )
    residual = trimmed(residual_two, 2)
    image = trimmed(image_one, 1)
    gram_rr, gram_ra, gram_aa, gram_ab = (
        one_axis_at_a_time(inner(residual, residual), ("plane", "planey")),
        one_axis_at_a_time(inner(residual, image), ("plane", "planey")),
        one_axis_at_a_time(inner(image, image), ("plane", "planey")),
        one_axis_at_a_time(inner(image, second_image), ("plane", "planey")),
    )
    first_step = gram_rr / gram_ra
    norm_next = gram_rr - 2.0 * first_step * gram_ra + first_step * first_step * gram_aa
    growth = 1.0 + norm_next / gram_rr
    curve = (
        growth * growth * gram_ra
        - 2.0 * growth * first_step * gram_aa
        + first_step * first_step * gram_ab
    )
    second_step = norm_next / curve
    solution = trimmed(start_three, 3)
    solution = (
        solution
        + spread(first_step + second_step * growth) * residual
        - spread(second_step * first_step) * image
    )
    local_sum = jnp.sum(solution, axis=0)
    summed = total_of_pieces(local_sum, "ens")
    return summed / (members * lax.axis_size("ens"))


def solution(mesh):
    in_specs = (
        P(("group", "ens"), None, None, "plane", "planey"),
        P(("group", "ens")),
        P("group", "plane", "planey"),
        P("plane", "planey"),
        P("plane", "planey"),
    )
    out_specs = P("group", None, "plane", "planey")
    return jax.shard_map(body, mesh=mesh, in_specs=in_specs, out_specs=out_specs, check_vma=False)
```

profile of v0, /device:TPU:65, one launch (start us, length us, event | category | flops | bytes accessed | tf_op | source)
XLA Modules:
  0.0 188.2 jit_solution(14085209569929018749)
XLA Ops:
  0.0 0.7 convert_bitcast_fusion
  0.7 6.6 %collective-permute-start.4 = (f32[1,1,1,4,128]{4,3,2,1,0:T(4,128)S(1)}, f32[1,1,1,4,128]{4,3,2,1,0:T(4,128)S(1)}, u32[]{:S(2)}, u32[]{:S(2)}) collective-permute-start(f32[1,1,1,4,128]{4,3,2,1,0:T(4,128)S(1)} %get-tuple-element.76), channel_id=1, source_target_pairs={{0,16},{16,32},{32,48},{48,64},{64,80},{80,96},{96,112},{112,128},... | collective-permute-start | bytes 6152 | tf_op jit(solution)/shard_map/ppermute | solution.py:19
  7.3 1.3 collective-permute-start.5
  8.6 0.7 multiply_bitcast_fusion
  9.3 6.4 %collective-permute-start.8 = (f32[1,1,1,4,128]{4,3,2,1,0:T(4,128)S(1)}, f32[1,1,1,4,128]{4,3,2,1,0:T(4,128)S(1)}, u32[]{:S(2)}, u32[]{:S(2)}) collective-permute-start(f32[1,1,1,4,128]{4,3,2,1,0:T(4,128)S(1)} %get-tuple-element.74), channel_id=1, source_target_pairs={{0,16},{16,32},{32,48},{48,64},{64,80},{80,96},{96,112},{112,128},... | collective-permute-start | bytes 6152 | tf_op jit(solution)/shard_map/ppermute | solution.py:19
  15.7 1.3 collective-permute-start.9
  17.0 0.7 compare_convert_fusion.1
  17.7 1.0 multiply_reduce_fusion.3
  18.7 6.4 %collective-permute-start.12 = (f32[2,1,1,4,128]{4,3,0,2,1:T(4,128)S(1)}, f32[2,1,1,4,128]{4,3,0,2,1:T(4,128)S(1)}, u32[]{:S(2)}, u32[]{:S(2)}) collective-permute-start(f32[2,1,1,4,128]{4,3,0,2,1:T(4,128)S(1)} %get-tuple-element.68), channel_id=1, source_target_pairs={{0,16},{16,32},{32,48},{48,64},{64,80},{80,96},{96,112},{112,128},... | collective-permute-start | bytes 12296 | tf_op jit(solution)/shard_map/ppermute | solution.py:19
  25.2 1.0 fusion.197
  26.2 0.0 collective-permute-done.4
  26.2 1.3 collective-permute-start.13
  27.5 7.6 %collective-permute-start = (f32[2,2,10,4,128]{4,3,2,1,0:T(4,128)S(1)}, f32[2,2,10,4,128]{4,3,2,1,0:T(4,128)S(1)}, u32[]{:S(2)}, u32[]{:S(2)}) collective-permute-start(f32[2,2,10,4,128]{4,3,2,1,0:T(4,128)S(1)} %get-tuple-element.60), channel_id=1, source_target_pairs={{0,16},{16,32},{32,48},{48,64},{64,80},{80,96},{96,112},{112,128},... | collective-permute-start | bytes 245768 | tf_op jit(solution)/shard_map/ppermute | solution.py:19
  35.2 0.1 fusion.201
  35.3 3.3 %collective-permute-start.6 = (f32[1,1,1,24,4]{4,3,2,1,0:T(8,128)S(1)}, f32[1,1,1,24,4]{4,3,2,1,0:T(8,128)S(1)}, u32[]{:S(2)}, u32[]{:S(2)}) collective-permute-start(f32[1,1,1,24,4]{4,3,2,1,0:T(8,128)S(1)} %get-tuple-element.72), channel_id=1, source_target_pairs={{0,2},{2,4},{4,6},{6,8},{8,10},{10,12},{12,14},{1,3},{3,5},{5,7},{... | collective-permute-start | bytes 1160 | tf_op jit(solution)/shard_map/ppermute | solution.py:19
  38.5 1.3 collective-permute-start.7
  39.9 0.1 fusion.200
  40.0 4.0 %collective-permute-start.10 = (f32[1,1,1,24,4]{4,3,2,1,0:T(8,128)S(1)}, f32[1,1,1,24,4]{4,3,2,1,0:T(8,128)S(1)}, u32[]{:S(2)}, u32[]{:S(2)}) collective-permute-start(f32[1,1,1,24,4]{4,3,2,1,0:T(8,128)S(1)} %get-tuple-element.70), channel_id=1, source_target_pairs={{0,2},{2,4},{4,6},{6,8},{8,10},{10,12},{12,14},{1,3},{3,5},{5,7},{... | collective-permute-start | bytes 1160 | tf_op jit(solution)/shard_map/ppermute | solution.py:19
  44.0 1.3 collective-permute-start.11
  45.3 0.1 pad_maximum_fusion.6
  45.4 0.0 collective-permute-done.10
  45.4 1.3 collective-permute-start.1
  46.7 1.8 collective-permute-done.11
  48.6 0.1 pad_maximum_fusion.7
  48.6 0.1 fusion.193
  48.8 0.1 slice_bitcast_fusion.9
  48.9 0.1 fusion.198
  48.9 4.2 %collective-permute-start.14 = (f32[2,1,1,24,4]{4,3,0,2,1:T(8,128)S(1)}, f32[2,1,1,24,4]{4,3,0,2,1:T(8,128)S(1)}, u32[]{:S(2)}, u32[]{:S(2)}) collective-permute-start(f32[2,1,1,24,4]{4,3,0,2,1:T(8,128)S(1)} %get-tuple-element.66), channel_id=1, source_target_pairs={{0,2},{2,4},{4,6},{6,8},{8,10},{10,12},{12,14},{1,3},{3,5},{5,7},{... | collective-permute-start | bytes 2312 | tf_op jit(solution)/shard_map/ppermute | solution.py:19
  53.1 1.3 collective-permute-start.15
  54.5 4.5 %collective-permute-done.15 = f32[2,1,1,24,4]{4,3,0,2,1:T(8,128)S(1)} collective-permute-done((f32[2,1,1,24,4]{4,3,0,2,1:T(8,128)S(1)}, f32[2,1,1,24,4]{4,3,0,2,1:T(8,128)S(1)}, u32[]{:S(2)}, u32[]{:S(2)}) %collective-permute-start.15) | collective-permute-done | bytes 800 | tf_op jit(solution)/shard_map/ppermute | solution.py:21
  58.9 0.1 fusion.187
  59.1 0.0 copy-start
  59.1 0.1 multiply_add_fusion
  59.2 0.2 slice_bitcast_fusion
  59.4 0.1 multiply_add_fusion.1
  59.5 0.5 copy-done
  60.0 0.1 pad_maximum_fusion.1
  60.1 0.2 fusion.196
  60.3 4.6 %collective-permute-start.2 = (f32[2,2,10,24,4]{4,3,2,1,0:T(8,128)S(1)}, f32[2,2,10,24,4]{4,3,2,1,0:T(8,128)S(1)}, u32[]{:S(2)}, u32[]{:S(2)}) collective-permute-start(f32[2,2,10,24,4]{4,3,2,1,0:T(8,128)S(1)} %get-tuple-element.58), channel_id=1, source_target_pairs={{0,2},{2,4},{4,6},{6,8},{8,10},{10,12},{12,14},{1,3},{3,5},{5,7},{... | collective-permute-start | bytes 46088 | tf_op jit(solution)/shard_map/ppermute | solution.py:19
  64.9 1.5 collective-permute-start.3
  66.4 0.1 slice_bitcast_fusion.7
  66.5 4.2 %collective-permute-done.2 = f32[2,2,10,24,4]{4,3,2,1,0:T(8,128)S(1)} collective-permute-done((f32[2,2,10,24,4]{4,3,2,1,0:T(8,128)S(1)}, f32[2,2,10,24,4]{4,3,2,1,0:T(8,128)S(1)}, u32[]{:S(2)}, u32[]{:S(2)}) %collective-permute-start.2) | collective-permute-done | bytes 15392 | tf_op jit(solution)/shard_map/ppermute | solution.py:19
  70.8 3.9 %collective-permute-done.3 = f32[2,2,10,24,4]{4,3,2,1,0:T(8,128)S(1)} collective-permute-done((f32[2,2,10,24,4]{4,3,2,1,0:T(8,128)S(1)}, f32[2,2,10,24,4]{4,3,2,1,0:T(8,128)S(1)}, u32[]{:S(2)}, u32[]{:S(2)}) %collective-permute-start.3) | collective-permute-done | bytes 15392 | tf_op jit(solution)/shard_map/ppermute | solution.py:21
  74.7 0.6 pad_maximum_fusion
  75.3 1.3 fusion.95
  76.6 0.5 fusion.101
  77.1 5.0 %fusion.103 = (f32[2,10,20,132]{3,2,1,0:T(8,128)S(1)}, f32[2,10,20,132]{3,2,1,0:T(8,128)}, f32[2,10,20,132]{3,2,1,0:T(8,128)}, f32[2,10,20,132]{3,2,1,0:T(8,128)...) fusion(f32[2,1,10,22,134]{4,3,2,1,0:T(8,128)S(1)} %fusion.101), kind=kLoop, calls=%fused_computation.200 | loop fusion | flops 580800 | bytes 4995840 | tf_op jit(solution)/shard_map/mul | solution.py:66
  82.1 2.6 %fusion.133 = (f32[2,10,20,132]{3,2,1,0:T(8,128)}, f32[2,10,20,132]{3,2,1,0:T(8,128)}, f32[2,10,20,132]{3,2,1,0:T(8,128)}, f32[2,10,20,132]{3,2,1,0:T(8,128)}, f...) fusion(f32[2,1,10,22,134]{4,3,2,1,0:T(8,128)S(1)} %fusion.101), kind=kLoop, calls=%fused_computation.240 | loop fusion | flops 158400 | bytes 3379200 | tf_op jit(solution)/shard_map/mul | solution.py:66
  84.7 1.0 slice_bitcast_fusion.1
  85.7 0.8 slice_bitcast_fusion.8
  86.5 0.3 broadcast_multiply_fusion.1
  86.9 0.3 copy-done.2
  87.2 0.0 copy-done.3
  87.2 0.0 copy-done.4
  87.2 0.0 copy-done.5
  87.2 8.9 %broadcast_multiply_fusion.2 = (f32[2,2,10,20,132]{4,3,2,1,0:T(8,128)S(1)}, f32[2,2,10,20,132]{4,3,2,1,0:T(8,128)S(1)}, f32[2,2,10,20,132]{4,3,2,1,0:T(8,128)S(1)}) fusion(f32[2,10,20,132]{3,2,1,0:T(8,128)} %get-tuple-element.57, f32[2,10,20,132]{3,2,1,0:T(8,128)S(1)} %multiply_add_fusion.1, f32[2,2,10,22,134]{4,3,2,1,0:T(8,128)S(1)} %get-tuple-element.25, ...), kind=kLoop, calls=%fused_computation.252 | loop fusion | flops 10032000 | bytes 17623040 | tf_op jit(solution)/shard_map/mul | solution.py:110
  96.1 0.0 copy-start.1
  96.1 5.9 %broadcast_multiply_fusion = (f32[2,2,10,18,130]{4,3,2,1,0:T(8,128)S(1)}, f32[2,2,10,18,130]{4,3,2,1,0:T(8,128)S(1)}) fusion(f32[2,10,18,130]{3,2,1,0:T(8,128)} %slice_bitcast_fusion.1, f32[2,10,18,130]{3,2,1,0:T(8,128)S(1)} %slice_bitcast_fusion, f32[2,2,10,20,132]{4,3,2,1,0:T(8,128)S(1)} %get-tuple-element.22, f32[2]{0:T(128)S(1)} %copy-done.5, ...), kind=kLoop, calls=%fused_computation.249 | loop fusion | flops 5335200 | bytes 12243008 | tf_op jit(solution)/shard_map/mul | solution.py:110
  102.0 1.8 multiply_reduce_fusion.1
  103.8 51.0 %all-reduce.5 = (f32[2]{0:T(128)S(1)}, f32[2]{0:T(128)S(1)}, f32[2]{0:T(128)S(1)}, f32[2]{0:T(128)S(1)}) all-reduce(f32[2]{0:T(128)S(1)} %get-tuple-element.27, f32[2]{0:T(128)S(1)} %get-tuple-element.6, f32[2]{0:T(128)S(1)} %get-tuple-element.7, ...), channel_id=1, replica_groups=mesh['group'=2,'plane'=16,'planey'=8,'ens'=2] {'plane'}, use_global_device_ids=true, to_apply=%region_11.12 | all-reduce | flops 8 | bytes 64 | tf_op jit(solution)/shard_map/psum | solution.py:30
  154.8 13.3 %all-reduce.6 = (f32[2]{0:T(128)S(1)}, f32[2]{0:T(128)S(1)}, f32[2]{0:T(128)S(1)}, f32[2]{0:T(128)S(1)}) all-reduce(f32[2]{0:T(128)S(1)} %get-tuple-element.8, f32[2]{0:T(128)S(1)} %get-tuple-element.9, f32[2]{0:T(128)S(1)} %get-tuple-element.10, ...), channel_id=1, replica_groups=mesh['group'=2,'plane'=16,'planey'=8,'ens'=2] {'planey'}, use_global_device_ids=true, to_apply=%region_12.13 | all-reduce | flops 8 | bytes 64 | tf_op jit(solution)/shard_map/psum | solution.py:30
  168.2 0.3 fusion.184
  168.5 19.0 %all-gather = f32[4,10,16,128]{3,2,1,0:T(8,128)S(1)} all-gather(f32[2,10,16,128]{3,2,1,0:T(8,128)S(1)} %fusion.184), channel_id=2, replica_groups=mesh['group'=2,'plane'=16,'planey'=8,'ens'=2] {'ens'}, dimensions={0}, use_global_device_ids=true | all-gather | bytes 491520 | tf_op jit(solution)/shard_map/all_gather | solution.py:35
  187.5 0.7 broadcast_multiply_fusion.3
  (28 shorter events, 0.2 us)
Async XLA Ops:
  0.7 25.5 %collective-permute-start.4 = (f32[1,1,1,4,128]{4,3,2,1,0:T(4,128)S(1)}, f32[1,1,1,4,128]{4,3,2,1,0:T(4,128)S(1)}, u32[]{:S(2)}, u32[]{:S(2)}) collective-permute-start(f32[1,1,1,4,128]{4,3,2,1,0:T(4,128)S(1)} %get-tuple-element.76), channel_id=1, source_target_pairs={{0,16},{16,32},{32,48},{48,64},{64,80},{80,96},{96,112},{112,128},... | collective-permute-start | bytes 6152 | tf_op jit(solution)/shard_map/ppermute | solution.py:19
  7.3 20.3 %collective-permute-start.5 = (f32[1,1,1,4,128]{4,3,2,1,0:T(4,128)S(1)}, f32[1,1,1,4,128]{4,3,2,1,0:T(4,128)S(1)}, u32[]{:S(2)}, u32[]{:S(2)}) collective-permute-start(f32[1,1,1,4,128]{4,3,2,1,0:T(4,128)S(1)} %get-tuple-element.77), channel_id=1, source_target_pairs={{16,0},{32,16},{48,32},{64,48},{80,64},{96,80},{112,96},{128,112},... | collective-permute-start | bytes 6152 | tf_op jit(solution)/shard_map/ppermute | solution.py:21
  9.3 26.0 %collective-permute-start.8 = (f32[1,1,1,4,128]{4,3,2,1,0:T(4,128)S(1)}, f32[1,1,1,4,128]{4,3,2,1,0:T(4,128)S(1)}, u32[]{:S(2)}, u32[]{:S(2)}) collective-permute-start(f32[1,1,1,4,128]{4,3,2,1,0:T(4,128)S(1)} %get-tuple-element.74), channel_id=1, source_target_pairs={{0,16},{16,32},{32,48},{48,64},{64,80},{80,96},{96,112},{112,128},... | collective-permute-start | bytes 6152 | tf_op jit(solution)/shard_map/ppermute | solution.py:19
  15.7 22.9 %collective-permute-start.9 = (f32[1,1,1,4,128]{4,3,2,1,0:T(4,128)S(1)}, f32[1,1,1,4,128]{4,3,2,1,0:T(4,128)S(1)}, u32[]{:S(2)}, u32[]{:S(2)}) collective-permute-start(f32[1,1,1,4,128]{4,3,2,1,0:T(4,128)S(1)} %get-tuple-element.75), channel_id=1, source_target_pairs={{16,0},{32,16},{48,32},{64,48},{80,64},{96,80},{112,96},{128,112},... | collective-permute-start | bytes 6152 | tf_op jit(solution)/shard_map/ppermute | solution.py:21
  18.7 30.1 %collective-permute-start.12 = (f32[2,1,1,4,128]{4,3,0,2,1:T(4,128)S(1)}, f32[2,1,1,4,128]{4,3,0,2,1:T(4,128)S(1)}, u32[]{:S(2)}, u32[]{:S(2)}) collective-permute-start(f32[2,1,1,4,128]{4,3,0,2,1:T(4,128)S(1)} %get-tuple-element.68), channel_id=1, source_target_pairs={{0,16},{16,32},{32,48},{48,64},{64,80},{80,96},{96,112},{112,128},... | collective-permute-start | bytes 12296 | tf_op jit(solution)/shard_map/ppermute | solution.py:19
  26.2 22.6 %collective-permute-start.13 = (f32[2,1,1,4,128]{4,3,0,2,1:T(4,128)S(1)}, f32[2,1,1,4,128]{4,3,0,2,1:T(4,128)S(1)}, u32[]{:S(2)}, u32[]{:S(2)}) collective-permute-start(f32[2,1,1,4,128]{4,3,0,2,1:T(4,128)S(1)} %get-tuple-element.69), channel_id=1, source_target_pairs={{16,0},{32,16},{48,32},{64,48},{80,64},{96,80},{112,96},{128,112},... | collective-permute-start | bytes 12296 | tf_op jit(solution)/shard_map/ppermute | solution.py:21
  27.5 32.0 %collective-permute-start = (f32[2,2,10,4,128]{4,3,2,1,0:T(4,128)S(1)}, f32[2,2,10,4,128]{4,3,2,1,0:T(4,128)S(1)}, u32[]{:S(2)}, u32[]{:S(2)}) collective-permute-start(f32[2,2,10,4,128]{4,3,2,1,0:T(4,128)S(1)} %get-tuple-element.60), channel_id=1, source_target_pairs={{0,16},{16,32},{32,48},{48,64},{64,80},{80,96},{96,112},{112,128},... | collective-permute-start | bytes 245768 | tf_op jit(solution)/shard_map/ppermute | solution.py:19
  35.3 4.7 %collective-permute-start.6 = (f32[1,1,1,24,4]{4,3,2,1,0:T(8,128)S(1)}, f32[1,1,1,24,4]{4,3,2,1,0:T(8,128)S(1)}, u32[]{:S(2)}, u32[]{:S(2)}) collective-permute-start(f32[1,1,1,24,4]{4,3,2,1,0:T(8,128)S(1)} %get-tuple-element.72), channel_id=1, source_target_pairs={{0,2},{2,4},{4,6},{6,8},{8,10},{10,12},{12,14},{1,3},{3,5},{5,7},{... | collective-permute-start | bytes 1160 | tf_op jit(solution)/shard_map/ppermute | solution.py:19
  38.5 5.4 %collective-permute-start.7 = (f32[1,1,1,24,4]{4,3,2,1,0:T(8,128)S(1)}, f32[1,1,1,24,4]{4,3,2,1,0:T(8,128)S(1)}, u32[]{:S(2)}, u32[]{:S(2)}) collective-permute-start(f32[1,1,1,24,4]{4,3,2,1,0:T(8,128)S(1)} %get-tuple-element.73), channel_id=1, source_target_pairs={{2,0},{4,2},{6,4},{8,6},{10,8},{12,10},{14,12},{3,1},{5,3},{7,5},{... | collective-permute-start | bytes 1160 | tf_op jit(solution)/shard_map/ppermute | solution.py:21
  40.0 5.4 %collective-permute-start.10 = (f32[1,1,1,24,4]{4,3,2,1,0:T(8,128)S(1)}, f32[1,1,1,24,4]{4,3,2,1,0:T(8,128)S(1)}, u32[]{:S(2)}, u32[]{:S(2)}) collective-permute-start(f32[1,1,1,24,4]{4,3,2,1,0:T(8,128)S(1)} %get-tuple-element.70), channel_id=1, source_target_pairs={{0,2},{2,4},{4,6},{6,8},{8,10},{10,12},{12,14},{1,3},{3,5},{5,7},{... | collective-permute-start | bytes 1160 | tf_op jit(solution)/shard_map/ppermute | solution.py:19
  44.0 4.6 %collective-permute-start.11 = (f32[1,1,1,24,4]{4,3,2,1,0:T(8,128)S(1)}, f32[1,1,1,24,4]{4,3,2,1,0:T(8,128)S(1)}, u32[]{:S(2)}, u32[]{:S(2)}) collective-permute-start(f32[1,1,1,24,4]{4,3,2,1,0:T(8,128)S(1)} %get-tuple-element.71), channel_id=1, source_target_pairs={{2,0},{4,2},{6,4},{8,6},{10,8},{12,10},{14,12},{3,1},{5,3},{7,5},{... | collective-permute-start | bytes 1160 | tf_op jit(solution)/shard_map/ppermute | solution.py:21
  45.4 14.1 %collective-permute-start.1 = (f32[2,2,10,4,128]{4,3,2,1,0:T(4,128)S(1)}, f32[2,2,10,4,128]{4,3,2,1,0:T(4,128)S(1)}, u32[]{:S(2)}, u32[]{:S(2)}) collective-permute-start(f32[2,2,10,4,128]{4,3,2,1,0:T(4,128)S(1)} %get-tuple-element.61), channel_id=1, source_target_pairs={{16,0},{32,16},{48,32},{64,48},{80,64},{96,80},{112,96},{128,112},... | collective-permute-start | bytes 245768 | tf_op jit(solution)/shard_map/ppermute | solution.py:21
  48.9 5.5 %collective-permute-start.14 = (f32[2,1,1,24,4]{4,3,0,2,1:T(8,128)S(1)}, f32[2,1,1,24,4]{4,3,0,2,1:T(8,128)S(1)}, u32[]{:S(2)}, u32[]{:S(2)}) collective-permute-start(f32[2,1,1,24,4]{4,3,0,2,1:T(8,128)S(1)} %get-tuple-element.66), channel_id=1, source_target_pairs={{0,2},{2,4},{4,6},{6,8},{8,10},{10,12},{12,14},{1,3},{3,5},{5,7},{... | collective-permute-start | bytes 2312 | tf_op jit(solution)/shard_map/ppermute | solution.py:19
  53.1 5.8 %collective-permute-start.15 = (f32[2,1,1,24,4]{4,3,0,2,1:T(8,128)S(1)}, f32[2,1,1,24,4]{4,3,0,2,1:T(8,128)S(1)}, u32[]{:S(2)}, u32[]{:S(2)}) collective-permute-start(f32[2,1,1,24,4]{4,3,0,2,1:T(8,128)S(1)} %get-tuple-element.67), channel_id=1, source_target_pairs={{2,0},{4,2},{6,4},{8,6},{10,8},{12,10},{14,12},{3,1},{5,3},{7,5},{... | collective-permute-start | bytes 2312 | tf_op jit(solution)/shard_map/ppermute | solution.py:21
  59.1 1.0 copy-start
  60.3 10.5 %collective-permute-start.2 = (f32[2,2,10,24,4]{4,3,2,1,0:T(8,128)S(1)}, f32[2,2,10,24,4]{4,3,2,1,0:T(8,128)S(1)}, u32[]{:S(2)}, u32[]{:S(2)}) collective-permute-start(f32[2,2,10,24,4]{4,3,2,1,0:T(8,128)S(1)} %get-tuple-element.58), channel_id=1, source_target_pairs={{0,2},{2,4},{4,6},{6,8},{8,10},{10,12},{12,14},{1,3},{3,5},{5,7},{... | collective-permute-start | bytes 46088 | tf_op jit(solution)/shard_map/ppermute | solution.py:19
  64.9 9.7 %collective-permute-start.3 = (f32[2,2,10,24,4]{4,3,2,1,0:T(8,128)S(1)}, f32[2,2,10,24,4]{4,3,2,1,0:T(8,128)S(1)}, u32[]{:S(2)}, u32[]{:S(2)}) collective-permute-start(f32[2,2,10,24,4]{4,3,2,1,0:T(8,128)S(1)} %get-tuple-element.59), channel_id=1, source_target_pairs={{2,0},{4,2},{6,4},{8,6},{10,8},{12,10},{14,12},{3,1},{5,3},{7,5},{... | collective-permute-start | bytes 46088 | tf_op jit(solution)/shard_map/ppermute | solution.py:21
  86.5 0.7 copy-start.2
  86.5 0.7 copy-start.3
  86.5 0.7 copy-start.4
  86.5 0.7 copy-start.5
  96.1 5.9 %copy-start.1 = (f32[2,10,16,128]{3,2,1,0:T(8,128)S(1)}, f32[2,10,16,128]{3,2,1,0:T(8,128)}, u32[]{:S(2)}) copy-start(f32[2,10,16,128]{3,2,1,0:T(8,128)} %slice_bitcast_fusion.8) | copy-start | bytes 491524
where the time goes:
time: 189 us; the launch traced here: 188 us
  blocking collectives  83.3 us (44%)
  starting transfers between devices  53.7 us (28%)
  other arithmetic  31.8 us (17%)
  waiting for transfers between devices  14.5 us (8%)
  local copies, waits for them, and re-layouts  4.53 us (2%)
    psum x2, blocking collectives, one_axis_at_a_time(): value = lax.psum(value, axis)  64.3 us
    ppermute x8, starting transfers between devices, extended_2(): lax.ppermute(tail, axis, [(i, (i + 1) % count) for i in range(ends)])  43 us
    all_gather x1, blocking collectives, total_of_pieces(): blocks = lax.all_gather(value, axis)  19 us
    mul x3, other arithmetic, apply_local(): product = roots_wide * field_wide  15.1 us
    ppermute x8, starting transfers between devices, extended_2(): lax.ppermute(head, axis, [((i + 1) % count, i) for i in range(ends)])  10.6 us
    ppermute x8, waiting for transfers between devices, extended_2(): lax.ppermute(head, axis, [((i + 1) % count, i) for i in range(ends)])  10.2 us
    mul x2, other arithmetic, neighbour_sum(): addend = coefficient((step_z, step_x, step_y)) * window  7.57 us
    ppermute x8, waiting for transfers between devices, extended_2(): lax.ppermute(tail, axis, [(i, (i + 1) % count) for i in range(ends)])  4.27 us
  transfers between devices with their start and end apart: 16, of which 4 were waited for; matrix products, arithmetic and copies ran while one was open for 2% of the time, Pallas kernels for 0%

commit v1 on v0

v1 whole, which is shorter than its diff:
```python
import jax
import jax.numpy as jnp
from jax import lax
from jax.experimental import pallas as pl
from jax.experimental.pallas import tpu as pltpu
from jax.sharding import PartitionSpec as P

bed_unit = 2.0 ** (-29)
HALO = 4
STRIP = 24
GROUPED = STRIP // HALO
MAIN_I = (0.25, 0.125)
MAIN_J = (0.125, 0.25)


VMEM = pl.BlockSpec(memory_space=pltpu.VMEM)
SMEM = pl.BlockSpec(memory_space=pltpu.SMEM)


def roll(x, shift, axis):
    return pltpu.roll(x, shift % x.shape[axis], axis)


def lanes(shape):
    return lax.broadcasted_iota(jnp.int32, shape, len(shape) - 1)


def rows(shape):
    return lax.broadcasted_iota(jnp.int32, shape, len(shape) - 2)


def pack_rows(rows_ref, u_ref, table_ref, bed_ref, mask_ref, up_ref, down_ref, geo_ref, sems):
    layers = u_ref.shape[2]
    copies = [
        pltpu.make_async_copy(table_ref.at[rows_ref[s]], geo_ref.at[2 + s], sems.at[s])
        for s in range(2)
    ]
    for copy in copies:
        copy.start()
    geo_ref[0] = mask_ref[...].astype(jnp.float32)
    geo_ref[1] = bed_ref[...].astype(jnp.float32) * bed_unit
    low = rows((8, 128)) < HALO
    for layer in range(layers + 1):
        if layer == layers:
            for copy in copies:
                copy.wait()
        for pair in range(2):
            tiles = [
                u_ref[s, pair, layer] if layer < layers else geo_ref[2 * pair + s] for s in range(2)
            ]
            top = [tile[0:8] for tile in tiles]
            end = [tile[8:16] for tile in tiles]
            up_ref[layer, pair] = jnp.where(low, roll(end[0], HALO, 0), end[1])
            down_ref[layer, pair] = jnp.where(low, top[0], roll(top[1], HALO, 0))


def pack_columns(u_ref, geo_ref, below_ref, above_ref, outer_ref, strip_ref, right_ref, left_ref):
    layers = u_ref.shape[2]
    low = rows((8, 128)) < HALO
    lane = lanes((8, 128))
    used = lane < 4 * STRIP
    place = lane % STRIP
    slot = place // HALO
    zero = jnp.zeros((8, 128), jnp.float32)
    sent_right = [[zero] * 3 for _ in range(2)]
    sent_left = [[zero] * 3 for _ in range(2)]
    for layer in range(layers + 1):
        outer = []
        for pair in range(2):
            below = below_ref[layer, pair]
            above = above_ref[layer, pair]
            outer.append(jnp.where(low, above, roll(below, HALO, 0)))
            outer.append(jnp.where(low, roll(above, HALO, 0), below))
        for k in range(4):
            outer_ref[layer, k] = outer[k]
        for t in range(3):
            strip = zero
            for k in range(4):
                if t == 2:
                    tile = outer[k]
                elif layer < layers:
                    tile = u_ref[k % 2, k // 2, layer, 8 * t : 8 * t + 8]
                else:
                    tile = geo_ref[k, 8 * t : 8 * t + 8]
                at = lane - STRIP * k
                strip = jnp.where((at >= 4) & (at < 12), roll(tile, STRIP * k + 4, 1), strip)
                strip = jnp.where((at >= 12) & (at < 20), roll(tile, STRIP * k + 12 - 120, 1), strip)
            strip_ref[layer, 8 * t : 8 * t + 8] = strip
            group, index = layer // GROUPED, layer % GROUPED
            here = used & (slot == index)
            sent_right[group][t] = jnp.where(
                here, roll(strip, HALO * index - 16, 1), sent_right[group][t]
            )
            sent_left[group][t] = jnp.where(
                here, roll(strip, HALO * index - 4, 1), sent_left[group][t]
            )
    for group in range(2):
        for t in range(3):
            right_ref[group, 8 * t : 8 * t + 8] = sent_right[group][t]
            left_ref[group, 8 * t : 8 * t + 8] = sent_left[group][t]


def operator(
    plane_ref, u_ref, geo_ref, outer_ref, strip_ref, from_left_ref, from_right_ref,
    residual_ref, image_ref, start_ref, gram_ref,
    wide_ref, roots_ref, scale_ref, field_ref, next_ref, *, total_x,
):
    layers = u_ref.shape[2]
    shape = (24, 128)
    lane = lanes(shape)
    row = rows(shape)
    used = lane < 4 * STRIP
    place = lane % STRIP
    number = lane // STRIP

    def around_i(x):
        return roll(x, 1, 0) + roll(x, -1, 0)

    def around_j(x):
        return roll(x, 1, 1) + roll(x, -1, 1)

    geo_strip = None
    for layer in range(layers + 1):
        group, index = layer // GROUPED, layer % GROUPED
        strip = strip_ref[layer]
        strip = jnp.where(used & (place < 4), roll(from_left_ref[group], -HALO * index, 1), strip)
        strip = jnp.where(used & (place >= 20), roll(from_right_ref[group], 20 - HALO * index, 1), strip)
        if layer < layers:
            wide_ref[layer] = strip
        else:
            geo_strip = strip

    def spread_strip(source, to):
        result = jnp.zeros(shape, jnp.float32)
        for k in range(4):
            result = jnp.where(number == k, roll(source, STRIP * (k - to), 1), result)
        return result

    def main_geo(k):
        return jnp.concatenate([geo_ref[k], outer_ref[layers, k]], axis=0)

    def main(k, layer):
        return jnp.concatenate([u_ref[k % 2, k // 2, layer], outer_ref[layer, k]], axis=0)

    mask = main_geo(0)
    bed = main_geo(1)
    strip_mask = spread_strip(geo_strip, 0)
    strip_bed = spread_strip(geo_strip, 1)
    strip_friction = jnp.where(lane < 2 * STRIP, roll(geo_strip, -2 * STRIP, 1), geo_strip)
    position = jnp.where(row < 20, row, row - 24).astype(jnp.float32) + plane_ref[0]
    thickness = 1.0 + 2.0 * position / (total_x - 1)

    def forces(cover, ground):
        slope_x = (roll(ground, -1, 0) - roll(ground, 1, 0)) * 0.5
        slope_y = (roll(ground, -1, 1) - roll(ground, 1, 1)) * 0.5
        return -(cover * thickness * slope_x), -(cover * thickness * slope_y)

    main_force = forces(mask, bed)
    strip_x, strip_y = forces(strip_mask, strip_bed)
    strip_force = jnp.where(lane < 2 * STRIP, strip_x, strip_y)
    bare = 1.0 - mask
    strip_bare = 1.0 - strip_mask

    def viscosity(u, v, below_u, below_v, above_u, above_v, cover):
        stretch_x = roll(u, -1, 0) - roll(u, 1, 0)
        stretch_y = roll(v, -1, 1) - roll(v, 1, 1)
        shear = (roll(u, -1, 1) - roll(u, 1, 1)) + (roll(v, -1, 0) - roll(v, 1, 0))
        rise_u = above_u - below_u
        rise_v = above_v - below_v
        strain = stretch_x * stretch_x + stretch_y * (stretch_y + stretch_x)
        strain = strain + 0.25 * (shear * shear + (rise_u * rise_u + rise_v * rise_v))
        return cover * jnp.exp(jnp.log(0.25 * strain + 0.1) * (-1.0 / 6.0))

    zero = jnp.zeros(shape, jnp.float32)

    def column(get, z):
        return get(z) if 0 <= z < layers else zero

    for s in range(2):
        for z in range(layers):
            get_u, get_v = (lambda y, s=s: main(s, y)), (lambda y, s=s: main(2 + s, y))
            roots_ref[s, z] = viscosity(
                get_u(z), get_v(z), column(get_u, z - 1), column(get_v, z - 1),
                column(get_u, z + 1), column(get_v, z + 1), mask,
            )
    for z in range(layers):
        get_u = lambda y: wide_ref[y]

        def get_v(y):
            return roll(wide_ref[y], -2 * STRIP, 1)

        found = viscosity(
            get_u(z), get_v(z), column(get_u, z - 1), column(get_v, z - 1),
            column(get_u, z + 1), column(get_v, z + 1), strip_mask,
        )
        roots_ref[2, z] = jnp.where(lane < 2 * STRIP, found, roll(found, 2 * STRIP, 1))

    side_i = jnp.where(lane < 2 * STRIP, MAIN_I[0], MAIN_I[1])
    side_j = jnp.where(lane < 2 * STRIP, MAIN_J[0], MAIN_J[1])
    for s in range(3):
        for z in range(layers):
            centre = roots_ref[s, z]
            if z > 0 and z + 1 < layers:
                centre = centre + 0.5 * (roots_ref[s, z - 1] + roots_ref[s, z + 1])
            elif z > 0:
                centre = centre + 0.5 * roots_ref[s, z - 1]
            else:
                centre = centre + 0.5 * roots_ref[s, z + 1]
            along_i = around_i(centre)
            along_j = around_j(centre)
            both = centre + 0.03125 * around_j(along_i)
            if s < 2:
                for c in range(2):
                    scale_ref[2 * c + s, z] = both + MAIN_I[c] * along_i + MAIN_J[c] * along_j
            else:
                scale_ref[4, z] = both + side_i * along_i + side_j * along_j

    def apply(k, get, put):
        if k < 4:
            weight_i, weight_j = MAIN_I[k // 2], MAIN_J[k // 2]
            friction = mask * main_geo(2 + k % 2) + bare
            empty, roots = bare, k % 2
        else:
            weight_i, weight_j = side_i, side_j
            friction = strip_mask * strip_friction + strip_bare
            empty, roots = strip_bare, 2

        def filtered(z):
            product = roots_ref[roots, z] * get(z)
            product = product + weight_i * around_i(product)
            return product + weight_j * around_j(product)

        before, now = None, filtered(0)
        for z in range(layers):
            after = filtered(z + 1) if z + 1 < layers else None
            if before is None:
                total = now + 0.5 * after
            elif after is None:
                total = now + 0.5 * before
            else:
                total = now + 0.5 * (before + after)
            field = get(z)
            result = 4.0 * roots_ref[roots, z] * (scale_ref[k, z] * field - total)
            put(z, result + (friction if z == 0 else empty) * field)
            before, now = now, after

    sums = []
    for k in range(5):
        cover = mask if k < 4 else strip_mask
        force = main_force[k // 2] if k < 4 else strip_force

        def start(z, k=k, cover=cover):
            return cover * (main(k, z) if k < 4 else wide_ref[z])

        def put_residual(z, value, k=k, force=force):
            residual = force - value
            field_ref[z] = residual
            residual_ref[k, z] = residual[0:16]

        def put_image(z, value, k=k):
            next_ref[z] = value
            image_ref[k, z] = value[0:16]

        totals = [jnp.zeros((8, 128), jnp.float32)] * 4

        def put_second(z, value):
            for t in range(2):
                at = slice(8 * t, 8 * t + 8)
                r, a, b = field_ref[z, at], next_ref[z, at], value[at]
                totals[0] = totals[0] + r * r
                totals[1] = totals[1] + r * a
                totals[2] = totals[2] + a * a
                totals[3] = totals[3] + a * b

        apply(k, start, put_residual)
        apply(k, lambda z: field_ref[z], put_image)
        apply(k, lambda z: next_ref[z], put_second)
        sums.append(totals)

    for c in range(2):
        for z in range(layers):
            start_ref[c, z] = mask[0:16] * u_ref[0, c, z] + mask[0:16] * u_ref[1, c, z]

    lane8 = lanes((8, 128))
    inside = (lane8 >= HALO) & (lane8 < 128 - HALO)
    spot = lane8 % STRIP
    edge = (lane8 < 4 * STRIP) & (((spot >= 4) & (spot < 8)) | ((spot >= 16) & (spot < 20)))
    row8 = rows((8, 128))
    table = jnp.zeros((8, 128), jnp.float32)
    for g in range(4):
        for s in range(2):
            value = jnp.where(inside, sums[s][g] + sums[2 + s][g], 0.0)
            value = value + jnp.where(edge & ((lane8 // STRIP) % 2 == s), sums[4][g], 0.0)
            value = jnp.sum(value, axis=0, keepdims=True)
            table = jnp.where(row8 == 2 * g + s, value, table)
    table = jnp.sum(table, axis=1, keepdims=True)
    line = jnp.sum(jnp.where(lane8 == row8, table, 0.0), axis=0, keepdims=True)
    gram_ref[...] = jnp.broadcast_to(line, gram_ref.shape)


def combine(gram_ref, residual_ref, image_ref, start_ref, out_ref):
    layers = start_ref.shape[1]
    shape = (8, 128)
    lane = lanes(shape)
    total = jnp.broadcast_to(jnp.sum(gram_ref[...], axis=0, keepdims=True), shape)
    rr = total
    ra = roll(total, -2, 1)
    aa = roll(total, -4, 1)
    ab = roll(total, -6, 1)
    first = rr / ra
    norm_next = rr - 2.0 * first * ra + first * first * aa
    growth = 1.0 + norm_next / rr
    curve = growth * growth * ra - 2.0 * growth * first * aa + first * first * ab
    second = norm_next / curve
    residual_part = first + second * growth
    image_part = second * first
    ks = [jnp.broadcast_to(residual_part[:, s : s + 1], shape) for s in range(2)]
    ms = [jnp.broadcast_to(image_part[:, s : s + 1], shape) for s in range(2)]
    odd = (lane // STRIP) % 2 == 1
    k_side = jnp.where(odd, ks[1], ks[0])
    m_side = jnp.where(odd, ms[1], ms[0])
    for z in range(layers):
        for t in range(2):
            at = slice(8 * t, 8 * t + 8)
            side = k_side * residual_ref[4, z, at] - m_side * image_ref[4, z, at]
            side = side + roll(side, -STRIP, 1)
            for c in range(2):
                step = ks[0] * residual_ref[2 * c, z, at] - ms[0] * image_ref[2 * c, z, at]
                step = step + ks[1] * residual_ref[2 * c + 1, z, at]
                step = step - ms[1] * image_ref[2 * c + 1, z, at]
                base = 2 * STRIP * c
                step = jnp.where(lane < HALO, roll(side, -(base + 4), 1), step)
                step = jnp.where(lane >= 128 - HALO, roll(side, 124 - base - 16, 1), step)
                out_ref[c, z, at] = start_ref[c, z, at] + step


def f32(*shape):
    return jax.ShapeDtypeStruct(shape, jnp.float32)


def call(kernel, outs, ins, name, scratch=(), in_specs=None):
    return pl.pallas_call(
        kernel,
        in_specs=in_specs or [VMEM] * len(ins),
        out_specs=[VMEM] * len(outs),
        out_shape=list(outs),
        scratch_shapes=list(scratch),
        name=name,
    )(*ins)


def swap_sides(forward, backward, axis):
    count = lax.axis_size(axis)
    up = [(i, i + 1) for i in range(count - 1)]
    down = [(i + 1, i) for i in range(count - 1)]
    return lax.ppermute(forward, axis, up), lax.ppermute(backward, axis, down)


def body(u_prior, friction_rows, friction_table, bed_fixed, ice_mask):
    members, parts, layers, rows_x, rows_y = u_prior.shape
    total_x = rows_x * lax.axis_size("plane")
    up, down, geo = call(
        pack_rows,
        [f32(layers + 1, 2, 8, rows_y), f32(layers + 1, 2, 8, rows_y), f32(4, rows_x, rows_y)],
        [friction_rows, u_prior, friction_table, bed_fixed, ice_mask],
        "pack_rows",
        scratch=[pltpu.SemaphoreType.DMA((2,))],
        in_specs=[SMEM, VMEM, pl.BlockSpec(memory_space=pl.ANY), VMEM, VMEM],
    )
    below, above = swap_sides(up, down, "plane")
    outer, strip, right, left = call(
        pack_columns,
        [f32(layers + 1, 4, 8, rows_y), f32(layers + 1, 24, 128), f32(2, 24, 128), f32(2, 24, 128)],
        [u_prior, geo, below, above],
        "pack_columns",
    )
    from_left, from_right = swap_sides(right, left, "planey")
    plane_start = (lax.axis_index("plane") * rows_x).astype(jnp.float32).reshape(1)
    devices = lax.axis_size("plane") * lax.axis_size("planey")
    ins = [u_prior, geo, outer, strip, from_left, from_right]
    residual, image, start, gram = call(
        lambda *refs: operator(*refs, total_x=total_x),
        [
            f32(5, layers, rows_x, 128),
            f32(5, layers, rows_x, 128),
            f32(2, layers, rows_x, 128),
            f32(devices, 128),
        ],
        [plane_start] + ins,
        "operator",
        scratch=[
            pltpu.VMEM((layers, 24, 128), jnp.float32),
            pltpu.VMEM((3, layers, 24, 128), jnp.float32),
            pltpu.VMEM((5, layers, 24, 128), jnp.float32),
            pltpu.VMEM((layers, 24, 128), jnp.float32),
            pltpu.VMEM((layers, 24, 128), jnp.float32),
        ],
        in_specs=[SMEM] + [VMEM] * len(ins),
    )
    gathered = lax.all_to_all(gram, ("plane", "planey"), 0, 0, tiled=True)
    (local_sum,) = call(
        combine, [f32(2, layers, rows_x, 128)], [gathered, residual, image, start], "combine"
    )
    summed = lax.all_gather(local_sum, "ens").sum(axis=0)
    return summed / (members * lax.axis_size("ens"))


def solution(mesh):
    in_specs = (
        P(("group", "ens"), None, None, "plane", "planey"),
        P(("group", "ens")),
        P("group", "plane", "planey"),
        P("plane", "planey"),
        P("plane", "planey"),
    )
    out_specs = P("group", None, "plane", "planey")
    return jax.shard_map(body, mesh=mesh, in_specs=in_specs, out_specs=out_specs, check_vma=False)
```

time: 189 us -> 108 us (0.57)
  starting transfers between devices: 53.7 us -> 12.5 us
  other arithmetic: 31.8 us -> 0.7 us
  Pallas kernels: 0 us -> 13.8 us
  blocking collectives: 83.3 us -> 69.5 us
  waiting for transfers between devices: 14.5 us -> 10 us
  local copies, waits for them, and re-layouts: 4.53 us -> 1.24 us
    psum x2 -> x0, blocking collectives: 64.3 us -> none  [one_axis_at_a_time(): value = lax.psum(value, axis)]
    all_to_all x0 -> x1, blocking collectives: none -> 62.6 us  [body(): gathered = lax.all_to_all(gram, ('plane', 'planey'), 0, 0, tiled=True)]
    ppermute x16 -> x4, starting transfers between devices: 53.7 us -> 12.5 us  [swap_sides(): return (lax.ppermute(forward, axis, up), lax.ppermute(backward, axis, down))]
    mul x9 -> x0, other arithmetic: 24.6 us -> none  [the longest x3 15.1 us: apply_local(): product = roots_wide * field_wide]
    pallas_call x0 -> x4, Pallas kernels: none -> 13.8 us  [call(): pl.pallas_call(kernel, in_specs=in_specs or [VMEM] * len(ins), out_specs=...]
    all_gather x1, blocking collectives: 19 us -> 6.88 us  [body(): summed = lax.all_gather(local_sum, 'ens').sum(axis=0)]
    ppermute x16 -> x4, waiting for transfers between devices: 14.5 us -> 10 us  [swap_sides(): return (lax.ppermute(forward, axis, up), lax.ppermute(backward, axis, down))]
    reduce_sum x4 -> x1, other arithmetic: 3.14 us -> 0.02 us  [body(): summed = lax.all_gather(local_sum, 'ens').sum(axis=0)]
  transfers between devices with their start and end apart: 16 -> 4, of which waited for: 4 -> 3; matrix products, arithmetic and copies ran while one was open for 2% -> 0% of each run, Pallas kernels for 0% -> 0%
where the time goes in v1:
time: 108 us
  blocking collectives  69.5 us (64%)
  Pallas kernels  13.8 us (13%)
  starting transfers between devices  12.5 us (12%)
  waiting for transfers between devices  10 us (9%)
  local copies, waits for them, and re-layouts  1.24 us (1%)
    all_to_all x1, blocking collectives, body(): gathered = lax.all_to_all(gram, ('plane', 'planey'), 0, 0, tiled=True)  62.6 us
    pallas_call x4, Pallas kernels, call(): pl.pallas_call(kernel, in_specs=in_specs or [VMEM] * len(ins), out_specs=...  13.8 us
    ppermute x4, starting transfers between devices, swap_sides(): return (lax.ppermute(forward, axis, up), lax.ppermute(backward, axis, down))  12.5 us
    ppermute x4, waiting for transfers between devices, swap_sides(): return (lax.ppermute(forward, axis, up), lax.ppermute(backward, axis, down))  10 us
    all_gather x1, blocking collectives, body(): summed = lax.all_gather(local_sum, 'ens').sum(axis=0)  6.88 us
  transfers between devices with their start and end apart: 4, of which 3 were waited for; matrix products, arithmetic and copies ran while one was open for 0% of the time, Pallas kernels for 0%

profile of v1, /device:TPU:65, one launch (start us, length us, event | category | flops | bytes accessed | tf_op | source)
XLA Modules:
  0.0 107.8 jit_solution(7605877809770453358)
XLA Ops:
  0.0 2.4 %pack_rows.1 = (f32[11,2,8,128]{3,2,1,0:T(8,128)}, f32[11,2,8,128]{3,2,1,0:T(8,128)}, f32[4,16,128]{2,1,0:T(8,128)}) custom-call(s32[2]{0:T(128)} %rows_ref.1, f32[2,2,10,16,128]{4,3,2,1,0:T(8,128)} %refs_1_.1, f32[16,16,128]{2,1,0:T(8,128)} %table_ref.1, s32[16,128]{1,0:T(8,128)} %bed_ref.1, s32[16,128]{1,0:T(8,128)} %mask_ref.1), custom_call_target="tpu_custom_call" | custom-call | tf_op jit(solution)/shard_map/pack_rows/pallas_call | solution.py:342
  2.4 6.6 %collective-permute-start = (f32[11,2,8,128]{3,2,1,0:T(8,128)}, f32[11,2,8,128]{3,2,1,0:T(8,128)S(1)}, u32[]{:S(2)}, u32[]{:S(2)}) collective-permute-start(f32[11,2,8,128]{3,2,1,0:T(8,128)} %get-tuple-element.17), channel_id=1, source_target_pairs={{0,16},{16,32},{32,48},{48,64},{64,80},{80,96},{96,112},{112,128},... | collective-permute-start | bytes 270344 | tf_op jit(solution)/shard_map/ppermute | solution.py:356
  9.0 1.3 %collective-permute-start.1 = (f32[11,2,8,128]{3,2,1,0:T(8,128)}, f32[11,2,8,128]{3,2,1,0:T(8,128)S(1)}, u32[]{:S(2)}, u32[]{:S(2)}) collective-permute-start(f32[11,2,8,128]{3,2,1,0:T(8,128)} %get-tuple-element.18), channel_id=1, source_target_pairs={{16,0},{32,16},{48,32},{64,48},{80,64},{96,80},{112,96},{128,112},... | collective-permute-start | bytes 270344 | tf_op jit(solution)/shard_map/ppermute | solution.py:356
  10.3 0.5 collective-permute-done.below_ref
  10.8 0.0 copy-start
  10.8 6.0 %collective-permute-done.1.above_ref = f32[11,2,8,128]{3,2,1,0:T(8,128)S(1)} collective-permute-done((f32[11,2,8,128]{3,2,1,0:T(8,128)}, f32[11,2,8,128]{3,2,1,0:T(8,128)S(1)}, u32[]{:S(2)}, u32[]{:S(2)}) %collective-permute-start.1) | collective-permute-done | bytes 90144 | tf_op jit(solution)/shard_map/ppermute | solution.py:356
  16.9 0.0 copy-start.1
  16.9 0.0 copy-done
  16.9 0.6 copy-done.1
  17.5 3.4 %pack_columns.1 = (f32[11,4,8,128]{3,2,1,0:T(8,128)}, f32[11,24,128]{2,1,0:T(8,128)}, f32[2,24,128]{2,1,0:T(8,128)}, f32[2,24,128]{2,1,0:T(8,128)}) custom-call(f32[2,2,10,16,128]{4,3,2,1,0:T(8,128)} %refs_1_.1, f32[4,16,128]{2,1,0:T(8,128)} %get-tuple-element.16.geo_ref.refs_2_, f32[11,2,8,128]{3,2,1,0:T(8,128)} %copy-done, f32[11,2,8,128]{3,2,1,0:T(8,128)} %copy-done.1), custom_call_target="tpu_custom_call" | custom-call | tf_op jit(solution)/shard_map/pack_columns/pallas_call | solution.py:342
  20.9 3.3 %collective-permute-start.2 = (f32[2,24,128]{2,1,0:T(8,128)}, f32[2,24,128]{2,1,0:T(8,128)S(1)}, u32[]{:S(2)}, u32[]{:S(2)}) collective-permute-start(f32[2,24,128]{2,1,0:T(8,128)} %get-tuple-element.21), channel_id=1, source_target_pairs={{0,2},{2,4},{4,6},{6,8},{8,10},{10,12},{12,14},{1,3},{3,5},{5,7},{... | collective-permute-start | bytes 73736 | tf_op jit(solution)/shard_map/ppermute | solution.py:356
  24.1 1.3 %collective-permute-start.3 = (f32[2,24,128]{2,1,0:T(8,128)}, f32[2,24,128]{2,1,0:T(8,128)S(1)}, u32[]{:S(2)}, u32[]{:S(2)}) collective-permute-start(f32[2,24,128]{2,1,0:T(8,128)} %get-tuple-element.22), channel_id=1, source_target_pairs={{2,0},{4,2},{6,4},{8,6},{10,8},{12,10},{14,12},{3,1},{5,3},{7,5},{... | collective-permute-start | bytes 73736 | tf_op jit(solution)/shard_map/ppermute | solution.py:356
  25.5 0.0 collective-permute-done.2.refs_5_
  25.5 0.0 copy-start.2
  25.5 3.5 %collective-permute-done.3.refs_6_ = f32[2,24,128]{2,1,0:T(8,128)S(1)} collective-permute-done((f32[2,24,128]{2,1,0:T(8,128)}, f32[2,24,128]{2,1,0:T(8,128)S(1)}, u32[]{:S(2)}, u32[]{:S(2)}) %collective-permute-start.3) | collective-permute-done | bytes 24608 | tf_op jit(solution)/shard_map/ppermute | solution.py:356
  29.0 0.0 copy-start.3
  29.0 0.0 copy-done.2
  29.0 0.6 copy-done.3
  29.6 5.8 %operator.1 = (f32[5,10,16,128]{3,2,1,0:T(8,128)}, f32[5,10,16,128]{3,2,1,0:T(8,128)}, f32[2,10,16,128]{3,2,1,0:T(8,128)}, f32[128,128]{1,0:T(8,128)}) custom-call(f32[1]{0:T(128)} %bitcast.refs_0_, f32[2,2,10,16,128]{4,3,2,1,0:T(8,128)} %refs_1_.1, f32[4,16,128]{2,1,0:T(8,128)} %get-tuple-element.16.geo_ref.refs_2_, ...), custom_call_target="tpu_custom_call" | custom-call | tf_op jit(solution)/shard_map/operator/pallas_call | solution.py:342
  35.3 62.6 %all_to_all.11 = f32[128,1,128]{2,1,0:T(1,128)} all-to-all(f32[128,1,128]{2,1,0:T(1,128)} %bitcast.8), channel_id=1, replica_groups=mesh['group'=2,'plane'=16,'planey'=8,'ens'=2] {'plane','planey'}, dimensions={0} | all-to-all | bytes 131072 | tf_op jit(solution)/shard_map/all_to_all | solution.py:400
  97.9 2.3 %combine.1 = f32[2,10,16,128]{3,2,1,0:T(8,128)} custom-call(f32[128,128]{1,0:T(8,128)} %bitcast.7, f32[5,10,16,128]{3,2,1,0:T(8,128)} %get-tuple-element.24.residual_ref, f32[5,10,16,128]{3,2,1,0:T(8,128)} %get-tuple-element.25.image_ref, f32[2,10,16,128]{3,2,1,0:T(8,128)} %get-tuple-element.26.start_ref), custom_call_target="tpu_custom_call" | custom-call | tf_op jit(solution)/shard_map/combine/pallas_call | solution.py:342
  100.2 6.9 %all-gather = f32[4,10,16,128]{3,2,1,0:T(8,128)S(1)} all-gather(f32[2,10,16,128]{3,2,1,0:T(8,128)} %combine.1), channel_id=2, replica_groups=mesh['group'=2,'plane'=16,'planey'=8,'ens'=2] {'ens'}, dimensions={0}, use_global_device_ids=true | all-gather | bytes 491520 | tf_op jit(solution)/shard_map/all_gather | solution.py:404
  107.1 0.7 broadcast_multiply_fusion
  (1 shorter events, 0.0 us)
Async XLA Ops:
  2.4 8.4 %collective-permute-start = (f32[11,2,8,128]{3,2,1,0:T(8,128)}, f32[11,2,8,128]{3,2,1,0:T(8,128)S(1)}, u32[]{:S(2)}, u32[]{:S(2)}) collective-permute-start(f32[11,2,8,128]{3,2,1,0:T(8,128)} %get-tuple-element.17), channel_id=1, source_target_pairs={{0,16},{16,32},{32,48},{48,64},{64,80},{80,96},{96,112},{112,128},... | collective-permute-start | bytes 270344 | tf_op jit(solution)/shard_map/ppermute | solution.py:356
  9.0 7.9 %collective-permute-start.1 = (f32[11,2,8,128]{3,2,1,0:T(8,128)}, f32[11,2,8,128]{3,2,1,0:T(8,128)S(1)}, u32[]{:S(2)}, u32[]{:S(2)}) collective-permute-start(f32[11,2,8,128]{3,2,1,0:T(8,128)} %get-tuple-element.18), channel_id=1, source_target_pairs={{16,0},{32,16},{48,32},{64,48},{80,64},{96,80},{112,96},{128,112},... | collective-permute-start | bytes 270344 | tf_op jit(solution)/shard_map/ppermute | solution.py:356
  10.8 6.0 %copy-start = (f32[11,2,8,128]{3,2,1,0:T(8,128)}, f32[11,2,8,128]{3,2,1,0:T(8,128)S(1)}, u32[]{:S(2)}) copy-start(f32[11,2,8,128]{3,2,1,0:T(8,128)S(1)} %collective-permute-done.below_ref) | copy-start | bytes 270340
  16.9 0.6 copy-start.1
  20.9 4.6 %collective-permute-start.2 = (f32[2,24,128]{2,1,0:T(8,128)}, f32[2,24,128]{2,1,0:T(8,128)S(1)}, u32[]{:S(2)}, u32[]{:S(2)}) collective-permute-start(f32[2,24,128]{2,1,0:T(8,128)} %get-tuple-element.21), channel_id=1, source_target_pairs={{0,2},{2,4},{4,6},{6,8},{8,10},{10,12},{12,14},{1,3},{3,5},{5,7},{... | collective-permute-start | bytes 73736 | tf_op jit(solution)/shard_map/ppermute | solution.py:356
  24.1 4.8 %collective-permute-start.3 = (f32[2,24,128]{2,1,0:T(8,128)}, f32[2,24,128]{2,1,0:T(8,128)S(1)}, u32[]{:S(2)}, u32[]{:S(2)}) collective-permute-start(f32[2,24,128]{2,1,0:T(8,128)} %get-tuple-element.22), channel_id=1, source_target_pairs={{2,0},{4,2},{6,4},{8,6},{10,8},{12,10},{14,12},{3,1},{5,3},{7,5},{... | collective-permute-start | bytes 73736 | tf_op jit(solution)/shard_map/ppermute | solution.py:356
  25.5 3.5 %copy-start.2 = (f32[2,24,128]{2,1,0:T(8,128)}, f32[2,24,128]{2,1,0:T(8,128)S(1)}, u32[]{:S(2)}) copy-start(f32[2,24,128]{2,1,0:T(8,128)S(1)} %collective-permute-done.2.refs_5_) | copy-start | bytes 73732
  29.0 0.6 copy-start.3

commit v2 on v1

--- a/solution.py
+++ b/solution.py
@@ -15,6 +15,7 @@
 
 VMEM = pl.BlockSpec(memory_space=pltpu.VMEM)
 SMEM = pl.BlockSpec(memory_space=pltpu.SMEM)
+ANY = pl.BlockSpec(memory_space=pl.ANY)
 
 
 def roll(x, shift, axis):
@@ -29,21 +30,27 @@
     return lax.broadcasted_iota(jnp.int32, shape, len(shape) - 2)
 
 
-def pack_rows(rows_ref, u_ref, table_ref, bed_ref, mask_ref, up_ref, down_ref, geo_ref, sems):
+def pack_rows(
+    rows_ref, u_hbm, table_hbm, bed_hbm, mask_hbm, up_ref, down_ref, geo_ref, u_ref, ints_ref, sems
+):
     layers = u_ref.shape[2]
-    copies = [
-        pltpu.make_async_copy(table_ref.at[rows_ref[s]], geo_ref.at[2 + s], sems.at[s])
-        for s in range(2)
+    moves = [
+        (u_hbm, u_ref),
+        (mask_hbm, ints_ref.at[0]),
+        (bed_hbm, ints_ref.at[1]),
+        (table_hbm.at[rows_ref[0]], geo_ref.at[2]),
+        (table_hbm.at[rows_ref[1]], geo_ref.at[3]),
     ]
+    copies = [pltpu.make_async_copy(*move, sems.at[i]) for i, move in enumerate(moves)]
     for copy in copies:
         copy.start()
-    geo_ref[0] = mask_ref[...].astype(jnp.float32)
-    geo_ref[1] = bed_ref[...].astype(jnp.float32) * bed_unit
+    for copy in copies[1:]:
+        copy.wait()
+    geo_ref[0] = ints_ref[0].astype(jnp.float32)
+    geo_ref[1] = ints_ref[1].astype(jnp.float32) * bed_unit
+    copies[0].wait()
     low = rows((8, 128)) < HALO
     for layer in range(layers + 1):
-        if layer == layers:
-            for copy in copies:
-                copy.wait()
         for pair in range(2):
             tiles = [
                 u_ref[s, pair, layer] if layer < layers else geo_ref[2 * pair + s] for s in range(2)
@@ -335,13 +342,18 @@
 
 
 def f32(*shape):
-    return jax.ShapeDtypeStruct(shape, jnp.float32)
+    return pltpu.VMEM(shape, jnp.float32)
 
 
 def call(kernel, outs, ins, name, scratch=(), in_specs=None):
+    specs = in_specs or [VMEM] * len(ins)
+    ins = [
+        pltpu.with_memory_space_constraint(x, pltpu.VMEM) if spec is VMEM else x
+        for x, spec in zip(ins, specs)
+    ]
     return pl.pallas_call(
         kernel,
-        in_specs=in_specs or [VMEM] * len(ins),
+        in_specs=specs,
         out_specs=[VMEM] * len(outs),
         out_shape=list(outs),
         scratch_shapes=list(scratch),
@@ -356,35 +368,43 @@
     return lax.ppermute(forward, axis, up), lax.ppermute(backward, axis, down)
 
 
+def copies_of_all(copies, axis):
+    return lax.all_to_all(copies, axis, 0, 0, tiled=True)
+
+
 def body(u_prior, friction_rows, friction_table, bed_fixed, ice_mask):
     members, parts, layers, rows_x, rows_y = u_prior.shape
     total_x = rows_x * lax.axis_size("plane")
-    up, down, geo = call(
+    up, down, geo, u_near = call(
         pack_rows,
-        [f32(layers + 1, 2, 8, rows_y), f32(layers + 1, 2, 8, rows_y), f32(4, rows_x, rows_y)],
+        [
+            f32(layers + 1, 2, 8, rows_y),
+            f32(layers + 1, 2, 8, rows_y),
+            f32(4, rows_x, rows_y),
+            f32(*u_prior.shape),
+        ],
         [friction_rows, u_prior, friction_table, bed_fixed, ice_mask],
         "pack_rows",
-        scratch=[pltpu.SemaphoreType.DMA((2,))],
-        in_specs=[SMEM, VMEM, pl.BlockSpec(memory_space=pl.ANY), VMEM, VMEM],
+        scratch=[pltpu.VMEM((2, rows_x, rows_y), jnp.int32), pltpu.SemaphoreType.DMA((5,))],
+        in_specs=[SMEM, ANY, ANY, ANY, ANY],
     )
     below, above = swap_sides(up, down, "plane")
     outer, strip, right, left = call(
         pack_columns,
         [f32(layers + 1, 4, 8, rows_y), f32(layers + 1, 24, 128), f32(2, 24, 128), f32(2, 24, 128)],
-        [u_prior, geo, below, above],
+        [u_near, geo, below, above],
         "pack_columns",
     )
     from_left, from_right = swap_sides(right, left, "planey")
     plane_start = (lax.axis_index("plane") * rows_x).astype(jnp.float32).reshape(1)
-    devices = lax.axis_size("plane") * lax.axis_size("planey")
-    ins = [u_prior, geo, outer, strip, from_left, from_right]
+    ins = [u_near, geo, outer, strip, from_left, from_right]
     residual, image, start, gram = call(
         lambda *refs: operator(*refs, total_x=total_x),
         [
             f32(5, layers, rows_x, 128),
             f32(5, layers, rows_x, 128),
             f32(2, layers, rows_x, 128),
-            f32(devices, 128),
+            f32(lax.axis_size("plane"), 128),
         ],
         [plane_start] + ins,
         "operator",
@@ -397,7 +417,9 @@
         ],
         in_specs=[SMEM] + [VMEM] * len(ins),
     )
-    gathered = lax.all_to_all(gram, ("plane", "planey"), 0, 0, tiled=True)
+    gathered = copies_of_all(gram, "plane")
+    line = jnp.sum(gathered, axis=0, keepdims=True)
+    gathered = copies_of_all(jnp.broadcast_to(line, (lax.axis_size("planey"), 128)), "planey")
     (local_sum,) = call(
         combine, [f32(2, layers, rows_x, 128)], [gathered, residual, image, start], "combine"
     )

time: 108 us -> 102 us (0.944)
  Pallas kernels: 13.8 us -> 7.94 us
  blocking collectives: 69.5 us -> 70.9 us
  local copies, waits for them, and re-layouts: 1.24 us -> 0.01 us
    pallas_call x4, Pallas kernels: 13.8 us -> 7.94 us  [call(): pl.pallas_call(kernel, in_specs=specs, out_specs=[VMEM] * len(outs), out_...]
    unnamed x8 -> x0, local copies, waits for them, and re-layouts: 1.24 us -> none
    all_gather x1, blocking collectives: 6.88 us -> 8.05 us  [body(): summed = lax.all_gather(local_sum, 'ens').sum(axis=0)]
    all_to_all x1 -> x2, blocking collectives: 62.6 us -> 62.9 us  [copies_of_all(): return lax.all_to_all(copies, axis, 0, 0, tiled=True)]
where the time goes in v2:
time: 102 us
  blocking collectives  70.9 us (70%)
  starting transfers between devices  12.5 us (12%)
  waiting for transfers between devices  9.62 us (9%)
  Pallas kernels  7.94 us (8%)
    all_to_all x2, blocking collectives, copies_of_all(): return lax.all_to_all(copies, axis, 0, 0, tiled=True)  62.9 us
    ppermute x4, starting transfers between devices, swap_sides(): return (lax.ppermute(forward, axis, up), lax.ppermute(backward, axis, down))  12.5 us
    ppermute x4, waiting for transfers between devices, swap_sides(): return (lax.ppermute(forward, axis, up), lax.ppermute(backward, axis, down))  9.62 us
    all_gather x1, blocking collectives, body(): summed = lax.all_gather(local_sum, 'ens').sum(axis=0)  8.05 us
    pallas_call x4, Pallas kernels, call(): pl.pallas_call(kernel, in_specs=specs, out_specs=[VMEM] * len(outs), out_...  7.94 us
  transfers between devices with their start and end apart: 4, of which 3 were waited for; matrix products, arithmetic and copies ran while one was open for 0% of the time, Pallas kernels for 0%

profile of v2, /device:TPU:65, one launch (start us, length us, event | category | flops | bytes accessed | tf_op | source)
XLA Modules:
  0.0 101.8 jit_solution(14053125150239945914)
XLA Ops:
  0.0 1.7 %pack_rows.1 = (f32[11,2,8,128]{3,2,1,0:T(8,128)S(1)}, f32[11,2,8,128]{3,2,1,0:T(8,128)S(1)}, f32[4,16,128]{2,1,0:T(8,128)S(1)}, f32[2,2,10,16,128]{4,3,2,1,0:T(8,128)S(1)}) custom-call(s32[2]{0:T(128)} %rows_ref.1, f32[2,2,10,16,128]{4,3,2,1,0:T(8,128)} %u_hbm.1, f32[16,16,128]{2,1,0:T(8,128)} %table_hbm.1, s32[16,128]{1,0:T(8,128)} %bed_hbm.1, ...), custom_call_target="tpu_custom_call" | custom-call | tf_op jit(solution)/shard_map/pack_rows/pallas_call | solution.py:354
  1.7 6.6 %collective-permute-start = (f32[11,2,8,128]{3,2,1,0:T(8,128)S(1)}, f32[11,2,8,128]{3,2,1,0:T(8,128)S(1)}, u32[]{:S(2)}, u32[]{:S(2)}) collective-permute-start(f32[11,2,8,128]{3,2,1,0:T(8,128)S(1)} %get-tuple-element.19), channel_id=1, source_target_pairs={{0,16},{16,32},{32,48},{48,64},{64,80},{80,96},{96,112},{112,128},... | collective-permute-start | bytes 270344 | tf_op jit(solution)/shard_map/ppermute | solution.py:368
  8.3 1.3 %collective-permute-start.1 = (f32[11,2,8,128]{3,2,1,0:T(8,128)S(1)}, f32[11,2,8,128]{3,2,1,0:T(8,128)S(1)}, u32[]{:S(2)}, u32[]{:S(2)}) collective-permute-start(f32[11,2,8,128]{3,2,1,0:T(8,128)S(1)} %get-tuple-element.20), channel_id=1, source_target_pairs={{16,0},{32,16},{48,32},{64,48},{80,64},{96,80},{112,96},{128,112},... | collective-permute-start | bytes 270344 | tf_op jit(solution)/shard_map/ppermute | solution.py:368
  9.6 0.2 collective-permute-done.below_ref
  9.8 6.1 %collective-permute-done.1.above_ref = f32[11,2,8,128]{3,2,1,0:T(8,128)S(1)} collective-permute-done((f32[11,2,8,128]{3,2,1,0:T(8,128)S(1)}, f32[11,2,8,128]{3,2,1,0:T(8,128)S(1)}, u32[]{:S(2)}, u32[]{:S(2)}) %collective-permute-start.1) | collective-permute-done | bytes 90144 | tf_op jit(solution)/shard_map/ppermute | solution.py:368
  15.9 1.7 %pack_columns.1 = (f32[11,4,8,128]{3,2,1,0:T(8,128)S(1)}, f32[11,24,128]{2,1,0:T(8,128)S(1)}, f32[2,24,128]{2,1,0:T(8,128)S(1)}, f32[2,24,128]{2,1,0:T(8,128)S(1)}) custom-call(f32[2,2,10,16,128]{4,3,2,1,0:T(8,128)S(1)} %get-tuple-element.17.u_ref.refs_1_, f32[4,16,128]{2,1,0:T(8,128)S(1)} %get-tuple-element.18.geo_ref.refs_2_, ...), custom_call_target="tpu_custom_call" | custom-call | tf_op jit(solution)/shard_map/pack_columns/pallas_call | solution.py:354
  17.7 3.3 %collective-permute-start.2 = (f32[2,24,128]{2,1,0:T(8,128)S(1)}, f32[2,24,128]{2,1,0:T(8,128)S(1)}, u32[]{:S(2)}, u32[]{:S(2)}) collective-permute-start(f32[2,24,128]{2,1,0:T(8,128)S(1)} %get-tuple-element.23), channel_id=1, source_target_pairs={{0,2},{2,4},{4,6},{6,8},{8,10},{10,12},{12,14},{1,3},{3,5},{5,7},{... | collective-permute-start | bytes 73736 | tf_op jit(solution)/shard_map/ppermute | solution.py:368
  20.9 1.3 %collective-permute-start.3 = (f32[2,24,128]{2,1,0:T(8,128)S(1)}, f32[2,24,128]{2,1,0:T(8,128)S(1)}, u32[]{:S(2)}, u32[]{:S(2)}) collective-permute-start(f32[2,24,128]{2,1,0:T(8,128)S(1)} %get-tuple-element.24), channel_id=1, source_target_pairs={{2,0},{4,2},{6,4},{8,6},{10,8},{12,10},{14,12},{3,1},{5,3},{7,5},{... | collective-permute-start | bytes 73736 | tf_op jit(solution)/shard_map/ppermute | solution.py:368
  22.3 0.0 collective-permute-done.2.refs_5_
  22.3 3.3 %collective-permute-done.3.refs_6_ = f32[2,24,128]{2,1,0:T(8,128)S(1)} collective-permute-done((f32[2,24,128]{2,1,0:T(8,128)S(1)}, f32[2,24,128]{2,1,0:T(8,128)S(1)}, u32[]{:S(2)}, u32[]{:S(2)}) %collective-permute-start.3) | collective-permute-done | bytes 24608 | tf_op jit(solution)/shard_map/ppermute | solution.py:368
  25.5 4.1 %operator.1 = (f32[5,10,16,128]{3,2,1,0:T(8,128)S(1)}, f32[5,10,16,128]{3,2,1,0:T(8,128)S(1)}, f32[2,10,16,128]{3,2,1,0:T(8,128)S(1)}, f32[16,128]{1,0:T(8,128)S(1)}) custom-call(f32[1]{0:T(128)} %bitcast.refs_0_, f32[2,2,10,16,128]{4,3,2,1,0:T(8,128)S(1)} %get-tuple-element.17.u_ref.refs_1_, f32[4,16,128]{2,1,0:T(8,128)S(1)} %get-tuple-element.18.geo_ref.refs_2_, ...), custom_call_target="tpu_custom_call" | custom-call | tf_op jit(solution)/shard_map/operator/pallas_call | solution.py:354
  29.7 49.3 %all_to_all.17 = f32[16,1,128]{2,1,0:T(1,128)S(1)} all-to-all(f32[16,1,128]{2,1,0:T(1,128)S(1)} %bitcast.7), channel_id=1, replica_groups=mesh['group'=2,'plane'=16,'planey'=8,'ens'=2] {'plane'}, dimensions={0} | all-to-all | bytes 16384 | tf_op jit(solution)/shard_map/all_to_all | solution.py:372
  79.1 13.5 %all_to_all.18 = f32[8,1,128]{2,1,0:T(1,128)S(1)} all-to-all(f32[8,1,128]{2,1,0:T(1,128)S(1)} %broadcast_in_dim.2), channel_id=1, replica_groups=mesh['group'=2,'plane'=16,'planey'=8,'ens'=2] {'planey'}, dimensions={0} | all-to-all | bytes 8192 | tf_op jit(solution)/shard_map/all_to_all | solution.py:372
  92.6 0.4 combine.1
  93.0 8.0 %all-gather = f32[4,10,16,128]{3,2,1,0:T(8,128)S(1)} all-gather(f32[2,10,16,128]{3,2,1,0:T(8,128)S(1)} %combine.1), channel_id=2, replica_groups=mesh['group'=2,'plane'=16,'planey'=8,'ens'=2] {'ens'}, dimensions={0}, use_global_device_ids=true | all-gather | bytes 491520 | tf_op jit(solution)/shard_map/all_gather | solution.py:426
  101.1 0.7 broadcast_multiply_fusion
  (3 shorter events, 0.1 us)
Async XLA Ops:
  1.7 8.1 %collective-permute-start = (f32[11,2,8,128]{3,2,1,0:T(8,128)S(1)}, f32[11,2,8,128]{3,2,1,0:T(8,128)S(1)}, u32[]{:S(2)}, u32[]{:S(2)}) collective-permute-start(f32[11,2,8,128]{3,2,1,0:T(8,128)S(1)} %get-tuple-element.19), channel_id=1, source_target_pairs={{0,16},{16,32},{32,48},{48,64},{64,80},{80,96},{96,112},{112,128},... | collective-permute-start | bytes 270344 | tf_op jit(solution)/shard_map/ppermute | solution.py:368
  8.3 7.7 %collective-permute-start.1 = (f32[11,2,8,128]{3,2,1,0:T(8,128)S(1)}, f32[11,2,8,128]{3,2,1,0:T(8,128)S(1)}, u32[]{:S(2)}, u32[]{:S(2)}) collective-permute-start(f32[11,2,8,128]{3,2,1,0:T(8,128)S(1)} %get-tuple-element.20), channel_id=1, source_target_pairs={{16,0},{32,16},{48,32},{64,48},{80,64},{96,80},{112,96},{128,112},... | collective-permute-start | bytes 270344 | tf_op jit(solution)/shard_map/ppermute | solution.py:368
  17.7 4.6 %collective-permute-start.2 = (f32[2,24,128]{2,1,0:T(8,128)S(1)}, f32[2,24,128]{2,1,0:T(8,128)S(1)}, u32[]{:S(2)}, u32[]{:S(2)}) collective-permute-start(f32[2,24,128]{2,1,0:T(8,128)S(1)} %get-tuple-element.23), channel_id=1, source_target_pairs={{0,2},{2,4},{4,6},{6,8},{8,10},{10,12},{12,14},{1,3},{3,5},{5,7},{... | collective-permute-start | bytes 73736 | tf_op jit(solution)/shard_map/ppermute | solution.py:368
  20.9 4.6 %collective-permute-start.3 = (f32[2,24,128]{2,1,0:T(8,128)S(1)}, f32[2,24,128]{2,1,0:T(8,128)S(1)}, u32[]{:S(2)}, u32[]{:S(2)}) collective-permute-start(f32[2,24,128]{2,1,0:T(8,128)S(1)} %get-tuple-element.24), channel_id=1, source_target_pairs={{2,0},{4,2},{6,4},{8,6},{10,8},{12,10},{14,12},{3,1},{5,3},{7,5},{... | collective-permute-start | bytes 73736 | tf_op jit(solution)/shard_map/ppermute | solution.py:368

commit v3 on v2

--- a/solution.py
+++ b/solution.py
@@ -31,7 +31,8 @@
 
 
 def pack_rows(
-    rows_ref, u_hbm, table_hbm, bed_hbm, mask_hbm, up_ref, down_ref, geo_ref, u_ref, ints_ref, sems
+    rows_ref, place_ref, u_hbm, table_hbm, bed_hbm, mask_hbm,
+    odd_ref, even_ref, geo_ref, u_ref, ints_ref, sems,
 ):
     layers = u_ref.shape[2]
     moves = [
@@ -50,6 +51,7 @@
     geo_ref[1] = ints_ref[1].astype(jnp.float32) * bed_unit
     copies[0].wait()
     low = rows((8, 128)) < HALO
+    odd = place_ref[0] % 2 == 1
     for layer in range(layers + 1):
         for pair in range(2):
             tiles = [
@@ -57,25 +59,30 @@
             ]
             top = [tile[0:8] for tile in tiles]
             end = [tile[8:16] for tile in tiles]
-            up_ref[layer, pair] = jnp.where(low, roll(end[0], HALO, 0), end[1])
-            down_ref[layer, pair] = jnp.where(low, top[0], roll(top[1], HALO, 0))
-
-
-def pack_columns(u_ref, geo_ref, below_ref, above_ref, outer_ref, strip_ref, right_ref, left_ref):
+            up = jnp.where(low, roll(end[0], HALO, 0), end[1])
+            down = jnp.where(low, top[0], roll(top[1], HALO, 0))
+            odd_ref[layer, pair] = jnp.where(odd, up, down)
+            even_ref[layer, pair] = jnp.where(odd, down, up)
+
+
+def pack_columns(
+    row_place_ref, column_place_ref, u_ref, geo_ref, by_odd_ref, by_even_ref,
+    outer_ref, strip_ref, odd_ref, even_ref,
+):
     layers = u_ref.shape[2]
     low = rows((8, 128)) < HALO
     lane = lanes((8, 128))
     used = lane < 4 * STRIP
-    place = lane % STRIP
-    slot = place // HALO
+    slot = (lane % STRIP) // HALO
     zero = jnp.zeros((8, 128), jnp.float32)
-    sent_right = [[zero] * 3 for _ in range(2)]
-    sent_left = [[zero] * 3 for _ in range(2)]
+    odd = row_place_ref[0] % 2 == 1
     for layer in range(layers + 1):
         outer = []
         for pair in range(2):
-            below = below_ref[layer, pair]
-            above = above_ref[layer, pair]
+            by_odd = by_odd_ref[layer, pair]
+            by_even = by_even_ref[layer, pair]
+            below = jnp.where(odd, by_even, by_odd)
+            above = jnp.where(odd, by_odd, by_even)
             outer.append(jnp.where(low, above, roll(below, HALO, 0)))
             outer.append(jnp.where(low, roll(above, HALO, 0), below))
         for k in range(4):
@@ -93,22 +100,26 @@
                 strip = jnp.where((at >= 4) & (at < 12), roll(tile, STRIP * k + 4, 1), strip)
                 strip = jnp.where((at >= 12) & (at < 20), roll(tile, STRIP * k + 12 - 120, 1), strip)
             strip_ref[layer, 8 * t : 8 * t + 8] = strip
-            group, index = layer // GROUPED, layer % GROUPED
-            here = used & (slot == index)
-            sent_right[group][t] = jnp.where(
-                here, roll(strip, HALO * index - 16, 1), sent_right[group][t]
-            )
-            sent_left[group][t] = jnp.where(
-                here, roll(strip, HALO * index - 4, 1), sent_left[group][t]
-            )
-    for group in range(2):
-        for t in range(3):
-            right_ref[group, 8 * t : 8 * t + 8] = sent_right[group][t]
-            left_ref[group, 8 * t : 8 * t + 8] = sent_left[group][t]
+
+    def send(t, carry):
+        at = pl.ds(pl.multiple_of(8 * t, 8), 8)
+        swapped = column_place_ref[0] % 2 == 1
+        for group in range(2):
+            right, left = zero, zero
+            for index in range(min(GROUPED, layers + 1 - GROUPED * group)):
+                strip = strip_ref[GROUPED * group + index, at]
+                here = used & (slot == index)
+                right = jnp.where(here, roll(strip, HALO * index - 16, 1), right)
+                left = jnp.where(here, roll(strip, HALO * index - 4, 1), left)
+            odd_ref[group, at] = jnp.where(swapped, right, left)
+            even_ref[group, at] = jnp.where(swapped, left, right)
+        return carry
+
+    lax.fori_loop(0, 3, send, 0)
 
 
 def operator(
-    plane_ref, u_ref, geo_ref, outer_ref, strip_ref, from_left_ref, from_right_ref,
+    row_place_ref, column_place_ref, u_ref, geo_ref, outer_ref, strip_ref, by_odd_ref, by_even_ref,
     residual_ref, image_ref, start_ref, gram_ref,
     wide_ref, roots_ref, scale_ref, field_ref, next_ref, *, total_x,
 ):
@@ -127,11 +138,14 @@
         return roll(x, 1, 1) + roll(x, -1, 1)
 
     geo_strip = None
+    odd = column_place_ref[0] % 2 == 1
+    from_left = [jnp.where(odd, by_even_ref[g], by_odd_ref[g]) for g in range(2)]
+    from_right = [jnp.where(odd, by_odd_ref[g], by_even_ref[g]) for g in range(2)]
     for layer in range(layers + 1):
         group, index = layer // GROUPED, layer % GROUPED
         strip = strip_ref[layer]
-        strip = jnp.where(used & (place < 4), roll(from_left_ref[group], -HALO * index, 1), strip)
-        strip = jnp.where(used & (place >= 20), roll(from_right_ref[group], 20 - HALO * index, 1), strip)
+        strip = jnp.where(used & (place < 4), roll(from_left[group], -HALO * index, 1), strip)
+        strip = jnp.where(used & (place >= 20), roll(from_right[group], 20 - HALO * index, 1), strip)
         if layer < layers:
             wide_ref[layer] = strip
         else:
@@ -154,7 +168,8 @@
     strip_mask = spread_strip(geo_strip, 0)
     strip_bed = spread_strip(geo_strip, 1)
     strip_friction = jnp.where(lane < 2 * STRIP, roll(geo_strip, -2 * STRIP, 1), geo_strip)
-    position = jnp.where(row < 20, row, row - 24).astype(jnp.float32) + plane_ref[0]
+    position = jnp.where(row < 20, row, row - 24) + row_place_ref[0] * 16
+    position = position.astype(jnp.float32)
     thickness = 1.0 + 2.0 * position / (total_x - 1)
 
     def forces(cover, ground):
@@ -361,11 +376,14 @@
     )(*ins)
 
 
-def swap_sides(forward, backward, axis):
+def swap_sides(by_odd, by_even, axis):
     count = lax.axis_size(axis)
-    up = [(i, i + 1) for i in range(count - 1)]
-    down = [(i + 1, i) for i in range(count - 1)]
-    return lax.ppermute(forward, axis, up), lax.ppermute(backward, axis, down)
+
+    def swap(message, first):
+        pairs = [(i, i + 1) for i in range(first, count - 1, 2)]
+        return lax.ppermute(message, axis, pairs + [(j, i) for i, j in pairs])
+
+    return swap(by_odd, 1), swap(by_even, 0)
 
 
 def copies_of_all(copies, axis):
@@ -375,7 +393,9 @@
 def body(u_prior, friction_rows, friction_table, bed_fixed, ice_mask):
     members, parts, layers, rows_x, rows_y = u_prior.shape
     total_x = rows_x * lax.axis_size("plane")
-    up, down, geo, u_near = call(
+    row_place = lax.axis_index("plane").reshape(1)
+    column_place = lax.axis_index("planey").reshape(1)
+    by_odd, by_even, geo, u_near = call(
         pack_rows,
         [
             f32(layers + 1, 2, 8, rows_y),
@@ -383,21 +403,21 @@
             f32(4, rows_x, rows_y),
             f32(*u_prior.shape),
         ],
-        [friction_rows, u_prior, friction_table, bed_fixed, ice_mask],
+        [friction_rows, row_place, u_prior, friction_table, bed_fixed, ice_mask],
         "pack_rows",
         scratch=[pltpu.VMEM((2, rows_x, rows_y), jnp.int32), pltpu.SemaphoreType.DMA((5,))],
-        in_specs=[SMEM, ANY, ANY, ANY, ANY],
+        in_specs=[SMEM, SMEM, ANY, ANY, ANY, ANY],
     )
-    below, above = swap_sides(up, down, "plane")
-    outer, strip, right, left = call(
+    by_odd, by_even = swap_sides(by_odd, by_even, "plane")
+    outer, strip, side_odd, side_even = call(
         pack_columns,
         [f32(layers + 1, 4, 8, rows_y), f32(layers + 1, 24, 128), f32(2, 24, 128), f32(2, 24, 128)],
-        [u_near, geo, below, above],
+        [row_place, column_place, u_near, geo, by_odd, by_even],
         "pack_columns",
+        in_specs=[SMEM, SMEM] + [VMEM] * 4,
     )
-    from_left, from_right = swap_sides(right, left, "planey")
-    plane_start = (lax.axis_index("plane") * rows_x).astype(jnp.float32).reshape(1)
-    ins = [u_near, geo, outer, strip, from_left, from_right]
+    side_odd, side_even = swap_sides(side_odd, side_even, "planey")
+    ins = [u_near, geo, outer, strip, side_odd, side_even]
     residual, image, start, gram = call(
         lambda *refs: operator(*refs, total_x=total_x),
         [
@@ -406,7 +426,7 @@
             f32(2, layers, rows_x, 128),
             f32(lax.axis_size("plane"), 128),
         ],
-        [plane_start] + ins,
+        [row_place, column_place] + ins,
         "operator",
         scratch=[
             pltpu.VMEM((layers, 24, 128), jnp.float32),
@@ -415,7 +435,7 @@
             pltpu.VMEM((layers, 24, 128), jnp.float32),
             pltpu.VMEM((layers, 24, 128), jnp.float32),
         ],
-        in_specs=[SMEM] + [VMEM] * len(ins),
+        in_specs=[SMEM, SMEM] + [VMEM] * len(ins),
     )
     gathered = copies_of_all(gram, "plane")
     line = jnp.sum(gathered, axis=0, keepdims=True)

time: 102 us -> 98.1 us (0.962)
  waiting for transfers between devices: 9.62 us -> 3.08 us
  starting transfers between devices: 12.5 us -> 18.9 us
  blocking collectives: 70.9 us -> 68.1 us
  Pallas kernels: 7.94 us -> 6.85 us
    ppermute x4, waiting for transfers between devices: 9.62 us -> 3.08 us  [swap(): return lax.ppermute(message, axis, pairs + [(j, i) for i, j in pairs])]
    ppermute x4, starting transfers between devices: 12.5 us -> 18.9 us  [swap(): return lax.ppermute(message, axis, pairs + [(j, i) for i, j in pairs])]
    all_to_all x2, blocking collectives: 62.9 us -> 60 us  [copies_of_all(): return lax.all_to_all(copies, axis, 0, 0, tiled=True)]
    pallas_call x4, Pallas kernels: 7.94 us -> 6.85 us  [call(): pl.pallas_call(kernel, in_specs=specs, out_specs=[VMEM] * len(outs), out_...]
  transfers between devices with their start and end apart: 4 -> 4, of which waited for: 3 -> 2; matrix products, arithmetic and copies ran while one was open for 0% -> 0% of each run, Pallas kernels for 0% -> 0%
where the time goes in v3:
time: 98.1 us; the launch traced here: 97.7 us
  blocking collectives  68.1 us (69%)
  starting transfers between devices  18.9 us (19%)
  Pallas kernels  6.85 us (7%)
  waiting for transfers between devices  3.08 us (3%)
    all_to_all x2, blocking collectives, copies_of_all(): return lax.all_to_all(copies, axis, 0, 0, tiled=True)  60 us
    ppermute x4, starting transfers between devices, swap(): return lax.ppermute(message, axis, pairs + [(j, i) for i, j in pairs])  18.9 us
    all_gather x1, blocking collectives, body(): summed = lax.all_gather(local_sum, 'ens').sum(axis=0)  8.05 us
    pallas_call x4, Pallas kernels, call(): pl.pallas_call(kernel, in_specs=specs, out_specs=[VMEM] * len(outs), out_...  6.85 us
    ppermute x4, waiting for transfers between devices, swap(): return lax.ppermute(message, axis, pairs + [(j, i) for i, j in pairs])  3.08 us
  transfers between devices with their start and end apart: 4, of which 2 were waited for; matrix products, arithmetic and copies ran while one was open for 0% of the time, Pallas kernels for 0%

profile of v3, /device:TPU:65, one launch (start us, length us, event | category | flops | bytes accessed | tf_op | source)
XLA Modules:
  0.0 97.7 jit_solution(16834660378460015845)
XLA Ops:
  0.0 1.7 %pack_rows.1 = (f32[11,2,8,128]{3,2,1,0:T(8,128)S(1)}, f32[11,2,8,128]{3,2,1,0:T(8,128)S(1)}, f32[4,16,128]{2,1,0:T(8,128)S(1)}, f32[2,2,10,16,128]{4,3,2,1,0:T(8,128)S(1)}) custom-call(s32[2]{0:T(128)} %rows_ref.1, s32[1]{0:T(128)} %bitcast.place_ref.row_place_ref.refs_0_, f32[2,2,10,16,128]{4,3,2,1,0:T(8,128)} %u_hbm.1, f32[16,16,128]{2,1,0:T(8,128)} %table_hbm.1, ...), custom_call_target="tpu_custom_call" | custom-call | tf_op jit(solution)/shard_map/pack_rows/pallas_call | solution.py:369
  1.7 0.7 collective-permute-start
  2.4 11.6 %collective-permute-start.1 = (f32[11,2,8,128]{3,2,1,0:T(8,128)S(1)}, f32[11,2,8,128]{3,2,1,0:T(8,128)S(1)}, u32[]{:S(2)}, u32[]{:S(2)}) collective-permute-start(f32[11,2,8,128]{3,2,1,0:T(8,128)S(1)} %get-tuple-element.20), channel_id=1, source_target_pairs={{0,16},{32,48},{64,80},{96,112},{128,144},{160,176},{192,208},{224... | collective-permute-start | bytes 270344 | tf_op jit(solution)/shard_map/ppermute | solution.py:384
  14.0 0.0 collective-permute-done.by_odd_ref
  14.1 1.9 %collective-permute-done.1.by_even_ref = f32[11,2,8,128]{3,2,1,0:T(8,128)S(1)} collective-permute-done((f32[11,2,8,128]{3,2,1,0:T(8,128)S(1)}, f32[11,2,8,128]{3,2,1,0:T(8,128)S(1)}, u32[]{:S(2)}, u32[]{:S(2)}) %collective-permute-start.1) | collective-permute-done | bytes 90144 | tf_op jit(solution)/shard_map/ppermute | solution.py:384
  15.9 0.6 pack_columns.1
  16.6 0.7 collective-permute-start.2
  17.2 5.9 %collective-permute-start.3 = (f32[2,24,128]{2,1,0:T(8,128)S(1)}, f32[2,24,128]{2,1,0:T(8,128)S(1)}, u32[]{:S(2)}, u32[]{:S(2)}) collective-permute-start(f32[2,24,128]{2,1,0:T(8,128)S(1)} %get-tuple-element.24), channel_id=1, source_target_pairs={{0,2},{4,6},{8,10},{12,14},{2,0},{6,4},{10,8},{14,12},{1,3},{5,7},... | collective-permute-start | bytes 73736 | tf_op jit(solution)/shard_map/ppermute | solution.py:384
  23.2 0.0 collective-permute-done.2.refs_6_
  23.2 1.2 %collective-permute-done.3.refs_7_ = f32[2,24,128]{2,1,0:T(8,128)S(1)} collective-permute-done((f32[2,24,128]{2,1,0:T(8,128)S(1)}, f32[2,24,128]{2,1,0:T(8,128)S(1)}, u32[]{:S(2)}, u32[]{:S(2)}) %collective-permute-start.3) | collective-permute-done | bytes 24608 | tf_op jit(solution)/shard_map/ppermute | solution.py:384
  24.4 4.1 %operator.1 = (f32[5,10,16,128]{3,2,1,0:T(8,128)S(1)}, f32[5,10,16,128]{3,2,1,0:T(8,128)S(1)}, f32[2,10,16,128]{3,2,1,0:T(8,128)S(1)}, f32[16,128]{1,0:T(8,128)S(1)}) custom-call(s32[1]{0:T(128)} %bitcast.place_ref.row_place_ref.refs_0_, s32[1]{0:T(128)} %bitcast.1.column_place_ref.refs_1_, f32[2,2,10,16,128]{4,3,2,1,0:T(8,128)S(1)} %get-tuple-element.17.u_ref.refs_2_, ...), custom_call_target="tpu_custom_call" | custom-call | tf_op jit(solution)/shard_map/operator/pallas_call | solution.py:369
  28.5 47.6 %all_to_all.17 = f32[16,1,128]{2,1,0:T(1,128)S(1)} all-to-all(f32[16,1,128]{2,1,0:T(1,128)S(1)} %bitcast.8), channel_id=1, replica_groups=mesh['group'=2,'plane'=16,'planey'=8,'ens'=2] {'plane'}, dimensions={0} | all-to-all | bytes 16384 | tf_op jit(solution)/shard_map/all_to_all | solution.py:390
  76.1 12.4 %all_to_all.18 = f32[8,1,128]{2,1,0:T(1,128)S(1)} all-to-all(f32[8,1,128]{2,1,0:T(1,128)S(1)} %broadcast_in_dim.2), channel_id=1, replica_groups=mesh['group'=2,'plane'=16,'planey'=8,'ens'=2] {'planey'}, dimensions={0} | all-to-all | bytes 8192 | tf_op jit(solution)/shard_map/all_to_all | solution.py:390
  88.6 0.4 combine.1
  89.0 8.0 %all-gather = f32[4,10,16,128]{3,2,1,0:T(8,128)S(1)} all-gather(f32[2,10,16,128]{3,2,1,0:T(8,128)S(1)} %combine.1), channel_id=2, replica_groups=mesh['group'=2,'plane'=16,'planey'=8,'ens'=2] {'ens'}, dimensions={0}, use_global_device_ids=true | all-gather | bytes 491520 | tf_op jit(solution)/shard_map/all_gather | solution.py:446
  97.1 0.7 broadcast_multiply_fusion
  (3 shorter events, 0.1 us)
Async XLA Ops:
  1.7 12.3 %collective-permute-start = (f32[11,2,8,128]{3,2,1,0:T(8,128)S(1)}, f32[11,2,8,128]{3,2,1,0:T(8,128)S(1)}, u32[]{:S(2)}, u32[]{:S(2)}) collective-permute-start(f32[11,2,8,128]{3,2,1,0:T(8,128)S(1)} %get-tuple-element.19), channel_id=1, source_target_pairs={{16,32},{48,64},{80,96},{112,128},{144,160},{176,192},{208,224},{3... | collective-permute-start | bytes 270344 | tf_op jit(solution)/shard_map/ppermute | solution.py:384
  2.4 13.6 %collective-permute-start.1 = (f32[11,2,8,128]{3,2,1,0:T(8,128)S(1)}, f32[11,2,8,128]{3,2,1,0:T(8,128)S(1)}, u32[]{:S(2)}, u32[]{:S(2)}) collective-permute-start(f32[11,2,8,128]{3,2,1,0:T(8,128)S(1)} %get-tuple-element.20), channel_id=1, source_target_pairs={{0,16},{32,48},{64,80},{96,112},{128,144},{160,176},{192,208},{224... | collective-permute-start | bytes 270344 | tf_op jit(solution)/shard_map/ppermute | solution.py:384
  16.6 6.6 %collective-permute-start.2 = (f32[2,24,128]{2,1,0:T(8,128)S(1)}, f32[2,24,128]{2,1,0:T(8,128)S(1)}, u32[]{:S(2)}, u32[]{:S(2)}) collective-permute-start(f32[2,24,128]{2,1,0:T(8,128)S(1)} %get-tuple-element.23), channel_id=1, source_target_pairs={{2,4},{6,8},{10,12},{4,2},{8,6},{12,10},{3,5},{7,9},{11,13},{5,3},... | collective-permute-start | bytes 73736 | tf_op jit(solution)/shard_map/ppermute | solution.py:384
  17.2 7.1 %collective-permute-start.3 = (f32[2,24,128]{2,1,0:T(8,128)S(1)}, f32[2,24,128]{2,1,0:T(8,128)S(1)}, u32[]{:S(2)}, u32[]{:S(2)}) collective-permute-start(f32[2,24,128]{2,1,0:T(8,128)S(1)} %get-tuple-element.24), channel_id=1, source_target_pairs={{0,2},{4,6},{8,10},{12,14},{2,0},{6,4},{10,8},{14,12},{1,3},{5,7},... | collective-permute-start | bytes 73736 | tf_op jit(solution)/shard_map/ppermute | solution.py:384

commit v4 on v3

v4 whole, which is shorter than its diff:
```python
import jax
import jax.numpy as jnp
from jax import lax
from jax.experimental import pallas as pl
from jax.experimental.pallas import tpu as pltpu
from jax.sharding import PartitionSpec as P

bed_unit = 2.0 ** (-29)
HALO = 4
STRIP = 24
GROUPED = STRIP // HALO
MAIN_I = (0.25, 0.125)
MAIN_J = (0.125, 0.25)


VMEM = pl.BlockSpec(memory_space=pltpu.VMEM)
SMEM = pl.BlockSpec(memory_space=pltpu.SMEM)
ANY = pl.BlockSpec(memory_space=pl.ANY)


def roll(x, shift, axis):
    return pltpu.roll(x, shift % x.shape[axis], axis)


def lanes(shape):
    return lax.broadcasted_iota(jnp.int32, shape, len(shape) - 1)


def rows(shape):
    return lax.broadcasted_iota(jnp.int32, shape, len(shape) - 2)


def pack_rows(
    place_ref, rows_hbm, u_hbm, table_hbm, bed_hbm, mask_hbm,
    odd_ref, even_ref, geo_ref, u_ref, rows_ref, table_ref, ints_ref, sems,
):
    layers = u_ref.shape[2]
    moves = [
        (u_hbm, u_ref),
        (rows_hbm, rows_ref),
        (table_hbm, table_ref),
        (mask_hbm, ints_ref.at[0]),
        (bed_hbm, ints_ref.at[1]),
    ]
    copies = [pltpu.make_async_copy(*move, sems.at[i]) for i, move in enumerate(moves)]
    for copy in copies:
        copy.start()
    for copy in copies:
        copy.wait()
    geo_ref[0] = ints_ref[0].astype(jnp.float32)
    geo_ref[1] = ints_ref[1].astype(jnp.float32) * bed_unit
    for s in range(2):
        geo_ref[2 + s] = table_ref[rows_ref[s]]
    low = rows((8, 128)) < HALO
    odd = place_ref[0] % 2 == 1
    for layer in range(layers + 1):
        for pair in range(2):
            tiles = [
                u_ref[s, pair, layer] if layer < layers else geo_ref[2 * pair + s] for s in range(2)
            ]
            top = [tile[0:8] for tile in tiles]
            end = [tile[8:16] for tile in tiles]
            up = jnp.where(low, roll(end[0], HALO, 0), end[1])
            down = jnp.where(low, top[0], roll(top[1], HALO, 0))
            odd_ref[layer, pair] = jnp.where(odd, up, down)
            even_ref[layer, pair] = jnp.where(odd, down, up)


def pack_columns(
    row_place_ref, column_place_ref, u_ref, geo_ref, by_odd_ref, by_even_ref,
    outer_ref, strip_ref, odd_ref, even_ref,
):
    layers = u_ref.shape[2]
    low = rows((8, 128)) < HALO
    lane = lanes((8, 128))
    used = lane < 4 * STRIP
    slot = (lane % STRIP) // HALO
    zero = jnp.zeros((8, 128), jnp.float32)
    odd = row_place_ref[0] % 2 == 1
    for layer in range(layers + 1):
        outer = []
        for pair in range(2):
            by_odd = by_odd_ref[layer, pair]
            by_even = by_even_ref[layer, pair]
            below = jnp.where(odd, by_even, by_odd)
            above = jnp.where(odd, by_odd, by_even)
            outer.append(jnp.where(low, above, roll(below, HALO, 0)))
            outer.append(jnp.where(low, roll(above, HALO, 0), below))
        for k in range(4):
            outer_ref[layer, k] = outer[k]
        for t in range(3):
            strip = zero
            for k in range(4):
                if t == 2:
                    tile = outer[k]
                elif layer < layers:
                    tile = u_ref[k % 2, k // 2, layer, 8 * t : 8 * t + 8]
                else:
                    tile = geo_ref[k, 8 * t : 8 * t + 8]
                at = lane - STRIP * k
                strip = jnp.where((at >= 4) & (at < 12), roll(tile, STRIP * k + 4, 1), strip)
                strip = jnp.where((at >= 12) & (at < 20), roll(tile, STRIP * k + 12 - 120, 1), strip)
            strip_ref[layer, 8 * t : 8 * t + 8] = strip

    def send(t, carry):
        at = pl.ds(pl.multiple_of(8 * t, 8), 8)
        swapped = column_place_ref[0] % 2 == 1
        for group in range(2):
            right, left = zero, zero
            for index in range(min(GROUPED, layers + 1 - GROUPED * group)):
                strip = strip_ref[GROUPED * group + index, at]
                here = used & (slot == index)
                right = jnp.where(here, roll(strip, HALO * index - 16, 1), right)
                left = jnp.where(here, roll(strip, HALO * index - 4, 1), left)
            odd_ref[group, at] = jnp.where(swapped, right, left)
            even_ref[group, at] = jnp.where(swapped, left, right)
        return carry

    lax.fori_loop(0, 3, send, 0)


def around_i(x):
    return roll(x, 1, 0) + roll(x, -1, 0)


def around_j(x):
    return roll(x, 1, 1) + roll(x, -1, 1)


def forces(cover, ground, row_start, total_x):
    row = rows(cover.shape)
    position = (jnp.where(row < 20, row, row - 24) + row_start).astype(jnp.float32)
    thickness = 1.0 + 2.0 * position / (total_x - 1)
    slope_x = (roll(ground, -1, 0) - roll(ground, 1, 0)) * 0.5
    slope_y = (roll(ground, -1, 1) - roll(ground, 1, 1)) * 0.5
    return -(cover * thickness * slope_x), -(cover * thickness * slope_y)


def difference(get, z, layers):
    if z == 0:
        return get(1)
    if z + 1 == layers:
        return -get(z - 1)
    return get(z + 1) - get(z - 1)


def viscosity(get_u, get_v, z, layers, cover):
    u, v = get_u(z), get_v(z)
    stretch_x = roll(u, -1, 0) - roll(u, 1, 0)
    stretch_y = roll(v, -1, 1) - roll(v, 1, 1)
    shear = (roll(u, -1, 1) - roll(u, 1, 1)) + (roll(v, -1, 0) - roll(v, 1, 0))
    rise_u = difference(get_u, z, layers)
    rise_v = difference(get_v, z, layers)
    strain = stretch_x * stretch_x + stretch_y * (stretch_y + stretch_x)
    strain = strain + 0.25 * (shear * shear + (rise_u * rise_u + rise_v * rise_v))
    return cover * jnp.exp(jnp.log(0.25 * strain + 0.1) * (-1.0 / 6.0))


def with_neighbours(get, z, layers):
    if z == 0:
        return get(0) + 0.5 * get(1)
    if z + 1 == layers:
        return get(z) + 0.5 * get(z - 1)
    return get(z) + 0.5 * (get(z - 1) + get(z + 1))


def apply(get, put, roots, scale, weight_i, weight_j, friction, empty, layers, kept=24):
    def kept_rows(x):
        return x[0:kept] if x.ndim else x

    def filtered(z):
        product = roots(z) * get(z)
        product = (product + weight_i * around_i(product))[0:kept]
        return product + kept_rows(weight_j) * around_j(product)

    done = {}
    for z in range(layers + 1):
        if z < layers:
            done[z] = filtered(z)
        if z > 0:
            at = z - 1
            total = with_neighbours(lambda y: done[y], at, layers)
            field = get(at)[0:kept]
            result = 4.0 * roots(at)[0:kept] * (scale(at)[0:kept] * field - total)
            put(at, result + (friction if at == 0 else empty)[0:kept] * field)


def products(field, image, second, layers, totals):
    totals = list(totals)
    for z in range(layers):
        for t in range(2):
            at = slice(8 * t, 8 * t + 8)
            r, a, b = field(z)[at], image(z)[at], second(z)[at]
            for i, (x, y) in enumerate(((r, r), (r, a), (a, a), (a, b))):
                totals[i] = totals[i] + x * y
    return totals


def main_part(
    row_place_ref, u_ref, geo_ref, outer_ref,
    residual_ref, image_ref, start_ref, table_ref,
    wide_ref, roots_ref, scale_ref, field_ref, next_ref, second_ref, *, total_x,
):
    layers = u_ref.shape[2]
    row_start = row_place_ref[0] * 16

    def geo(k):
        return jnp.concatenate([geo_ref[k], outer_ref[layers, k]], axis=0)

    mask = geo(0)
    bare = 1.0 - mask
    force = forces(mask, geo(1), row_start, total_x)
    lane8 = lanes((8, 128))
    inside = (lane8 >= HALO) & (lane8 < 128 - HALO)
    row8 = rows((8, 128))
    table_ref[...] = jnp.zeros((8, 128), jnp.float32)

    def sample(s, carry):
        friction = mask * jnp.concatenate([geo_ref[2 + s], outer_ref[layers, 2 + s]], axis=0) + bare
        for c in range(2):
            for z in range(layers):
                wide_ref[c, z, 0:16] = u_ref[s, c, z]
                wide_ref[c, z, 16:24] = outer_ref[z, 2 * c + s]
        for z in range(layers):
            roots_ref[z] = viscosity(
                lambda y: wide_ref[0, y], lambda y: wide_ref[1, y], z, layers, mask
            )
        for z in range(layers):
            centre = with_neighbours(lambda y: roots_ref[y], z, layers)
            along_i = around_i(centre)
            along_j = around_j(centre)
            both = centre + 0.03125 * around_j(along_i)
            for c in range(2):
                scale_ref[c, z] = both + MAIN_I[c] * along_i + MAIN_J[c] * along_j

        def component(c, carry):
            first = c == 0
            weight_i = jnp.where(first, MAIN_I[0], MAIN_I[1])
            weight_j = jnp.where(first, MAIN_J[0], MAIN_J[1])
            pull = jnp.where(first, force[0], force[1])
            shared = (
                lambda z: roots_ref[z], lambda z: scale_ref[c, z],
                weight_i, weight_j, friction, bare, layers,
            )

            def put_residual(z, value):
                residual = pull - value
                field_ref[z] = residual
                residual_ref[2 * c + s, z] = residual[0:16]

            def put_image(z, value):
                next_ref[z] = value
                image_ref[2 * c + s, z] = value[0:16]

            def put_second(z, value):
                second_ref[z] = value

            apply(lambda z: mask * wide_ref[c, z], put_residual, *shared)
            apply(lambda z: field_ref[z], put_image, *shared)
            apply(lambda z: next_ref[z], put_second, *shared, kept=16)
            totals = products(
                lambda z: field_ref[z], lambda z: next_ref[z], lambda z: second_ref[z], layers,
                [jnp.zeros((8, 128), jnp.float32)] * 4,
            )
            for g in range(4):
                line = jnp.sum(jnp.where(inside, totals[g], 0.0), axis=0, keepdims=True)
                table_ref[...] += jnp.where(row8 == 2 * g + s, line, 0.0)
            return carry

        return lax.fori_loop(0, 2, component, carry)

    lax.fori_loop(0, 2, sample, 0)
    for c in range(2):
        for z in range(layers):
            start_ref[c, z] = mask[0:16] * u_ref[0, c, z] + mask[0:16] * u_ref[1, c, z]


def strip_part(
    row_place_ref, column_place_ref, strip_ref, by_odd_ref, by_even_ref, table_ref,
    residual_ref, image_ref, gram_ref,
    wide_ref, roots_ref, scale_ref, field_ref, next_ref, second_ref, *, total_x,
):
    layers = strip_ref.shape[0] - 1
    shape = (24, 128)
    lane = lanes(shape)
    used = lane < 4 * STRIP
    place = lane % STRIP
    number = lane // STRIP
    low = lane < 2 * STRIP

    geo = None
    odd = column_place_ref[0] % 2 == 1
    from_left = [jnp.where(odd, by_even_ref[g], by_odd_ref[g]) for g in range(2)]
    from_right = [jnp.where(odd, by_odd_ref[g], by_even_ref[g]) for g in range(2)]
    for layer in range(layers + 1):
        group, index = layer // GROUPED, layer % GROUPED
        strip = strip_ref[layer]
        strip = jnp.where(used & (place < 4), roll(from_left[group], -HALO * index, 1), strip)
        strip = jnp.where(used & (place >= 20), roll(from_right[group], 20 - HALO * index, 1), strip)
        if layer < layers:
            wide_ref[layer] = strip
        else:
            geo = strip

    def spread(to):
        result = jnp.zeros(shape, jnp.float32)
        for k in range(4):
            result = jnp.where(number == k, roll(geo, STRIP * (k - to), 1), result)
        return result

    mask = spread(0)
    bare = 1.0 - mask
    friction = mask * jnp.where(low, roll(geo, -2 * STRIP, 1), geo) + bare
    force_x, force_y = forces(mask, spread(1), row_place_ref[0] * 16, total_x)
    force = jnp.where(low, force_x, force_y)
    weight_i = jnp.where(low, MAIN_I[0], MAIN_I[1])
    weight_j = jnp.where(low, MAIN_J[0], MAIN_J[1])

    for z in range(layers):
        found = viscosity(
            lambda y: wide_ref[y], lambda y: roll(wide_ref[y], -2 * STRIP, 1), z, layers, mask
        )
        roots_ref[z] = jnp.where(low, found, roll(found, 2 * STRIP, 1))
    for z in range(layers):
        centre = with_neighbours(lambda y: roots_ref[y], z, layers)
        centre = centre + weight_i * around_i(centre)
        scale_ref[z] = centre + weight_j * around_j(centre)

    def put_residual(z, value):
        residual = force - value
        field_ref[z] = residual
        residual_ref[z] = residual[0:16]

    def put_image(z, value):
        next_ref[z] = value
        image_ref[z] = value[0:16]

    def put_second(z, value):
        second_ref[z] = value

    shared = (
        lambda z: roots_ref[z], lambda z: scale_ref[z], weight_i, weight_j, friction, bare, layers,
    )
    apply(lambda z: mask * wide_ref[z], put_residual, *shared)
    apply(lambda z: field_ref[z], put_image, *shared)
    apply(lambda z: next_ref[z], put_second, *shared, kept=16)
    totals = products(
        lambda z: field_ref[z], lambda z: next_ref[z], lambda z: second_ref[z], layers,
        [jnp.zeros((8, 128), jnp.float32)] * 4,
    )

    lane8 = lanes((8, 128))
    row8 = rows((8, 128))
    spot = lane8 % STRIP
    edge = (lane8 < 4 * STRIP) & (((spot >= 4) & (spot < 8)) | ((spot >= 16) & (spot < 20)))
    table = table_ref[...]
    for g in range(4):
        line = jnp.broadcast_to(jnp.sum(totals[g], axis=0, keepdims=True), (8, 128))
        for s in range(2):
            here = edge & ((lane8 // STRIP) % 2 == s) & (row8 == 2 * g + s)
            table = table + jnp.where(here, line, 0.0)
    table = jnp.sum(table, axis=1, keepdims=True)
    line = jnp.sum(jnp.where(lane8 == row8, table, 0.0), axis=0, keepdims=True)
    gram_ref[...] = jnp.broadcast_to(line, gram_ref.shape)


def combine(
    gram_ref, residual_ref, image_ref, start_ref, side_residual_ref, side_image_ref, out_ref
):
    layers = start_ref.shape[1]
    shape = (8, 128)
    lane = lanes(shape)
    total = jnp.broadcast_to(jnp.sum(gram_ref[...], axis=0, keepdims=True), shape)
    rr = total
    ra = roll(total, -2, 1)
    aa = roll(total, -4, 1)
    ab = roll(total, -6, 1)
    first = rr / ra
    norm_next = rr - 2.0 * first * ra + first * first * aa
    growth = 1.0 + norm_next / rr
    curve = growth * growth * ra - 2.0 * growth * first * aa + first * first * ab
    second = norm_next / curve
    residual_part = first + second * growth
    image_part = second * first
    ks = [jnp.broadcast_to(residual_part[:, s : s + 1], shape) for s in range(2)]
    ms = [jnp.broadcast_to(image_part[:, s : s + 1], shape) for s in range(2)]
    odd = (lane // STRIP) % 2 == 1
    k_side = jnp.where(odd, ks[1], ks[0])
    m_side = jnp.where(odd, ms[1], ms[0])
    for z in range(layers):
        for t in range(2):
            at = slice(8 * t, 8 * t + 8)
            side = k_side * side_residual_ref[z, at] - m_side * side_image_ref[z, at]
            side = side + roll(side, -STRIP, 1)
            for c in range(2):
                step = ks[0] * residual_ref[2 * c, z, at] - ms[0] * image_ref[2 * c, z, at]
                step = step + ks[1] * residual_ref[2 * c + 1, z, at]
                step = step - ms[1] * image_ref[2 * c + 1, z, at]
                base = 2 * STRIP * c
                step = jnp.where(lane < HALO, roll(side, -(base + 4), 1), step)
                step = jnp.where(lane >= 128 - HALO, roll(side, 124 - base - 16, 1), step)
                out_ref[c, z, at] = start_ref[c, z, at] + step


def f32(*shape):
    return pltpu.VMEM(shape, jnp.float32)


def call(kernel, outs, ins, name, scratch=(), in_specs=None):
    specs = in_specs or [VMEM] * len(ins)
    ins = [
        pltpu.with_memory_space_constraint(x, pltpu.VMEM) if spec is VMEM else x
        for x, spec in zip(ins, specs)
    ]
    return pl.pallas_call(
        kernel,
        in_specs=specs,
        out_specs=[VMEM] * len(outs),
        out_shape=list(outs),
        scratch_shapes=list(scratch),
        name=name,
    )(*ins)


def swap_sides(by_odd, by_even, axis):
    count = lax.axis_size(axis)

    def swap(message, first):
        pairs = [(i, i + 1) for i in range(first, count - 1, 2)]
        return lax.ppermute(message, axis, pairs + [(j, i) for i, j in pairs])

    return swap(by_odd, 1), swap(by_even, 0)


def copies_of_all(copies, axis):
    return lax.all_to_all(copies, axis, 0, 0, tiled=True)


def body(u_prior, friction_rows, friction_table, bed_fixed, ice_mask):
    members, parts, layers, rows_x, rows_y = u_prior.shape
    total_x = rows_x * lax.axis_size("plane")
    row_place = lax.axis_index("plane").reshape(1)
    column_place = lax.axis_index("planey").reshape(1)
    by_odd, by_even, geo, u_near = call(
        pack_rows,
        [
            f32(layers + 1, 2, 8, rows_y),
            f32(layers + 1, 2, 8, rows_y),
            f32(4, rows_x, rows_y),
            f32(*u_prior.shape),
        ],
        [row_place, friction_rows, u_prior, friction_table, bed_fixed, ice_mask],
        "pack_rows",
        scratch=[
            pltpu.SMEM(friction_rows.shape, jnp.int32),
            pltpu.VMEM(friction_table.shape, jnp.float32),
            pltpu.VMEM((2, rows_x, rows_y), jnp.int32),
            pltpu.SemaphoreType.DMA((5,)),
        ],
        in_specs=[SMEM] + [ANY] * 5,
    )
    by_odd, by_even = swap_sides(by_odd, by_even, "plane")
    outer, strip, side_odd, side_even = call(
        pack_columns,
        [f32(layers + 1, 4, 8, rows_y), f32(layers + 1, 24, 128), f32(2, 24, 128), f32(2, 24, 128)],
        [row_place, column_place, u_near, geo, by_odd, by_even],
        "pack_columns",
        in_specs=[SMEM, SMEM] + [VMEM] * 4,
    )
    side_odd, side_even = swap_sides(side_odd, side_even, "planey")
    residual, image, start, table = call(
        lambda *refs: main_part(*refs, total_x=total_x),
        [
            f32(4, layers, rows_x, 128),
            f32(4, layers, rows_x, 128),
            f32(2, layers, rows_x, 128),
            f32(8, 128),
        ],
        [row_place, u_near, geo, outer],
        "main_part",
        scratch=[
            pltpu.VMEM((2, layers, 24, 128), jnp.float32),
            pltpu.VMEM((layers, 24, 128), jnp.float32),
            pltpu.VMEM((2, layers, 24, 128), jnp.float32),
            pltpu.VMEM((layers, 24, 128), jnp.float32),
            pltpu.VMEM((layers, 24, 128), jnp.float32),
            pltpu.VMEM((layers, 16, 128), jnp.float32),
        ],
        in_specs=[SMEM] + [VMEM] * 3,
    )
    side_residual, side_image, gram = call(
        lambda *refs: strip_part(*refs, total_x=total_x),
        [
            f32(layers, rows_x, 128),
            f32(layers, rows_x, 128),
            f32(lax.axis_size("plane"), 128),
        ],
        [row_place, column_place, strip, side_odd, side_even, table],
        "strip_part",
        scratch=[pltpu.VMEM((layers, 24, 128), jnp.float32)] * 5
        + [pltpu.VMEM((layers, 16, 128), jnp.float32)],
        in_specs=[SMEM, SMEM] + [VMEM] * 4,
    )
    gathered = copies_of_all(gram, "plane")
    line = jnp.sum(gathered, axis=0, keepdims=True)
    gathered = copies_of_all(jnp.broadcast_to(line, (lax.axis_size("planey"), 128)), "planey")
    (local_sum,) = call(
        combine, [f32(2, layers, rows_x, 128)], [gathered, residual, image, start, side_residual, side_image],
        "combine",

    )
    summed = lax.all_gather(local_sum, "ens").sum(axis=0)
    return summed / (members * lax.axis_size("ens"))


def solution(mesh):
    in_specs = (
        P(("group", "ens"), None, None, "plane", "planey"),
        P(("group", "ens")),
        P("group", "plane", "planey"),
        P("plane", "planey"),
        P("plane", "planey"),
    )
    out_specs = P("group", None, "plane", "planey")
    return jax.shard_map(body, mesh=mesh, in_specs=in_specs, out_specs=out_specs, check_vma=False)
```

time: 98.1 us -> 94.5 us (0.963)
  blocking collectives: 68.1 us -> 66.9 us
  waiting for transfers between devices: 3.08 us -> 1.9 us
  Pallas kernels: 6.85 us -> 5.73 us
    ppermute x4, waiting for transfers between devices: 3.08 us -> 1.9 us  [swap(): return lax.ppermute(message, axis, pairs + [(j, i) for i, j in pairs])]
    pallas_call x4 -> x5, Pallas kernels: 6.85 us -> 5.73 us  [call(): pl.pallas_call(kernel, in_specs=specs, out_specs=[VMEM] * len(outs), out_...]
  transfers between devices with their start and end apart: 4 -> 4, of which waited for: 2 -> 1; matrix products, arithmetic and copies ran while one was open for 0% -> 0% of each run, Pallas kernels for 0% -> 3%
where the time goes in v4:
time: 94.5 us; the launch traced here: 94.2 us
  blocking collectives  66.9 us (71%)
  starting transfers between devices  18.9 us (20%)
  Pallas kernels  5.73 us (6%)
  waiting for transfers between devices  1.9 us (2%)
    all_to_all x2, blocking collectives, copies_of_all(): return lax.all_to_all(copies, axis, 0, 0, tiled=True)  59.2 us
    ppermute x4, starting transfers between devices, swap(): return lax.ppermute(message, axis, pairs + [(j, i) for i, j in pairs])  18.9 us
    all_gather x1, blocking collectives, body(): summed = lax.all_gather(local_sum, 'ens').sum(axis=0)  7.69 us
    pallas_call x5, Pallas kernels, call(): pl.pallas_call(kernel, in_specs=specs, out_specs=[VMEM] * len(outs), out_...  5.73 us
    ppermute x4, waiting for transfers between devices, swap(): return lax.ppermute(message, axis, pairs + [(j, i) for i, j in pairs])  1.9 us
  transfers between devices with their start and end apart: 4, of which 1 were waited for; matrix products, arithmetic and copies ran while one was open for 0% of the time, Pallas kernels for 3%

profile of v4, /device:TPU:65, one launch (start us, length us, event | category | flops | bytes accessed | tf_op | source)
XLA Modules:
  0.0 94.2 jit_solution(10980198363107908742)
XLA Ops:
  0.0 1.1 %pack_rows.1 = (f32[11,2,8,128]{3,2,1,0:T(8,128)S(1)}, f32[11,2,8,128]{3,2,1,0:T(8,128)S(1)}, f32[4,16,128]{2,1,0:T(8,128)S(1)}, f32[2,2,10,16,128]{4,3,2,1,0:T(8,128)S(1)}) custom-call(s32[1]{0:T(128)} %bitcast.place_ref.row_place_ref.refs_0_, s32[2]{0:T(128)} %rows_hbm.1, f32[2,2,10,16,128]{4,3,2,1,0:T(8,128)} %u_hbm.1, f32[16,16,128]{2,1,0:T(8,128)} %table_hbm.1, ...), custom_call_target="tpu_custom_call" | custom-call | tf_op jit(solution)/shard_map/pack_rows/pallas_call | solution.py:415
  1.1 0.7 collective-permute-start
  1.8 11.6 %collective-permute-start.1 = (f32[11,2,8,128]{3,2,1,0:T(8,128)S(1)}, f32[11,2,8,128]{3,2,1,0:T(8,128)S(1)}, u32[]{:S(2)}, u32[]{:S(2)}) collective-permute-start(f32[11,2,8,128]{3,2,1,0:T(8,128)S(1)} %get-tuple-element.23), channel_id=1, source_target_pairs={{0,16},{32,48},{64,80},{96,112},{128,144},{160,176},{192,208},{224... | collective-permute-start | bytes 270344 | tf_op jit(solution)/shard_map/ppermute | solution.py:430
  13.4 0.0 collective-permute-done.by_odd_ref
  13.4 1.9 %collective-permute-done.1.by_even_ref = f32[11,2,8,128]{3,2,1,0:T(8,128)S(1)} collective-permute-done((f32[11,2,8,128]{3,2,1,0:T(8,128)S(1)}, f32[11,2,8,128]{3,2,1,0:T(8,128)S(1)}, u32[]{:S(2)}, u32[]{:S(2)}) %collective-permute-start.1) | collective-permute-done | bytes 90144 | tf_op jit(solution)/shard_map/ppermute | solution.py:430
  15.3 0.6 pack_columns.1
  15.9 0.7 collective-permute-start.2
  16.6 5.9 %collective-permute-start.3 = (f32[2,24,128]{2,1,0:T(8,128)S(1)}, f32[2,24,128]{2,1,0:T(8,128)S(1)}, u32[]{:S(2)}, u32[]{:S(2)}) collective-permute-start(f32[2,24,128]{2,1,0:T(8,128)S(1)} %get-tuple-element.26), channel_id=1, source_target_pairs={{0,2},{4,6},{8,10},{12,14},{2,0},{6,4},{10,8},{14,12},{1,3},{5,7},... | collective-permute-start | bytes 73736 | tf_op jit(solution)/shard_map/ppermute | solution.py:430
  22.5 2.4 %main_part.1 = (f32[4,10,16,128]{3,2,1,0:T(8,128)S(1)}, f32[4,10,16,128]{3,2,1,0:T(8,128)S(1)}, f32[2,10,16,128]{3,2,1,0:T(8,128)S(1)}, f32[8,128]{1,0:T(8,128)S(1)}) custom-call(s32[1]{0:T(128)} %bitcast.place_ref.row_place_ref.refs_0_, f32[2,2,10,16,128]{4,3,2,1,0:T(8,128)S(1)} %get-tuple-element.20.u_ref.refs_1_, ...), custom_call_target="tpu_custom_call" | custom-call | tf_op jit(solution)/shard_map/main_part/pallas_call | solution.py:415
  24.9 0.0 collective-permute-done.2.refs_3_
  24.9 0.0 collective-permute-done.3.refs_4_
  24.9 1.3 %strip_part.1 = (f32[10,16,128]{2,1,0:T(8,128)S(1)}, f32[10,16,128]{2,1,0:T(8,128)S(1)}, f32[16,128]{1,0:T(8,128)S(1)}) custom-call(s32[1]{0:T(128)} %bitcast.place_ref.row_place_ref.refs_0_, s32[1]{0:T(128)} %bitcast.1.column_place_ref.refs_1_, f32[11,24,128]{2,1,0:T(8,128)S(1)} %get-tuple-element.24.refs_2_, ...), custom_call_target="tpu_custom_call" | custom-call | tf_op jit(solution)/shard_map/strip_part/pallas_call | solution.py:415
  26.2 47.6 %all_to_all.17 = f32[16,1,128]{2,1,0:T(1,128)S(1)} all-to-all(f32[16,1,128]{2,1,0:T(1,128)S(1)} %bitcast.8), channel_id=1, replica_groups=mesh['group'=2,'plane'=16,'planey'=8,'ens'=2] {'plane'}, dimensions={0} | all-to-all | bytes 16384 | tf_op jit(solution)/shard_map/all_to_all | solution.py:436
  73.9 11.6 %all_to_all.18 = f32[8,1,128]{2,1,0:T(1,128)S(1)} all-to-all(f32[8,1,128]{2,1,0:T(1,128)S(1)} %broadcast_in_dim.2), channel_id=1, replica_groups=mesh['group'=2,'plane'=16,'planey'=8,'ens'=2] {'planey'}, dimensions={0} | all-to-all | bytes 8192 | tf_op jit(solution)/shard_map/all_to_all | solution.py:436
  85.4 0.4 combine.1
  85.8 7.7 %all-gather = f32[4,10,16,128]{3,2,1,0:T(8,128)S(1)} all-gather(f32[2,10,16,128]{3,2,1,0:T(8,128)S(1)} %combine.1), channel_id=2, replica_groups=mesh['group'=2,'plane'=16,'planey'=8,'ens'=2] {'ens'}, dimensions={0}, use_global_device_ids=true | all-gather | bytes 491520 | tf_op jit(solution)/shard_map/all_gather | solution.py:512
  93.6 0.7 broadcast_multiply_fusion
  (3 shorter events, 0.1 us)
Async XLA Ops:
  1.1 12.3 %collective-permute-start = (f32[11,2,8,128]{3,2,1,0:T(8,128)S(1)}, f32[11,2,8,128]{3,2,1,0:T(8,128)S(1)}, u32[]{:S(2)}, u32[]{:S(2)}) collective-permute-start(f32[11,2,8,128]{3,2,1,0:T(8,128)S(1)} %get-tuple-element.22), channel_id=1, source_target_pairs={{16,32},{48,64},{80,96},{112,128},{144,160},{176,192},{208,224},{3... | collective-permute-start | bytes 270344 | tf_op jit(solution)/shard_map/ppermute | solution.py:430
  1.8 13.6 %collective-permute-start.1 = (f32[11,2,8,128]{3,2,1,0:T(8,128)S(1)}, f32[11,2,8,128]{3,2,1,0:T(8,128)S(1)}, u32[]{:S(2)}, u32[]{:S(2)}) collective-permute-start(f32[11,2,8,128]{3,2,1,0:T(8,128)S(1)} %get-tuple-element.23), channel_id=1, source_target_pairs={{0,16},{32,48},{64,80},{96,112},{128,144},{160,176},{192,208},{224... | collective-permute-start | bytes 270344 | tf_op jit(solution)/shard_map/ppermute | solution.py:430
  15.9 9.0 %collective-permute-start.2 = (f32[2,24,128]{2,1,0:T(8,128)S(1)}, f32[2,24,128]{2,1,0:T(8,128)S(1)}, u32[]{:S(2)}, u32[]{:S(2)}) collective-permute-start(f32[2,24,128]{2,1,0:T(8,128)S(1)} %get-tuple-element.25), channel_id=1, source_target_pairs={{2,4},{6,8},{10,12},{4,2},{8,6},{12,10},{3,5},{7,9},{11,13},{5,3},... | collective-permute-start | bytes 73736 | tf_op jit(solution)/shard_map/ppermute | solution.py:430
  16.6 8.3 %collective-permute-start.3 = (f32[2,24,128]{2,1,0:T(8,128)S(1)}, f32[2,24,128]{2,1,0:T(8,128)S(1)}, u32[]{:S(2)}, u32[]{:S(2)}) collective-permute-start(f32[2,24,128]{2,1,0:T(8,128)S(1)} %get-tuple-element.26), channel_id=1, source_target_pairs={{0,2},{4,6},{8,10},{12,14},{2,0},{6,4},{10,8},{14,12},{1,3},{5,7},... | collective-permute-start | bytes 73736 | tf_op jit(solution)/shard_map/ppermute | solution.py:430

commit v5 on v4

--- a/solution.py
+++ b/solution.py
@@ -66,16 +66,57 @@
             even_ref[layer, pair] = jnp.where(odd, down, up)
 
 
-def pack_columns(
-    row_place_ref, column_place_ref, u_ref, geo_ref, by_odd_ref, by_even_ref,
-    outer_ref, strip_ref, odd_ref, even_ref,
-):
-    layers = u_ref.shape[2]
-    low = rows((8, 128)) < HALO
+def strip_tile(tiles):
+    lane = lanes((8, 128))
+    strip = jnp.zeros((8, 128), jnp.float32)
+    for k, tile in enumerate(tiles):
+        at = lane - STRIP * k
+        strip = jnp.where((at >= 4) & (at < 12), roll(tile, STRIP * k + 4, 1), strip)
+        strip = jnp.where((at >= 12) & (at < 20), roll(tile, STRIP * k + 12 - 120, 1), strip)
+    return strip
+
+
+def side_messages(strip_of, layers, swapped):
     lane = lanes((8, 128))
     used = lane < 4 * STRIP
     slot = (lane % STRIP) // HALO
-    zero = jnp.zeros((8, 128), jnp.float32)
+    for group in range(2):
+        right = jnp.zeros((8, 128), jnp.float32)
+        left = right
+        for index in range(min(GROUPED, layers + 1 - GROUPED * group)):
+            strip = strip_of(GROUPED * group + index)
+            here = used & (slot == index)
+            right = jnp.where(here, roll(strip, HALO * index - 16, 1), right)
+            left = jnp.where(here, roll(strip, HALO * index - 4, 1), left)
+        yield group, jnp.where(swapped, right, left), jnp.where(swapped, left, right)
+
+
+def pack_strips(column_place_ref, u_ref, geo_ref, own_ref, odd_ref, even_ref):
+    layers = u_ref.shape[2]
+    for layer in range(layers + 1):
+        for t in range(2):
+            at = slice(8 * t, 8 * t + 8)
+            own_ref[layer, at] = strip_tile(
+                [u_ref[k % 2, k // 2, layer, at] if layer < layers else geo_ref[k, at] for k in range(4)]
+            )
+    swapped = column_place_ref[0] % 2 == 1
+
+    def send(t, carry):
+        at = pl.ds(pl.multiple_of(8 * t, 8), 8)
+        for group, by_odd, by_even in side_messages(lambda layer: own_ref[layer, at], layers, swapped):
+            odd_ref[group, at] = by_odd
+            even_ref[group, at] = by_even
+        return carry
+
+    lax.fori_loop(0, 2, send, 0)
+
+
+def pack_columns(
+    row_place_ref, column_place_ref, own_ref, own_odd_ref, own_even_ref, by_odd_ref, by_even_ref,
+    outer_ref, strip_ref, odd_ref, even_ref,
+):
+    layers = own_ref.shape[0] - 1
+    low = rows((8, 128)) < HALO
     odd = row_place_ref[0] % 2 == 1
     for layer in range(layers + 1):
         outer = []
@@ -88,35 +129,16 @@
             outer.append(jnp.where(low, roll(above, HALO, 0), below))
         for k in range(4):
             outer_ref[layer, k] = outer[k]
-        for t in range(3):
-            strip = zero
-            for k in range(4):
-                if t == 2:
-                    tile = outer[k]
-                elif layer < layers:
-                    tile = u_ref[k % 2, k // 2, layer, 8 * t : 8 * t + 8]
-                else:
-                    tile = geo_ref[k, 8 * t : 8 * t + 8]
-                at = lane - STRIP * k
-                strip = jnp.where((at >= 4) & (at < 12), roll(tile, STRIP * k + 4, 1), strip)
-                strip = jnp.where((at >= 12) & (at < 20), roll(tile, STRIP * k + 12 - 120, 1), strip)
-            strip_ref[layer, 8 * t : 8 * t + 8] = strip
-
-    def send(t, carry):
-        at = pl.ds(pl.multiple_of(8 * t, 8), 8)
-        swapped = column_place_ref[0] % 2 == 1
-        for group in range(2):
-            right, left = zero, zero
-            for index in range(min(GROUPED, layers + 1 - GROUPED * group)):
-                strip = strip_ref[GROUPED * group + index, at]
-                here = used & (slot == index)
-                right = jnp.where(here, roll(strip, HALO * index - 16, 1), right)
-                left = jnp.where(here, roll(strip, HALO * index - 4, 1), left)
-            odd_ref[group, at] = jnp.where(swapped, right, left)
-            even_ref[group, at] = jnp.where(swapped, left, right)
-        return carry
-
-    lax.fori_loop(0, 3, send, 0)
+        strip_ref[layer, 0:16] = own_ref[layer]
+        strip_ref[layer, 16:24] = strip_tile(outer)
+    for group in range(2):
+        odd_ref[group, 0:16] = own_odd_ref[group]
+        even_ref[group, 0:16] = own_even_ref[group]
+    swapped = column_place_ref[0] % 2 == 1
+
+    for group, by_odd, by_even in side_messages(lambda layer: strip_ref[layer, 16:24], layers, swapped):
+        odd_ref[group, 16:24] = by_odd
+        even_ref[group, 16:24] = by_even
 
 
 def around_i(x):
@@ -432,10 +454,6 @@
     return swap(by_odd, 1), swap(by_even, 0)
 
 
-def copies_of_all(copies, axis):
-    return lax.all_to_all(copies, axis, 0, 0, tiled=True)
-
-
 def body(u_prior, friction_rows, friction_table, bed_fixed, ice_mask):
     members, parts, layers, rows_x, rows_y = u_prior.shape
     total_x = rows_x * lax.axis_size("plane")
@@ -460,12 +478,19 @@
         in_specs=[SMEM] + [ANY] * 5,
     )
     by_odd, by_even = swap_sides(by_odd, by_even, "plane")
+    own = call(
+        pack_strips,
+        [f32(layers + 1, rows_x, 128), f32(2, rows_x, 128), f32(2, rows_x, 128)],
+        [column_place, u_near, geo],
+        "pack_strips",
+        in_specs=[SMEM, VMEM, VMEM],
+    )
     outer, strip, side_odd, side_even = call(
         pack_columns,
         [f32(layers + 1, 4, 8, rows_y), f32(layers + 1, 24, 128), f32(2, 24, 128), f32(2, 24, 128)],
-        [row_place, column_place, u_near, geo, by_odd, by_even],
+        [row_place, column_place, *own, by_odd, by_even],
         "pack_columns",
-        in_specs=[SMEM, SMEM] + [VMEM] * 4,
+        in_specs=[SMEM, SMEM] + [VMEM] * 5,
     )
     side_odd, side_even = swap_sides(side_odd, side_even, "planey")
     residual, image, start, table = call(
@@ -493,7 +518,7 @@
         [
             f32(layers, rows_x, 128),
             f32(layers, rows_x, 128),
-            f32(lax.axis_size("plane"), 128),
+            f32(lax.axis_size("plane") * lax.axis_size("planey"), 128),
         ],
         [row_place, column_place, strip, side_odd, side_even, table],
         "strip_part",
@@ -501,9 +526,7 @@
         + [pltpu.VMEM((layers, 16, 128), jnp.float32)],
         in_specs=[SMEM, SMEM] + [VMEM] * 4,
     )
-    gathered = copies_of_all(gram, "plane")
-    line = jnp.sum(gathered, axis=0, keepdims=True)
-    gathered = copies_of_all(jnp.broadcast_to(line, (lax.axis_size("planey"), 128)), "planey")
+    gathered = lax.all_to_all(gram, ("plane", "planey"), 0, 0, tiled=True)
     (local_sum,) = call(
         combine, [f32(2, layers, rows_x, 128)], [gathered, residual, image, start, side_residual, side_image],
         "combine",

time: 94.5 us -> 92.2 us (0.976)
  blocking collectives: 66.9 us -> 65 us
    all_gather x1, blocking collectives: 7.69 us -> 6.25 us  [body(): summed = lax.all_gather(local_sum, 'ens').sum(axis=0)]
    all_to_all x2 -> x1, blocking collectives: 59.2 us -> 58.8 us  [body(): gathered = lax.all_to_all(gram, ('plane', 'planey'), 0, 0, tiled=True)]
    pallas_call x5 -> x6, Pallas kernels: 5.73 us -> 5.81 us  [call(): pl.pallas_call(kernel, in_specs=specs, out_specs=[VMEM] * len(outs), out_...]
where the time goes in v5:
time: 92.2 us; the launch traced here: 91.9 us
  blocking collectives  65 us (70%)
  starting transfers between devices  18.9 us (20%)
  Pallas kernels  5.81 us (6%)
  waiting for transfers between devices  1.46 us (2%)
    all_to_all x1, blocking collectives, body(): gathered = lax.all_to_all(gram, ('plane', 'planey'), 0, 0, tiled=True)  58.8 us
    ppermute x4, starting transfers between devices, swap(): return lax.ppermute(message, axis, pairs + [(j, i) for i, j in pairs])  18.9 us
    all_gather x1, blocking collectives, body(): summed = lax.all_gather(local_sum, 'ens').sum(axis=0)  6.25 us
    pallas_call x6, Pallas kernels, call(): pl.pallas_call(kernel, in_specs=specs, out_specs=[VMEM] * len(outs), out_...  5.81 us
  transfers between devices with their start and end apart: 4, of which 1 were waited for; matrix products, arithmetic and copies ran while one was open for 0% of the time, Pallas kernels for 3%

profile of v5, /device:TPU:65, one launch (start us, length us, event | category | flops | bytes accessed | tf_op | source)
XLA Modules:
  0.0 91.9 jit_solution(3362674331689032291)
XLA Ops:
  0.0 1.1 %pack_rows.1 = (f32[11,2,8,128]{3,2,1,0:T(8,128)S(1)}, f32[11,2,8,128]{3,2,1,0:T(8,128)S(1)}, f32[4,16,128]{2,1,0:T(8,128)S(1)}, f32[2,2,10,16,128]{4,3,2,1,0:T(8,128)S(1)}) custom-call(s32[1]{0:T(128)} %bitcast.place_ref.row_place_ref.refs_0_, s32[2]{0:T(128)} %rows_hbm.1, f32[2,2,10,16,128]{4,3,2,1,0:T(8,128)} %u_hbm.1, f32[16,16,128]{2,1,0:T(8,128)} %table_hbm.1, ...), custom_call_target="tpu_custom_call" | custom-call | tf_op jit(solution)/shard_map/pack_rows/pallas_call | solution.py:437
  1.1 0.7 collective-permute-start
  1.8 11.6 %collective-permute-start.1 = (f32[11,2,8,128]{3,2,1,0:T(8,128)S(1)}, f32[11,2,8,128]{3,2,1,0:T(8,128)S(1)}, u32[]{:S(2)}, u32[]{:S(2)}) collective-permute-start(f32[11,2,8,128]{3,2,1,0:T(8,128)S(1)} %get-tuple-element.29), channel_id=1, source_target_pairs={{0,16},{32,48},{64,80},{96,112},{128,144},{160,176},{192,208},{224... | collective-permute-start | bytes 270344 | tf_op jit(solution)/shard_map/ppermute | solution.py:452
  13.4 0.4 pack_strips.1
  13.9 0.0 collective-permute-done.by_odd_ref
  13.9 1.5 %collective-permute-done.1.by_even_ref = f32[11,2,8,128]{3,2,1,0:T(8,128)S(1)} collective-permute-done((f32[11,2,8,128]{3,2,1,0:T(8,128)S(1)}, f32[11,2,8,128]{3,2,1,0:T(8,128)S(1)}, u32[]{:S(2)}, u32[]{:S(2)}) %collective-permute-start.1) | collective-permute-done | bytes 90144 | tf_op jit(solution)/shard_map/ppermute | solution.py:452
  15.3 0.2 pack_columns.1
  15.6 0.7 collective-permute-start.2
  16.2 5.9 %collective-permute-start.3 = (f32[2,24,128]{2,1,0:T(8,128)S(1)}, f32[2,24,128]{2,1,0:T(8,128)S(1)}, u32[]{:S(2)}, u32[]{:S(2)}) collective-permute-start(f32[2,24,128]{2,1,0:T(8,128)S(1)} %get-tuple-element.32), channel_id=1, source_target_pairs={{0,2},{4,6},{8,10},{12,14},{2,0},{6,4},{10,8},{14,12},{1,3},{5,7},... | collective-permute-start | bytes 73736 | tf_op jit(solution)/shard_map/ppermute | solution.py:452
  22.1 2.4 %main_part.1 = (f32[4,10,16,128]{3,2,1,0:T(8,128)S(1)}, f32[4,10,16,128]{3,2,1,0:T(8,128)S(1)}, f32[2,10,16,128]{3,2,1,0:T(8,128)S(1)}, f32[8,128]{1,0:T(8,128)S(1)}) custom-call(s32[1]{0:T(128)} %bitcast.place_ref.row_place_ref.refs_0_, f32[2,2,10,16,128]{4,3,2,1,0:T(8,128)S(1)} %get-tuple-element.23.u_ref.refs_1_, ...), custom_call_target="tpu_custom_call" | custom-call | tf_op jit(solution)/shard_map/main_part/pallas_call | solution.py:437
  24.5 0.0 collective-permute-done.2.refs_3_
  24.5 0.0 collective-permute-done.3.refs_4_
  24.5 1.3 %strip_part.1 = (f32[10,16,128]{2,1,0:T(8,128)S(1)}, f32[10,16,128]{2,1,0:T(8,128)S(1)}, f32[128,128]{1,0:T(8,128)S(1)}) custom-call(s32[1]{0:T(128)} %bitcast.place_ref.row_place_ref.refs_0_, s32[1]{0:T(128)} %bitcast.1.column_place_ref.refs_1_, f32[11,24,128]{2,1,0:T(8,128)S(1)} %get-tuple-element.30.refs_2_, ...), custom_call_target="tpu_custom_call" | custom-call | tf_op jit(solution)/shard_map/strip_part/pallas_call | solution.py:437
  25.8 58.8 %all_to_all.11 = f32[128,1,128]{2,1,0:T(1,128)S(1)} all-to-all(f32[128,1,128]{2,1,0:T(1,128)S(1)} %bitcast.8), channel_id=1, replica_groups=mesh['group'=2,'plane'=16,'planey'=8,'ens'=2] {'plane','planey'}, dimensions={0} | all-to-all | bytes 131072 | tf_op jit(solution)/shard_map/all_to_all | solution.py:529
  84.6 0.4 combine.1
  85.0 6.2 %all-gather = f32[4,10,16,128]{3,2,1,0:T(8,128)S(1)} all-gather(f32[2,10,16,128]{3,2,1,0:T(8,128)S(1)} %combine.1), channel_id=2, replica_groups=mesh['group'=2,'plane'=16,'planey'=8,'ens'=2] {'ens'}, dimensions={0}, use_global_device_ids=true | all-gather | bytes 491520 | tf_op jit(solution)/shard_map/all_gather | solution.py:535
  91.3 0.7 broadcast_multiply_fusion
  (1 shorter events, 0.0 us)
Async XLA Ops:
  1.1 12.8 %collective-permute-start = (f32[11,2,8,128]{3,2,1,0:T(8,128)S(1)}, f32[11,2,8,128]{3,2,1,0:T(8,128)S(1)}, u32[]{:S(2)}, u32[]{:S(2)}) collective-permute-start(f32[11,2,8,128]{3,2,1,0:T(8,128)S(1)} %get-tuple-element.28), channel_id=1, source_target_pairs={{16,32},{48,64},{80,96},{112,128},{144,160},{176,192},{208,224},{3... | collective-permute-start | bytes 270344 | tf_op jit(solution)/shard_map/ppermute | solution.py:452
  1.8 13.6 %collective-permute-start.1 = (f32[11,2,8,128]{3,2,1,0:T(8,128)S(1)}, f32[11,2,8,128]{3,2,1,0:T(8,128)S(1)}, u32[]{:S(2)}, u32[]{:S(2)}) collective-permute-start(f32[11,2,8,128]{3,2,1,0:T(8,128)S(1)} %get-tuple-element.29), channel_id=1, source_target_pairs={{0,16},{32,48},{64,80},{96,112},{128,144},{160,176},{192,208},{224... | collective-permute-start | bytes 270344 | tf_op jit(solution)/shard_map/ppermute | solution.py:452
  15.6 9.0 %collective-permute-start.2 = (f32[2,24,128]{2,1,0:T(8,128)S(1)}, f32[2,24,128]{2,1,0:T(8,128)S(1)}, u32[]{:S(2)}, u32[]{:S(2)}) collective-permute-start(f32[2,24,128]{2,1,0:T(8,128)S(1)} %get-tuple-element.31), channel_id=1, source_target_pairs={{2,4},{6,8},{10,12},{4,2},{8,6},{12,10},{3,5},{7,9},{11,13},{5,3},... | collective-permute-start | bytes 73736 | tf_op jit(solution)/shard_map/ppermute | solution.py:452
  16.2 8.3 %collective-permute-start.3 = (f32[2,24,128]{2,1,0:T(8,128)S(1)}, f32[2,24,128]{2,1,0:T(8,128)S(1)}, u32[]{:S(2)}, u32[]{:S(2)}) collective-permute-start(f32[2,24,128]{2,1,0:T(8,128)S(1)} %get-tuple-element.32), channel_id=1, source_target_pairs={{0,2},{4,6},{8,10},{12,14},{2,0},{6,4},{10,8},{14,12},{1,3},{5,7},... | collective-permute-start | bytes 73736 | tf_op jit(solution)/shard_map/ppermute | solution.py:452

commit v6 on v5

--- a/solution.py
+++ b/solution.py
@@ -31,7 +31,7 @@
 
 
 def pack_rows(
-    place_ref, rows_hbm, u_hbm, table_hbm, bed_hbm, mask_hbm,
+    row_turn_ref, rows_hbm, u_hbm, table_hbm, bed_hbm, mask_hbm,
     odd_ref, even_ref, geo_ref, u_ref, rows_ref, table_ref, ints_ref, sems,
 ):
     layers = u_ref.shape[2]
@@ -52,7 +52,7 @@
     for s in range(2):
         geo_ref[2 + s] = table_ref[rows_ref[s]]
     low = rows((8, 128)) < HALO
-    odd = place_ref[0] % 2 == 1
+    odd = row_turn_ref[0] % 2 == 1
     for layer in range(layers + 1):
         for pair in range(2):
             tiles = [
@@ -112,12 +112,12 @@
 
 
 def pack_columns(
-    row_place_ref, column_place_ref, own_ref, own_odd_ref, own_even_ref, by_odd_ref, by_even_ref,
+    row_turn_ref, column_place_ref, own_ref, own_odd_ref, own_even_ref, by_odd_ref, by_even_ref,
     outer_ref, strip_ref, odd_ref, even_ref,
 ):
     layers = own_ref.shape[0] - 1
     low = rows((8, 128)) < HALO
-    odd = row_place_ref[0] % 2 == 1
+    odd = row_turn_ref[0] % 2 == 1
     for layer in range(layers + 1):
         outer = []
         for pair in range(2):
@@ -393,19 +393,18 @@
     shape = (8, 128)
     lane = lanes(shape)
     total = jnp.broadcast_to(jnp.sum(gram_ref[...], axis=0, keepdims=True), shape)
-    rr = total
-    ra = roll(total, -2, 1)
-    aa = roll(total, -4, 1)
-    ab = roll(total, -6, 1)
-    first = rr / ra
-    norm_next = rr - 2.0 * first * ra + first * first * aa
-    growth = 1.0 + norm_next / rr
-    curve = growth * growth * ra - 2.0 * growth * first * aa + first * first * ab
-    second = norm_next / curve
-    residual_part = first + second * growth
-    image_part = second * first
-    ks = [jnp.broadcast_to(residual_part[:, s : s + 1], shape) for s in range(2)]
-    ms = [jnp.broadcast_to(image_part[:, s : s + 1], shape) for s in range(2)]
+    ks, ms = [], []
+    for s in range(2):
+        rr, ra, aa, ab = (
+            jnp.broadcast_to(total[:, q : q + 1], shape) for q in (s, 2 + s, 4 + s, 6 + s)
+        )
+        first = rr / ra
+        norm_next = rr - 2.0 * first * ra + first * first * aa
+        growth = 1.0 + norm_next / rr
+        curve = growth * growth * ra - 2.0 * growth * first * aa + first * first * ab
+        second = norm_next / curve
+        ks.append(first + second * growth)
+        ms.append(second * first)
     odd = (lane // STRIP) % 2 == 1
     k_side = jnp.where(odd, ks[1], ks[0])
     m_side = jnp.where(odd, ms[1], ms[0])
@@ -413,14 +412,15 @@
         for t in range(2):
             at = slice(8 * t, 8 * t + 8)
             side = k_side * side_residual_ref[z, at] - m_side * side_image_ref[z, at]
-            side = side + roll(side, -STRIP, 1)
             for c in range(2):
                 step = ks[0] * residual_ref[2 * c, z, at] - ms[0] * image_ref[2 * c, z, at]
                 step = step + ks[1] * residual_ref[2 * c + 1, z, at]
                 step = step - ms[1] * image_ref[2 * c + 1, z, at]
                 base = 2 * STRIP * c
-                step = jnp.where(lane < HALO, roll(side, -(base + 4), 1), step)
-                step = jnp.where(lane >= 128 - HALO, roll(side, 124 - base - 16, 1), step)
+                left = roll(side, -(base + 4), 1) + roll(side, -(base + STRIP + 4), 1)
+                right = roll(side, 124 - base - 16, 1) + roll(side, 124 - base - STRIP - 16, 1)
+                step = jnp.where(lane < HALO, left, step)
+                step = jnp.where(lane >= 128 - HALO, right, step)
                 out_ref[c, z, at] = start_ref[c, z, at] + step
 
 
@@ -444,12 +444,17 @@
     )(*ins)
 
 
-def swap_sides(by_odd, by_even, axis):
+def swap_sides(by_odd, by_even, axis, other="ens"):
     count = lax.axis_size(axis)
+    others = lax.axis_size(other) if other else 1
 
     def swap(message, first):
-        pairs = [(i, i + 1) for i in range(first, count - 1, 2)]
-        return lax.ppermute(message, axis, pairs + [(j, i) for i, j in pairs])
+        pairs = []
+        for o in range(others):
+            for i in range((first + o) % 2, count - 1, 2):
+                low, high = i * others + o, (i + 1) * others + o
+                pairs += [(low, high), (high, low)]
+        return lax.ppermute(message, (axis, other) if other else axis, pairs)
 
     return swap(by_odd, 1), swap(by_even, 0)
 
@@ -458,6 +463,7 @@
     members, parts, layers, rows_x, rows_y = u_prior.shape
     total_x = rows_x * lax.axis_size("plane")
     row_place = lax.axis_index("plane").reshape(1)
+    row_turn = row_place + lax.axis_index("ens")
     column_place = lax.axis_index("planey").reshape(1)
     by_odd, by_even, geo, u_near = call(
         pack_rows,
@@ -467,7 +473,7 @@
             f32(4, rows_x, rows_y),
             f32(*u_prior.shape),
         ],
-        [row_place, friction_rows, u_prior, friction_table, bed_fixed, ice_mask],
+        [row_turn, friction_rows, u_prior, friction_table, bed_fixed, ice_mask],
         "pack_rows",
         scratch=[
             pltpu.SMEM(friction_rows.shape, jnp.int32),
@@ -488,11 +494,11 @@
     outer, strip, side_odd, side_even = call(
         pack_columns,
         [f32(layers + 1, 4, 8, rows_y), f32(layers + 1, 24, 128), f32(2, 24, 128), f32(2, 24, 128)],
-        [row_place, column_place, *own, by_odd, by_even],
+        [row_turn, column_place, *own, by_odd, by_even],
         "pack_columns",
         in_specs=[SMEM, SMEM] + [VMEM] * 5,
     )
-    side_odd, side_even = swap_sides(side_odd, side_even, "planey")
+    side_odd, side_even = swap_sides(side_odd, side_even, "planey", None)
     residual, image, start, table = call(
         lambda *refs: main_part(*refs, total_x=total_x),
         [

time: 92.2 us -> 92.2 us (level)
  blocking collectives: 65 us -> 70.8 us
  starting transfers between devices: 18.9 us -> 13.8 us
    all_to_all x1, blocking collectives: 58.8 us -> 66.2 us  [body(): gathered = lax.all_to_all(gram, ('plane', 'planey'), 0, 0, tiled=True)]
    ppermute x4, starting transfers between devices: 18.9 us -> 13.8 us  [swap(): return lax.ppermute(message, (axis, other) if other else axis, pairs)]
    all_gather x1, blocking collectives: 6.25 us -> 4.53 us  [body(): summed = lax.all_gather(local_sum, 'ens').sum(axis=0)]
where the time goes in v6:
time: 92.2 us; the launch traced here: 91.9 us
  blocking collectives  70.8 us (77%)
  starting transfers between devices  13.8 us (15%)
  Pallas kernels  5.75 us (6%)
    all_to_all x1, blocking collectives, body(): gathered = lax.all_to_all(gram, ('plane', 'planey'), 0, 0, tiled=True)  66.2 us
    ppermute x4, starting transfers between devices, swap(): return lax.ppermute(message, (axis, other) if other else axis, pairs)  13.8 us
    pallas_call x6, Pallas kernels, call(): pl.pallas_call(kernel, in_specs=specs, out_specs=[VMEM] * len(outs), out_...  5.75 us
    all_gather x1, blocking collectives, body(): summed = lax.all_gather(local_sum, 'ens').sum(axis=0)  4.53 us
  transfers between devices with their start and end apart: 4, of which 1 were waited for; matrix products, arithmetic and copies ran while one was open for 0% of the time, Pallas kernels for 3%

profile of v6, /device:TPU:65, one launch (start us, length us, event | category | flops | bytes accessed | tf_op | source)
XLA Modules:
  0.0 91.9 jit_solution(16534222453326132303)
XLA Ops:
  0.0 1.1 %pack_rows.1 = (f32[11,2,8,128]{3,2,1,0:T(8,128)S(1)}, f32[11,2,8,128]{3,2,1,0:T(8,128)S(1)}, f32[4,16,128]{2,1,0:T(8,128)S(1)}, f32[2,2,10,16,128]{4,3,2,1,0:T(8,128)S(1)}) custom-call(s32[1]{0:T(128)S(6)} %add.7.row_turn_ref, s32[2]{0:T(128)} %rows_hbm.1, f32[2,2,10,16,128]{4,3,2,1,0:T(8,128)} %u_hbm.1, f32[16,16,128]{2,1,0:T(8,128)} %table_hbm.1, ...), custom_call_target="tpu_custom_call" | custom-call | tf_op jit(solution)/shard_map/pack_rows/pallas_call | solution.py:437
  1.1 6.6 %collective-permute-start = (f32[11,2,8,128]{3,2,1,0:T(8,128)S(1)}, f32[11,2,8,128]{3,2,1,0:T(8,128)S(1)}, u32[]{:S(2)}, u32[]{:S(2)}) collective-permute-start(f32[11,2,8,128]{3,2,1,0:T(8,128)S(1)} %get-tuple-element.28), channel_id=1, source_target_pairs={{16,32},{32,16},{48,64},{64,48},{80,96},{96,80},{112,128},{128,112... | collective-permute-start | bytes 270344 | tf_op jit(solution)/shard_map/ppermute | solution.py:457
  7.7 0.7 collective-permute-start.1
  8.3 0.4 pack_strips.1
  8.8 0.8 collective-permute-done.by_odd_ref
  9.6 0.0 collective-permute-done.1.by_even_ref
  9.6 0.2 pack_columns.1
  9.8 0.7 collective-permute-start.2
  10.5 5.9 %collective-permute-start.3 = (f32[2,24,128]{2,1,0:T(8,128)S(1)}, f32[2,24,128]{2,1,0:T(8,128)S(1)}, u32[]{:S(2)}, u32[]{:S(2)}) collective-permute-start(f32[2,24,128]{2,1,0:T(8,128)S(1)} %get-tuple-element.32), channel_id=1, source_target_pairs={{0,2},{2,0},{4,6},{6,4},{8,10},{10,8},{12,14},{14,12},{1,3},{3,1},... | collective-permute-start | bytes 73736 | tf_op jit(solution)/shard_map/ppermute | solution.py:457
  16.4 2.4 %main_part.1 = (f32[4,10,16,128]{3,2,1,0:T(8,128)S(1)}, f32[4,10,16,128]{3,2,1,0:T(8,128)S(1)}, f32[2,10,16,128]{3,2,1,0:T(8,128)S(1)}, f32[8,128]{1,0:T(8,128)S(1)}) custom-call(s32[1]{0:T(128)} %bitcast.refs_0_, f32[2,2,10,16,128]{4,3,2,1,0:T(8,128)S(1)} %get-tuple-element.23.u_ref.refs_1_, f32[4,16,128]{2,1,0:T(8,128)S(1)} %get-tuple-element.24.geo_ref.refs_2_, ...), custom_call_target="tpu_custom_call" | custom-call | tf_op jit(solution)/shard_map/main_part/pallas_call | solution.py:437
  18.8 0.0 collective-permute-done.2.refs_3_
  18.8 0.0 collective-permute-done.3.refs_4_
  18.8 1.3 %strip_part.1 = (f32[10,16,128]{2,1,0:T(8,128)S(1)}, f32[10,16,128]{2,1,0:T(8,128)S(1)}, f32[128,128]{1,0:T(8,128)S(1)}) custom-call(s32[1]{0:T(128)} %bitcast.refs_0_, s32[1]{0:T(128)} %bitcast.1.column_place_ref.refs_1_, f32[11,24,128]{2,1,0:T(8,128)S(1)} %get-tuple-element.30.refs_2_, f32[2,24,128]{2,1,0:T(8,128)S(1)} %collective-permute-done.2.refs_3_, ...), custom_call_target="tpu_custom_call" | custom-call | tf_op jit(solution)/shard_map/strip_part/pallas_call | solution.py:437
  20.1 66.2 %all_to_all.11 = f32[128,1,128]{2,1,0:T(1,128)S(1)} all-to-all(f32[128,1,128]{2,1,0:T(1,128)S(1)} %bitcast.9), channel_id=1, replica_groups=mesh['group'=2,'plane'=16,'planey'=8,'ens'=2] {'plane','planey'}, dimensions={0} | all-to-all | bytes 131072 | tf_op jit(solution)/shard_map/all_to_all | solution.py:535
  86.3 0.4 combine.1
  86.7 4.5 %all-gather = f32[4,10,16,128]{3,2,1,0:T(8,128)S(1)} all-gather(f32[2,10,16,128]{3,2,1,0:T(8,128)S(1)} %combine.1), channel_id=2, replica_groups=mesh['group'=2,'plane'=16,'planey'=8,'ens'=2] {'ens'}, dimensions={0}, use_global_device_ids=true | all-gather | bytes 491520 | tf_op jit(solution)/shard_map/all_gather | solution.py:541
  91.2 0.7 broadcast_multiply_fusion
  (1 shorter events, 0.0 us)
Async XLA Ops:
  1.1 8.5 %collective-permute-start = (f32[11,2,8,128]{3,2,1,0:T(8,128)S(1)}, f32[11,2,8,128]{3,2,1,0:T(8,128)S(1)}, u32[]{:S(2)}, u32[]{:S(2)}) collective-permute-start(f32[11,2,8,128]{3,2,1,0:T(8,128)S(1)} %get-tuple-element.28), channel_id=1, source_target_pairs={{16,32},{32,16},{48,64},{64,48},{80,96},{96,80},{112,128},{128,112... | collective-permute-start | bytes 270344 | tf_op jit(solution)/shard_map/ppermute | solution.py:457
  7.7 1.9 %collective-permute-start.1 = (f32[11,2,8,128]{3,2,1,0:T(8,128)S(1)}, f32[11,2,8,128]{3,2,1,0:T(8,128)S(1)}, u32[]{:S(2)}, u32[]{:S(2)}) collective-permute-start(f32[11,2,8,128]{3,2,1,0:T(8,128)S(1)} %get-tuple-element.29), channel_id=1, source_target_pairs={{0,16},{16,0},{32,48},{48,32},{64,80},{80,64},{96,112},{112,96},{1... | collective-permute-start | bytes 270344 | tf_op jit(solution)/shard_map/ppermute | solution.py:457
  9.8 9.0 %collective-permute-start.2 = (f32[2,24,128]{2,1,0:T(8,128)S(1)}, f32[2,24,128]{2,1,0:T(8,128)S(1)}, u32[]{:S(2)}, u32[]{:S(2)}) collective-permute-start(f32[2,24,128]{2,1,0:T(8,128)S(1)} %get-tuple-element.31), channel_id=1, source_target_pairs={{2,4},{4,2},{6,8},{8,6},{10,12},{12,10},{3,5},{5,3},{7,9},{9,7},{1... | collective-permute-start | bytes 73736 | tf_op jit(solution)/shard_map/ppermute | solution.py:457
  10.5 8.3 %collective-permute-start.3 = (f32[2,24,128]{2,1,0:T(8,128)S(1)}, f32[2,24,128]{2,1,0:T(8,128)S(1)}, u32[]{:S(2)}, u32[]{:S(2)}) collective-permute-start(f32[2,24,128]{2,1,0:T(8,128)S(1)} %get-tuple-element.32), channel_id=1, source_target_pairs={{0,2},{2,0},{4,6},{6,4},{8,10},{10,8},{12,14},{14,12},{1,3},{3,1},... | collective-permute-start | bytes 73736 | tf_op jit(solution)/shard_map/ppermute | solution.py:457

commit v7 on v6

--- a/solution.py
+++ b/solution.py
@@ -339,9 +339,18 @@
     weight_j = jnp.where(low, MAIN_J[0], MAIN_J[1])
 
     for z in range(layers):
-        found = viscosity(
-            lambda y: wide_ref[y], lambda y: roll(wide_ref[y], -2 * STRIP, 1), z, layers, mask
-        )
+        wide = wide_ref[z]
+        slope_i = roll(wide, -1, 0) - roll(wide, 1, 0)
+        slope_j = roll(wide, -1, 1) - roll(wide, 1, 1)
+        rise = difference(lambda y: wide_ref[y], z, layers)
+        rise = rise * rise
+        stretch = jnp.where(low, slope_i, slope_j)
+        shear = jnp.where(low, slope_j, slope_i)
+        stretch_y = roll(stretch, -2 * STRIP, 1)
+        shear = shear + roll(shear, -2 * STRIP, 1)
+        strain = stretch * stretch + stretch_y * (stretch_y + stretch)
+        strain = strain + 0.25 * (shear * shear + (rise + roll(rise, -2 * STRIP, 1)))
+        found = mask * jnp.exp(jnp.log(0.25 * strain + 0.1) * (-1.0 / 6.0))
         roots_ref[z] = jnp.where(low, found, roll(found, 2 * STRIP, 1))
     for z in range(layers):
         centre = with_neighbours(lambda y: roots_ref[y], z, layers)

time: 92.2 us -> 91.9 us (level)
  no operation moved by 1% of the time
where the time goes in v7:
time: 91.9 us; the launch traced here: 91.6 us
  blocking collectives  70.8 us (77%)
  starting transfers between devices  13.8 us (15%)
  Pallas kernels  5.45 us (6%)
    all_to_all x1, blocking collectives, body(): gathered = lax.all_to_all(gram, ('plane', 'planey'), 0, 0, tiled=True)  66.2 us
    ppermute x4, starting transfers between devices, swap(): return lax.ppermute(message, (axis, other) if other else axis, pairs)  13.8 us
    pallas_call x6, Pallas kernels, call(): pl.pallas_call(kernel, in_specs=specs, out_specs=[VMEM] * len(outs), out_...  5.45 us
    all_gather x1, blocking collectives, body(): summed = lax.all_gather(local_sum, 'ens').sum(axis=0)  4.53 us
  transfers between devices with their start and end apart: 4, of which 1 were waited for; matrix products, arithmetic and copies ran while one was open for 0% of the time, Pallas kernels for 3%

profile of v7, /device:TPU:65, one launch (start us, length us, event | category | flops | bytes accessed | tf_op | source)
XLA Modules:
  0.0 91.6 jit_solution(14926204339376920370)
XLA Ops:
  0.0 1.1 %pack_rows.1 = (f32[11,2,8,128]{3,2,1,0:T(8,128)S(1)}, f32[11,2,8,128]{3,2,1,0:T(8,128)S(1)}, f32[4,16,128]{2,1,0:T(8,128)S(1)}, f32[2,2,10,16,128]{4,3,2,1,0:T(8,128)S(1)}) custom-call(s32[1]{0:T(128)S(6)} %add.7.row_turn_ref, s32[2]{0:T(128)} %rows_hbm.1, f32[2,2,10,16,128]{4,3,2,1,0:T(8,128)} %u_hbm.1, f32[16,16,128]{2,1,0:T(8,128)} %table_hbm.1, ...), custom_call_target="tpu_custom_call" | custom-call | tf_op jit(solution)/shard_map/pack_rows/pallas_call | solution.py:446
  1.1 6.6 %collective-permute-start = (f32[11,2,8,128]{3,2,1,0:T(8,128)S(1)}, f32[11,2,8,128]{3,2,1,0:T(8,128)S(1)}, u32[]{:S(2)}, u32[]{:S(2)}) collective-permute-start(f32[11,2,8,128]{3,2,1,0:T(8,128)S(1)} %get-tuple-element.28), channel_id=1, source_target_pairs={{16,32},{32,16},{48,64},{64,48},{80,96},{96,80},{112,128},{128,112... | collective-permute-start | bytes 270344 | tf_op jit(solution)/shard_map/ppermute | solution.py:466
  7.7 0.7 collective-permute-start.1
  8.3 0.4 pack_strips.1
  8.8 0.8 collective-permute-done.by_odd_ref
  9.6 0.0 collective-permute-done.1.by_even_ref
  9.6 0.2 pack_columns.1
  9.8 0.7 collective-permute-start.2
  10.5 5.9 %collective-permute-start.3 = (f32[2,24,128]{2,1,0:T(8,128)S(1)}, f32[2,24,128]{2,1,0:T(8,128)S(1)}, u32[]{:S(2)}, u32[]{:S(2)}) collective-permute-start(f32[2,24,128]{2,1,0:T(8,128)S(1)} %get-tuple-element.32), channel_id=1, source_target_pairs={{0,2},{2,0},{4,6},{6,4},{8,10},{10,8},{12,14},{14,12},{1,3},{3,1},... | collective-permute-start | bytes 73736 | tf_op jit(solution)/shard_map/ppermute | solution.py:466
  16.4 2.4 %main_part.1 = (f32[4,10,16,128]{3,2,1,0:T(8,128)S(1)}, f32[4,10,16,128]{3,2,1,0:T(8,128)S(1)}, f32[2,10,16,128]{3,2,1,0:T(8,128)S(1)}, f32[8,128]{1,0:T(8,128)S(1)}) custom-call(s32[1]{0:T(128)} %bitcast.refs_0_, f32[2,2,10,16,128]{4,3,2,1,0:T(8,128)S(1)} %get-tuple-element.23.u_ref.refs_1_, f32[4,16,128]{2,1,0:T(8,128)S(1)} %get-tuple-element.24.geo_ref.refs_2_, ...), custom_call_target="tpu_custom_call" | custom-call | tf_op jit(solution)/shard_map/main_part/pallas_call | solution.py:446
  18.8 0.0 collective-permute-done.2.refs_3_
  18.8 0.0 collective-permute-done.3.refs_4_
  18.8 1.0 %strip_part.1 = (f32[10,16,128]{2,1,0:T(8,128)S(1)}, f32[10,16,128]{2,1,0:T(8,128)S(1)}, f32[128,128]{1,0:T(8,128)S(1)}) custom-call(s32[1]{0:T(128)} %bitcast.refs_0_, s32[1]{0:T(128)} %bitcast.1.column_place_ref.refs_1_, f32[11,24,128]{2,1,0:T(8,128)S(1)} %get-tuple-element.30.refs_2_, f32[2,24,128]{2,1,0:T(8,128)S(1)} %collective-permute-done.2.refs_3_, ...), custom_call_target="tpu_custom_call" | custom-call | tf_op jit(solution)/shard_map/strip_part/pallas_call | solution.py:446
  19.8 66.2 %all_to_all.11 = f32[128,1,128]{2,1,0:T(1,128)S(1)} all-to-all(f32[128,1,128]{2,1,0:T(1,128)S(1)} %bitcast.9), channel_id=1, replica_groups=mesh['group'=2,'plane'=16,'planey'=8,'ens'=2] {'plane','planey'}, dimensions={0} | all-to-all | bytes 131072 | tf_op jit(solution)/shard_map/all_to_all | solution.py:544
  86.0 0.4 combine.1
  86.4 4.5 %all-gather = f32[4,10,16,128]{3,2,1,0:T(8,128)S(1)} all-gather(f32[2,10,16,128]{3,2,1,0:T(8,128)S(1)} %combine.1), channel_id=2, replica_groups=mesh['group'=2,'plane'=16,'planey'=8,'ens'=2] {'ens'}, dimensions={0}, use_global_device_ids=true | all-gather | bytes 491520 | tf_op jit(solution)/shard_map/all_gather | solution.py:550
  90.9 0.7 broadcast_multiply_fusion
  (1 shorter events, 0.0 us)
Async XLA Ops:
  1.1 8.5 %collective-permute-start = (f32[11,2,8,128]{3,2,1,0:T(8,128)S(1)}, f32[11,2,8,128]{3,2,1,0:T(8,128)S(1)}, u32[]{:S(2)}, u32[]{:S(2)}) collective-permute-start(f32[11,2,8,128]{3,2,1,0:T(8,128)S(1)} %get-tuple-element.28), channel_id=1, source_target_pairs={{16,32},{32,16},{48,64},{64,48},{80,96},{96,80},{112,128},{128,112... | collective-permute-start | bytes 270344 | tf_op jit(solution)/shard_map/ppermute | solution.py:466
  7.7 1.9 %collective-permute-start.1 = (f32[11,2,8,128]{3,2,1,0:T(8,128)S(1)}, f32[11,2,8,128]{3,2,1,0:T(8,128)S(1)}, u32[]{:S(2)}, u32[]{:S(2)}) collective-permute-start(f32[11,2,8,128]{3,2,1,0:T(8,128)S(1)} %get-tuple-element.29), channel_id=1, source_target_pairs={{0,16},{16,0},{32,48},{48,32},{64,80},{80,64},{96,112},{112,96},{1... | collective-permute-start | bytes 270344 | tf_op jit(solution)/shard_map/ppermute | solution.py:466
  9.8 9.0 %collective-permute-start.2 = (f32[2,24,128]{2,1,0:T(8,128)S(1)}, f32[2,24,128]{2,1,0:T(8,128)S(1)}, u32[]{:S(2)}, u32[]{:S(2)}) collective-permute-start(f32[2,24,128]{2,1,0:T(8,128)S(1)} %get-tuple-element.31), channel_id=1, source_target_pairs={{2,4},{4,2},{6,8},{8,6},{10,12},{12,10},{3,5},{5,3},{7,9},{9,7},{1... | collective-permute-start | bytes 73736 | tf_op jit(solution)/shard_map/ppermute | solution.py:466
  10.5 8.3 %collective-permute-start.3 = (f32[2,24,128]{2,1,0:T(8,128)S(1)}, f32[2,24,128]{2,1,0:T(8,128)S(1)}, u32[]{:S(2)}, u32[]{:S(2)}) collective-permute-start(f32[2,24,128]{2,1,0:T(8,128)S(1)} %get-tuple-element.32), channel_id=1, source_target_pairs={{0,2},{2,0},{4,6},{6,4},{8,10},{10,8},{12,14},{14,12},{1,3},{3,1},... | collective-permute-start | bytes 73736 | tf_op jit(solution)/shard_map/ppermute | solution.py:466

commit v8 on v7

--- a/solution.py
+++ b/solution.py
@@ -9,6 +9,8 @@
 HALO = 4
 STRIP = 24
 GROUPED = STRIP // HALO
+SECOND = 64
+STARTS = (0, STRIP, SECOND, SECOND + STRIP)
 MAIN_I = (0.25, 0.125)
 MAIN_J = (0.125, 0.25)
 
@@ -70,16 +72,16 @@
     lane = lanes((8, 128))
     strip = jnp.zeros((8, 128), jnp.float32)
     for k, tile in enumerate(tiles):
-        at = lane - STRIP * k
-        strip = jnp.where((at >= 4) & (at < 12), roll(tile, STRIP * k + 4, 1), strip)
-        strip = jnp.where((at >= 12) & (at < 20), roll(tile, STRIP * k + 12 - 120, 1), strip)
+        at = lane - STARTS[k]
+        strip = jnp.where((at >= 4) & (at < 12), roll(tile, STARTS[k] + 4, 1), strip)
+        strip = jnp.where((at >= 12) & (at < 20), roll(tile, STARTS[k] + 12 - 120, 1), strip)
     return strip
 
 
 def side_messages(strip_of, layers, swapped):
     lane = lanes((8, 128))
-    used = lane < 4 * STRIP
-    slot = (lane % STRIP) // HALO
+    used = lane % SECOND < 2 * STRIP
+    slot = (lane % SECOND % STRIP) // HALO
     for group in range(2):
         right = jnp.zeros((8, 128), jnp.float32)
         left = right
@@ -305,10 +307,10 @@
     layers = strip_ref.shape[0] - 1
     shape = (24, 128)
     lane = lanes(shape)
-    used = lane < 4 * STRIP
-    place = lane % STRIP
-    number = lane // STRIP
-    low = lane < 2 * STRIP
+    used = lane % SECOND < 2 * STRIP
+    place = lane % SECOND % STRIP
+    number = jnp.where(used, 2 * (lane // SECOND) + lane % SECOND // STRIP, -1)
+    low = lane < SECOND
 
     geo = None
     odd = column_place_ref[0] % 2 == 1
@@ -327,12 +329,12 @@
     def spread(to):
         result = jnp.zeros(shape, jnp.float32)
         for k in range(4):
-            result = jnp.where(number == k, roll(geo, STRIP * (k - to), 1), result)
+            result = jnp.where(number == k, roll(geo, STARTS[k] - STARTS[to], 1), result)
         return result
 
     mask = spread(0)
     bare = 1.0 - mask
-    friction = mask * jnp.where(low, roll(geo, -2 * STRIP, 1), geo) + bare
+    friction = mask * jnp.where(low, roll(geo, -SECOND, 1), geo) + bare
     force_x, force_y = forces(mask, spread(1), row_place_ref[0] * 16, total_x)
     force = jnp.where(low, force_x, force_y)
     weight_i = jnp.where(low, MAIN_I[0], MAIN_I[1])
@@ -346,12 +348,11 @@
         rise = rise * rise
         stretch = jnp.where(low, slope_i, slope_j)
         shear = jnp.where(low, slope_j, slope_i)
-        stretch_y = roll(stretch, -2 * STRIP, 1)
-        shear = shear + roll(shear, -2 * STRIP, 1)
+        stretch_y = roll(stretch, SECOND, 1)
+        shear = shear + roll(shear, SECOND, 1)
         strain = stretch * stretch + stretch_y * (stretch_y + stretch)
-        strain = strain + 0.25 * (shear * shear + (rise + roll(rise, -2 * STRIP, 1)))
-        found = mask * jnp.exp(jnp.log(0.25 * strain + 0.1) * (-1.0 / 6.0))
-        roots_ref[z] = jnp.where(low, found, roll(found, 2 * STRIP, 1))
+        strain = strain + 0.25 * (shear * shear + (rise + roll(rise, SECOND, 1)))
+        roots_ref[z] = mask * jnp.exp(jnp.log(0.25 * strain + 0.1) * (-1.0 / 6.0))
     for z in range(layers):
         centre = with_neighbours(lambda y: roots_ref[y], z, layers)
         centre = centre + weight_i * around_i(centre)
@@ -382,13 +383,13 @@
 
     lane8 = lanes((8, 128))
     row8 = rows((8, 128))
-    spot = lane8 % STRIP
-    edge = (lane8 < 4 * STRIP) & (((spot >= 4) & (spot < 8)) | ((spot >= 16) & (spot < 20)))
+    spot = lane8 % SECOND % STRIP
+    edge = (lane8 % SECOND < 2 * STRIP) & (((spot >= 4) & (spot < 8)) | ((spot >= 16) & (spot < 20)))
     table = table_ref[...]
     for g in range(4):
         line = jnp.broadcast_to(jnp.sum(totals[g], axis=0, keepdims=True), (8, 128))
         for s in range(2):
-            here = edge & ((lane8 // STRIP) % 2 == s) & (row8 == 2 * g + s)
+            here = edge & (lane8 % SECOND // STRIP == s) & (row8 == 2 * g + s)
             table = table + jnp.where(here, line, 0.0)
     table = jnp.sum(table, axis=1, keepdims=True)
     line = jnp.sum(jnp.where(lane8 == row8, table, 0.0), axis=0, keepdims=True)
@@ -414,7 +415,7 @@
         second = norm_next / curve
         ks.append(first + second * growth)
         ms.append(second * first)
-    odd = (lane // STRIP) % 2 == 1
+    odd = lane % SECOND // STRIP == 1
     k_side = jnp.where(odd, ks[1], ks[0])
     m_side = jnp.where(odd, ms[1], ms[0])
     for z in range(layers):
@@ -425,7 +426,7 @@
                 step = ks[0] * residual_ref[2 * c, z, at] - ms[0] * image_ref[2 * c, z, at]
                 step = step + ks[1] * residual_ref[2 * c + 1, z, at]
                 step = step - ms[1] * image_ref[2 * c + 1, z, at]
-                base = 2 * STRIP * c
+                base = SECOND * c
                 left = roll(side, -(base + 4), 1) + roll(side, -(base + STRIP + 4), 1)
                 right = roll(side, 124 - base - 16, 1) + roll(side, 124 - base - STRIP - 16, 1)
                 step = jnp.where(lane < HALO, left, step)

time: 91.9 us -> 91.8 us (level)
  no operation moved by 1% of the time
where the time goes in v8:
time: 91.8 us; the launch traced here: 91.6 us
  blocking collectives  70.8 us (77%)
  starting transfers between devices  13.8 us (15%)
  Pallas kernels  5.42 us (6%)
    all_to_all x1, blocking collectives, body(): gathered = lax.all_to_all(gram, ('plane', 'planey'), 0, 0, tiled=True)  66.2 us
    ppermute x4, starting transfers between devices, swap(): return lax.ppermute(message, (axis, other) if other else axis, pairs)  13.8 us
    pallas_call x6, Pallas kernels, call(): pl.pallas_call(kernel, in_specs=specs, out_specs=[VMEM] * len(outs), out_...  5.42 us
    all_gather x1, blocking collectives, body(): summed = lax.all_gather(local_sum, 'ens').sum(axis=0)  4.53 us
  transfers between devices with their start and end apart: 4, of which 1 were waited for; matrix products, arithmetic and copies ran while one was open for 0% of the time, Pallas kernels for 3%

profile of v8, /device:TPU:65, one launch (start us, length us, event | category | flops | bytes accessed | tf_op | source)
XLA Modules:
  0.0 91.6 jit_solution(7478883114636775671)
XLA Ops:
  0.0 1.1 %pack_rows.1 = (f32[11,2,8,128]{3,2,1,0:T(8,128)S(1)}, f32[11,2,8,128]{3,2,1,0:T(8,128)S(1)}, f32[4,16,128]{2,1,0:T(8,128)S(1)}, f32[2,2,10,16,128]{4,3,2,1,0:T(8,128)S(1)}) custom-call(s32[1]{0:T(128)S(6)} %add.7.row_turn_ref, s32[2]{0:T(128)} %rows_hbm.1, f32[2,2,10,16,128]{4,3,2,1,0:T(8,128)} %u_hbm.1, f32[16,16,128]{2,1,0:T(8,128)} %table_hbm.1, ...), custom_call_target="tpu_custom_call" | custom-call | tf_op jit(solution)/shard_map/pack_rows/pallas_call | solution.py:447
  1.1 6.6 %collective-permute-start = (f32[11,2,8,128]{3,2,1,0:T(8,128)S(1)}, f32[11,2,8,128]{3,2,1,0:T(8,128)S(1)}, u32[]{:S(2)}, u32[]{:S(2)}) collective-permute-start(f32[11,2,8,128]{3,2,1,0:T(8,128)S(1)} %get-tuple-element.28), channel_id=1, source_target_pairs={{16,32},{32,16},{48,64},{64,48},{80,96},{96,80},{112,128},{128,112... | collective-permute-start | bytes 270344 | tf_op jit(solution)/shard_map/ppermute | solution.py:467
  7.7 0.7 collective-permute-start.1
  8.3 0.4 pack_strips.1
  8.8 0.8 collective-permute-done.by_odd_ref
  9.6 0.0 collective-permute-done.1.by_even_ref
  9.6 0.2 pack_columns.1
  9.8 0.7 collective-permute-start.2
  10.5 5.9 %collective-permute-start.3 = (f32[2,24,128]{2,1,0:T(8,128)S(1)}, f32[2,24,128]{2,1,0:T(8,128)S(1)}, u32[]{:S(2)}, u32[]{:S(2)}) collective-permute-start(f32[2,24,128]{2,1,0:T(8,128)S(1)} %get-tuple-element.32), channel_id=1, source_target_pairs={{0,2},{2,0},{4,6},{6,4},{8,10},{10,8},{12,14},{14,12},{1,3},{3,1},... | collective-permute-start | bytes 73736 | tf_op jit(solution)/shard_map/ppermute | solution.py:467
  16.4 2.4 %main_part.1 = (f32[4,10,16,128]{3,2,1,0:T(8,128)S(1)}, f32[4,10,16,128]{3,2,1,0:T(8,128)S(1)}, f32[2,10,16,128]{3,2,1,0:T(8,128)S(1)}, f32[8,128]{1,0:T(8,128)S(1)}) custom-call(s32[1]{0:T(128)} %bitcast.refs_0_, f32[2,2,10,16,128]{4,3,2,1,0:T(8,128)S(1)} %get-tuple-element.23.u_ref.refs_1_, f32[4,16,128]{2,1,0:T(8,128)S(1)} %get-tuple-element.24.geo_ref.refs_2_, ...), custom_call_target="tpu_custom_call" | custom-call | tf_op jit(solution)/shard_map/main_part/pallas_call | solution.py:447
  18.8 0.0 collective-permute-done.2.refs_3_
  18.8 0.0 collective-permute-done.3.refs_4_
  18.8 1.0 %strip_part.1 = (f32[10,16,128]{2,1,0:T(8,128)S(1)}, f32[10,16,128]{2,1,0:T(8,128)S(1)}, f32[128,128]{1,0:T(8,128)S(1)}) custom-call(s32[1]{0:T(128)} %bitcast.refs_0_, s32[1]{0:T(128)} %bitcast.1.column_place_ref.refs_1_, f32[11,24,128]{2,1,0:T(8,128)S(1)} %get-tuple-element.30.refs_2_, f32[2,24,128]{2,1,0:T(8,128)S(1)} %collective-permute-done.2.refs_3_, ...), custom_call_target="tpu_custom_call" | custom-call | tf_op jit(solution)/shard_map/strip_part/pallas_call | solution.py:447
  19.7 66.2 %all_to_all.11 = f32[128,1,128]{2,1,0:T(1,128)S(1)} all-to-all(f32[128,1,128]{2,1,0:T(1,128)S(1)} %bitcast.9), channel_id=1, replica_groups=mesh['group'=2,'plane'=16,'planey'=8,'ens'=2] {'plane','planey'}, dimensions={0} | all-to-all | bytes 131072 | tf_op jit(solution)/shard_map/all_to_all | solution.py:545
  86.0 0.4 combine.1
  86.3 4.5 %all-gather = f32[4,10,16,128]{3,2,1,0:T(8,128)S(1)} all-gather(f32[2,10,16,128]{3,2,1,0:T(8,128)S(1)} %combine.1), channel_id=2, replica_groups=mesh['group'=2,'plane'=16,'planey'=8,'ens'=2] {'ens'}, dimensions={0}, use_global_device_ids=true | all-gather | bytes 491520 | tf_op jit(solution)/shard_map/all_gather | solution.py:551
  90.9 0.7 broadcast_multiply_fusion
  (1 shorter events, 0.0 us)
Async XLA Ops:
  1.1 8.5 %collective-permute-start = (f32[11,2,8,128]{3,2,1,0:T(8,128)S(1)}, f32[11,2,8,128]{3,2,1,0:T(8,128)S(1)}, u32[]{:S(2)}, u32[]{:S(2)}) collective-permute-start(f32[11,2,8,128]{3,2,1,0:T(8,128)S(1)} %get-tuple-element.28), channel_id=1, source_target_pairs={{16,32},{32,16},{48,64},{64,48},{80,96},{96,80},{112,128},{128,112... | collective-permute-start | bytes 270344 | tf_op jit(solution)/shard_map/ppermute | solution.py:467
  7.7 1.9 %collective-permute-start.1 = (f32[11,2,8,128]{3,2,1,0:T(8,128)S(1)}, f32[11,2,8,128]{3,2,1,0:T(8,128)S(1)}, u32[]{:S(2)}, u32[]{:S(2)}) collective-permute-start(f32[11,2,8,128]{3,2,1,0:T(8,128)S(1)} %get-tuple-element.29), channel_id=1, source_target_pairs={{0,16},{16,0},{32,48},{48,32},{64,80},{80,64},{96,112},{112,96},{1... | collective-permute-start | bytes 270344 | tf_op jit(solution)/shard_map/ppermute | solution.py:467
  9.8 9.0 %collective-permute-start.2 = (f32[2,24,128]{2,1,0:T(8,128)S(1)}, f32[2,24,128]{2,1,0:T(8,128)S(1)}, u32[]{:S(2)}, u32[]{:S(2)}) collective-permute-start(f32[2,24,128]{2,1,0:T(8,128)S(1)} %get-tuple-element.31), channel_id=1, source_target_pairs={{2,4},{4,2},{6,8},{8,6},{10,12},{12,10},{3,5},{5,3},{7,9},{9,7},{1... | collective-permute-start | bytes 73736 | tf_op jit(solution)/shard_map/ppermute | solution.py:467
  10.5 8.3 %collective-permute-start.3 = (f32[2,24,128]{2,1,0:T(8,128)S(1)}, f32[2,24,128]{2,1,0:T(8,128)S(1)}, u32[]{:S(2)}, u32[]{:S(2)}) collective-permute-start(f32[2,24,128]{2,1,0:T(8,128)S(1)} %get-tuple-element.32), channel_id=1, source_target_pairs={{0,2},{2,0},{4,6},{6,4},{8,10},{10,8},{12,14},{14,12},{1,3},{3,1},... | collective-permute-start | bytes 73736 | tf_op jit(solution)/shard_map/ppermute | solution.py:467

commit v9 on v7

--- a/solution.py
+++ b/solution.py
@@ -91,7 +91,7 @@
         yield group, jnp.where(swapped, right, left), jnp.where(swapped, left, right)
 
 
-def pack_strips(column_place_ref, u_ref, geo_ref, own_ref, odd_ref, even_ref):
+def pack_strips(column_turn_ref, u_ref, geo_ref, own_ref, odd_ref, even_ref):
     layers = u_ref.shape[2]
     for layer in range(layers + 1):
         for t in range(2):
@@ -99,7 +99,7 @@
             own_ref[layer, at] = strip_tile(
                 [u_ref[k % 2, k // 2, layer, at] if layer < layers else geo_ref[k, at] for k in range(4)]
             )
-    swapped = column_place_ref[0] % 2 == 1
+    swapped = column_turn_ref[0] % 2 == 1
 
     def send(t, carry):
         at = pl.ds(pl.multiple_of(8 * t, 8), 8)
@@ -112,7 +112,7 @@
 
 
 def pack_columns(
-    row_turn_ref, column_place_ref, own_ref, own_odd_ref, own_even_ref, by_odd_ref, by_even_ref,
+    row_turn_ref, column_turn_ref, own_ref, own_odd_ref, own_even_ref, by_odd_ref, by_even_ref,
     outer_ref, strip_ref, odd_ref, even_ref,
 ):
     layers = own_ref.shape[0] - 1
@@ -134,7 +134,7 @@
     for group in range(2):
         odd_ref[group, 0:16] = own_odd_ref[group]
         even_ref[group, 0:16] = own_even_ref[group]
-    swapped = column_place_ref[0] % 2 == 1
+    swapped = column_turn_ref[0] % 2 == 1
 
     for group, by_odd, by_even in side_messages(lambda layer: strip_ref[layer, 16:24], layers, swapped):
         odd_ref[group, 16:24] = by_odd
@@ -298,7 +298,7 @@
 
 
 def strip_part(
-    row_place_ref, column_place_ref, strip_ref, by_odd_ref, by_even_ref, table_ref,
+    row_place_ref, column_turn_ref, strip_ref, by_odd_ref, by_even_ref, table_ref,
     residual_ref, image_ref, gram_ref,
     wide_ref, roots_ref, scale_ref, field_ref, next_ref, second_ref, *, total_x,
 ):
@@ -311,7 +311,7 @@
     low = lane < 2 * STRIP
 
     geo = None
-    odd = column_place_ref[0] % 2 == 1
+    odd = column_turn_ref[0] % 2 == 1
     from_left = [jnp.where(odd, by_even_ref[g], by_odd_ref[g]) for g in range(2)]
     from_right = [jnp.where(odd, by_odd_ref[g], by_even_ref[g]) for g in range(2)]
     for layer in range(layers + 1):
@@ -473,7 +473,7 @@
     total_x = rows_x * lax.axis_size("plane")
     row_place = lax.axis_index("plane").reshape(1)
     row_turn = row_place + lax.axis_index("ens")
-    column_place = lax.axis_index("planey").reshape(1)
+    column_turn = (lax.axis_index("planey") + lax.axis_index("ens")).reshape(1)
     by_odd, by_even, geo, u_near = call(
         pack_rows,
         [
@@ -496,18 +496,18 @@
     own = call(
         pack_strips,
         [f32(layers + 1, rows_x, 128), f32(2, rows_x, 128), f32(2, rows_x, 128)],
-        [column_place, u_near, geo],
+        [column_turn, u_near, geo],
         "pack_strips",
         in_specs=[SMEM, VMEM, VMEM],
     )
     outer, strip, side_odd, side_even = call(
         pack_columns,
         [f32(layers + 1, 4, 8, rows_y), f32(layers + 1, 24, 128), f32(2, 24, 128), f32(2, 24, 128)],
-        [row_turn, column_place, *own, by_odd, by_even],
+        [row_turn, column_turn, *own, by_odd, by_even],
         "pack_columns",
         in_specs=[SMEM, SMEM] + [VMEM] * 5,
     )
-    side_odd, side_even = swap_sides(side_odd, side_even, "planey", None)
+    side_odd, side_even = swap_sides(side_odd, side_even, "planey")
     residual, image, start, table = call(
         lambda *refs: main_part(*refs, total_x=total_x),
         [
@@ -535,7 +535,7 @@
             f32(layers, rows_x, 128),
             f32(lax.axis_size("plane") * lax.axis_size("planey"), 128),
         ],
-        [row_place, column_place, strip, side_odd, side_even, table],
+        [row_place, column_turn, strip, side_odd, side_even, table],
         "strip_part",
         scratch=[pltpu.VMEM((layers, 24, 128), jnp.float32)] * 5
         + [pltpu.VMEM((layers, 16, 128), jnp.float32)],

time: 91.9 us -> 91.9 us (level)
  blocking collectives: 70.8 us -> 73.4 us
  starting transfers between devices: 13.8 us -> 11.2 us
    all_to_all x1, blocking collectives: 66.2 us -> 69.9 us  [body(): gathered = lax.all_to_all(gram, ('plane', 'planey'), 0, 0, tiled=True)]
    ppermute x4, starting transfers between devices: 13.8 us -> 11.2 us  [swap(): return lax.ppermute(message, (axis, other) if other else axis, pairs)]
    all_gather x1, blocking collectives: 4.53 us -> 3.48 us  [body(): summed = lax.all_gather(local_sum, 'ens').sum(axis=0)]
where the time goes in v9:
time: 91.9 us; the launch traced here: 91.6 us
  blocking collectives  73.4 us (80%)
  starting transfers between devices  11.2 us (12%)
  Pallas kernels  5.45 us (6%)
    all_to_all x1, blocking collectives, body(): gathered = lax.all_to_all(gram, ('plane', 'planey'), 0, 0, tiled=True)  69.9 us
    ppermute x4, starting transfers between devices, swap(): return lax.ppermute(message, (axis, other) if other else axis, pairs)  11.2 us
    pallas_call x6, Pallas kernels, call(): pl.pallas_call(kernel, in_specs=specs, out_specs=[VMEM] * len(outs), out_...  5.45 us
    all_gather x1, blocking collectives, body(): summed = lax.all_gather(local_sum, 'ens').sum(axis=0)  3.48 us
  transfers between devices with their start and end apart: 4, of which 1 were waited for; matrix products, arithmetic and copies ran while one was open for 0% of the time, Pallas kernels for 3%

profile of v9, /device:TPU:65, one launch (start us, length us, event | category | flops | bytes accessed | tf_op | source)
XLA Modules:
  0.0 91.6 jit_solution(4996926494330624596)
XLA Ops:
  0.0 1.1 %pack_rows.1 = (f32[11,2,8,128]{3,2,1,0:T(8,128)S(1)}, f32[11,2,8,128]{3,2,1,0:T(8,128)S(1)}, f32[4,16,128]{2,1,0:T(8,128)S(1)}, f32[2,2,10,16,128]{4,3,2,1,0:T(8,128)S(1)}) custom-call(s32[1]{0:T(128)S(6)} %add.11.row_turn_ref, s32[2]{0:T(128)} %rows_hbm.1, f32[2,2,10,16,128]{4,3,2,1,0:T(8,128)} %u_hbm.1, f32[16,16,128]{2,1,0:T(8,128)} %table_hbm.1, ...), custom_call_target="tpu_custom_call" | custom-call | tf_op jit(solution)/shard_map/pack_rows/pallas_call | solution.py:446
  1.1 6.6 %collective-permute-start = (f32[11,2,8,128]{3,2,1,0:T(8,128)S(1)}, f32[11,2,8,128]{3,2,1,0:T(8,128)S(1)}, u32[]{:S(2)}, u32[]{:S(2)}) collective-permute-start(f32[11,2,8,128]{3,2,1,0:T(8,128)S(1)} %get-tuple-element.28), channel_id=1, source_target_pairs={{16,32},{32,16},{48,64},{64,48},{80,96},{96,80},{112,128},{128,112... | collective-permute-start | bytes 270344 | tf_op jit(solution)/shard_map/ppermute | solution.py:466
  7.7 0.7 collective-permute-start.1
  8.3 0.4 pack_strips.1
  8.8 0.8 collective-permute-done.by_odd_ref
  9.6 0.0 collective-permute-done.1.by_even_ref
  9.6 0.2 pack_columns.1
  9.8 3.3 %collective-permute-start.2 = (f32[2,24,128]{2,1,0:T(8,128)S(1)}, f32[2,24,128]{2,1,0:T(8,128)S(1)}, u32[]{:S(2)}, u32[]{:S(2)}) collective-permute-start(f32[2,24,128]{2,1,0:T(8,128)S(1)} %get-tuple-element.31), channel_id=1, source_target_pairs={{2,4},{4,2},{6,8},{8,6},{10,12},{12,10},{1,3},{3,1},{5,7},{7,5},{9... | collective-permute-start | bytes 73736 | tf_op jit(solution)/shard_map/ppermute | solution.py:466
  13.1 0.7 collective-permute-start.3
  13.8 2.4 %main_part.1 = (f32[4,10,16,128]{3,2,1,0:T(8,128)S(1)}, f32[4,10,16,128]{3,2,1,0:T(8,128)S(1)}, f32[2,10,16,128]{3,2,1,0:T(8,128)S(1)}, f32[8,128]{1,0:T(8,128)S(1)}) custom-call(s32[1]{0:T(128)} %bitcast.refs_0_, f32[2,2,10,16,128]{4,3,2,1,0:T(8,128)S(1)} %get-tuple-element.23.u_ref.refs_1_, f32[4,16,128]{2,1,0:T(8,128)S(1)} %get-tuple-element.24.geo_ref.refs_2_, ...), custom_call_target="tpu_custom_call" | custom-call | tf_op jit(solution)/shard_map/main_part/pallas_call | solution.py:446
  16.1 0.0 collective-permute-done.2.refs_3_
  16.2 0.0 collective-permute-done.3.refs_4_
  16.2 1.0 %strip_part.1 = (f32[10,16,128]{2,1,0:T(8,128)S(1)}, f32[10,16,128]{2,1,0:T(8,128)S(1)}, f32[128,128]{1,0:T(8,128)S(1)}) custom-call(s32[1]{0:T(128)} %bitcast.refs_0_, s32[1]{0:T(128)} %bitcast.1.column_turn_ref.refs_1_, f32[11,24,128]{2,1,0:T(8,128)S(1)} %get-tuple-element.30.refs_2_, f32[2,24,128]{2,1,0:T(8,128)S(1)} %collective-permute-done.2.refs_3_, ...), custom_call_target="tpu_custom_call" | custom-call | tf_op jit(solution)/shard_map/strip_part/pallas_call | solution.py:446
  17.1 69.9 %all_to_all.11 = f32[128,1,128]{2,1,0:T(1,128)S(1)} all-to-all(f32[128,1,128]{2,1,0:T(1,128)S(1)} %bitcast.9), channel_id=1, replica_groups=mesh['group'=2,'plane'=16,'planey'=8,'ens'=2] {'plane','planey'}, dimensions={0} | all-to-all | bytes 131072 | tf_op jit(solution)/shard_map/all_to_all | solution.py:544
  87.1 0.4 combine.1
  87.4 3.5 %all-gather = f32[4,10,16,128]{3,2,1,0:T(8,128)S(1)} all-gather(f32[2,10,16,128]{3,2,1,0:T(8,128)S(1)} %combine.1), channel_id=2, replica_groups=mesh['group'=2,'plane'=16,'planey'=8,'ens'=2] {'ens'}, dimensions={0}, use_global_device_ids=true | all-gather | bytes 491520 | tf_op jit(solution)/shard_map/all_gather | solution.py:550
  90.9 0.7 broadcast_multiply_fusion
  (1 shorter events, 0.0 us)
Async XLA Ops:
  1.1 8.5 %collective-permute-start = (f32[11,2,8,128]{3,2,1,0:T(8,128)S(1)}, f32[11,2,8,128]{3,2,1,0:T(8,128)S(1)}, u32[]{:S(2)}, u32[]{:S(2)}) collective-permute-start(f32[11,2,8,128]{3,2,1,0:T(8,128)S(1)} %get-tuple-element.28), channel_id=1, source_target_pairs={{16,32},{32,16},{48,64},{64,48},{80,96},{96,80},{112,128},{128,112... | collective-permute-start | bytes 270344 | tf_op jit(solution)/shard_map/ppermute | solution.py:466
  7.7 1.9 %collective-permute-start.1 = (f32[11,2,8,128]{3,2,1,0:T(8,128)S(1)}, f32[11,2,8,128]{3,2,1,0:T(8,128)S(1)}, u32[]{:S(2)}, u32[]{:S(2)}) collective-permute-start(f32[11,2,8,128]{3,2,1,0:T(8,128)S(1)} %get-tuple-element.29), channel_id=1, source_target_pairs={{0,16},{16,0},{32,48},{48,32},{64,80},{80,64},{96,112},{112,96},{1... | collective-permute-start | bytes 270344 | tf_op jit(solution)/shard_map/ppermute | solution.py:466
  9.8 6.3 %collective-permute-start.2 = (f32[2,24,128]{2,1,0:T(8,128)S(1)}, f32[2,24,128]{2,1,0:T(8,128)S(1)}, u32[]{:S(2)}, u32[]{:S(2)}) collective-permute-start(f32[2,24,128]{2,1,0:T(8,128)S(1)} %get-tuple-element.31), channel_id=1, source_target_pairs={{2,4},{4,2},{6,8},{8,6},{10,12},{12,10},{1,3},{3,1},{5,7},{7,5},{9... | collective-permute-start | bytes 73736 | tf_op jit(solution)/shard_map/ppermute | solution.py:466
  13.1 3.1 %collective-permute-start.3 = (f32[2,24,128]{2,1,0:T(8,128)S(1)}, f32[2,24,128]{2,1,0:T(8,128)S(1)}, u32[]{:S(2)}, u32[]{:S(2)}) collective-permute-start(f32[2,24,128]{2,1,0:T(8,128)S(1)} %get-tuple-element.32), channel_id=1, source_target_pairs={{0,2},{2,0},{4,6},{6,4},{8,10},{10,8},{12,14},{14,12},{3,5},{5,3},... | collective-permute-start | bytes 73736 | tf_op jit(solution)/shard_map/ppermute | solution.py:466

commit v10 on v8

--- a/solution.py
+++ b/solution.py
@@ -93,7 +93,7 @@
         yield group, jnp.where(swapped, right, left), jnp.where(swapped, left, right)
 
 
-def pack_strips(column_place_ref, u_ref, geo_ref, own_ref, odd_ref, even_ref):
+def pack_strips(column_turn_ref, u_ref, geo_ref, own_ref, odd_ref, even_ref):
     layers = u_ref.shape[2]
     for layer in range(layers + 1):
         for t in range(2):
@@ -101,7 +101,7 @@
             own_ref[layer, at] = strip_tile(
                 [u_ref[k % 2, k // 2, layer, at] if layer < layers else geo_ref[k, at] for k in range(4)]
             )
-    swapped = column_place_ref[0] % 2 == 1
+    swapped = column_turn_ref[0] % 2 == 1
 
     def send(t, carry):
         at = pl.ds(pl.multiple_of(8 * t, 8), 8)
@@ -114,7 +114,7 @@
 
 
 def pack_columns(
-    row_turn_ref, column_place_ref, own_ref, own_odd_ref, own_even_ref, by_odd_ref, by_even_ref,
+    row_turn_ref, column_turn_ref, own_ref, own_odd_ref, own_even_ref, by_odd_ref, by_even_ref,
     outer_ref, strip_ref, odd_ref, even_ref,
 ):
     layers = own_ref.shape[0] - 1
@@ -136,7 +136,7 @@
     for group in range(2):
         odd_ref[group, 0:16] = own_odd_ref[group]
         even_ref[group, 0:16] = own_even_ref[group]
-    swapped = column_place_ref[0] % 2 == 1
+    swapped = column_turn_ref[0] % 2 == 1
 
     for group, by_odd, by_even in side_messages(lambda layer: strip_ref[layer, 16:24], layers, swapped):
         odd_ref[group, 16:24] = by_odd
@@ -300,7 +300,7 @@
 
 
 def strip_part(
-    row_place_ref, column_place_ref, strip_ref, by_odd_ref, by_even_ref, table_ref,
+    row_place_ref, column_turn_ref, strip_ref, by_odd_ref, by_even_ref, table_ref,
     residual_ref, image_ref, gram_ref,
     wide_ref, roots_ref, scale_ref, field_ref, next_ref, second_ref, *, total_x,
 ):
@@ -313,7 +313,7 @@
     low = lane < SECOND
 
     geo = None
-    odd = column_place_ref[0] % 2 == 1
+    odd = column_turn_ref[0] % 2 == 1
     from_left = [jnp.where(odd, by_even_ref[g], by_odd_ref[g]) for g in range(2)]
     from_right = [jnp.where(odd, by_odd_ref[g], by_even_ref[g]) for g in range(2)]
     for layer in range(layers + 1):
@@ -474,7 +474,7 @@
     total_x = rows_x * lax.axis_size("plane")
     row_place = lax.axis_index("plane").reshape(1)
     row_turn = row_place + lax.axis_index("ens")
-    column_place = lax.axis_index("planey").reshape(1)
+    column_turn = (lax.axis_index("planey") + lax.axis_index("ens")).reshape(1)
     by_odd, by_even, geo, u_near = call(
         pack_rows,
         [
@@ -497,18 +497,18 @@
     own = call(
         pack_strips,
         [f32(layers + 1, rows_x, 128), f32(2, rows_x, 128), f32(2, rows_x, 128)],
-        [column_place, u_near, geo],
+        [column_turn, u_near, geo],
         "pack_strips",
         in_specs=[SMEM, VMEM, VMEM],
     )
     outer, strip, side_odd, side_even = call(
         pack_columns,
         [f32(layers + 1, 4, 8, rows_y), f32(layers + 1, 24, 128), f32(2, 24, 128), f32(2, 24, 128)],
-        [row_turn, column_place, *own, by_odd, by_even],
+        [row_turn, column_turn, *own, by_odd, by_even],
         "pack_columns",
         in_specs=[SMEM, SMEM] + [VMEM] * 5,
     )
-    side_odd, side_even = swap_sides(side_odd, side_even, "planey", None)
+    side_odd, side_even = swap_sides(side_odd, side_even, "planey")
     residual, image, start, table = call(
         lambda *refs: main_part(*refs, total_x=total_x),
         [
@@ -536,7 +536,7 @@
             f32(layers, rows_x, 128),
             f32(lax.axis_size("plane") * lax.axis_size("planey"), 128),
         ],
-        [row_place, column_place, strip, side_odd, side_even, table],
+        [row_place, column_turn, strip, side_odd, side_even, table],
         "strip_part",
         scratch=[pltpu.VMEM((layers, 24, 128), jnp.float32)] * 5
         + [pltpu.VMEM((layers, 16, 128), jnp.float32)],

time: 91.8 us -> 91.9 us (level)
  blocking collectives: 70.8 us -> 73.4 us
  starting transfers between devices: 13.8 us -> 11.2 us
    all_to_all x1, blocking collectives: 66.2 us -> 69.9 us  [body(): gathered = lax.all_to_all(gram, ('plane', 'planey'), 0, 0, tiled=True)]
    ppermute x4, starting transfers between devices: 13.8 us -> 11.2 us  [swap(): return lax.ppermute(message, (axis, other) if other else axis, pairs)]
    all_gather x1, blocking collectives: 4.53 us -> 3.48 us  [body(): summed = lax.all_gather(local_sum, 'ens').sum(axis=0)]
where the time goes in v10:
time: 91.9 us; the launch traced here: 91.6 us
  blocking collectives  73.4 us (80%)
  starting transfers between devices  11.2 us (12%)
  Pallas kernels  5.42 us (6%)
    all_to_all x1, blocking collectives, body(): gathered = lax.all_to_all(gram, ('plane', 'planey'), 0, 0, tiled=True)  69.9 us
    ppermute x4, starting transfers between devices, swap(): return lax.ppermute(message, (axis, other) if other else axis, pairs)  11.2 us
    pallas_call x6, Pallas kernels, call(): pl.pallas_call(kernel, in_specs=specs, out_specs=[VMEM] * len(outs), out_...  5.42 us
    all_gather x1, blocking collectives, body(): summed = lax.all_gather(local_sum, 'ens').sum(axis=0)  3.48 us
  transfers between devices with their start and end apart: 4, of which 1 were waited for; matrix products, arithmetic and copies ran while one was open for 0% of the time, Pallas kernels for 3%

profile of v10, /device:TPU:65, one launch (start us, length us, event | category | flops | bytes accessed | tf_op | source)
XLA Modules:
  0.0 91.6 jit_solution(6577361187419801543)
XLA Ops:
  0.0 1.1 %pack_rows.1 = (f32[11,2,8,128]{3,2,1,0:T(8,128)S(1)}, f32[11,2,8,128]{3,2,1,0:T(8,128)S(1)}, f32[4,16,128]{2,1,0:T(8,128)S(1)}, f32[2,2,10,16,128]{4,3,2,1,0:T(8,128)S(1)}) custom-call(s32[1]{0:T(128)S(6)} %add.11.row_turn_ref, s32[2]{0:T(128)} %rows_hbm.1, f32[2,2,10,16,128]{4,3,2,1,0:T(8,128)} %u_hbm.1, f32[16,16,128]{2,1,0:T(8,128)} %table_hbm.1, ...), custom_call_target="tpu_custom_call" | custom-call | tf_op jit(solution)/shard_map/pack_rows/pallas_call | solution.py:447
  1.1 6.6 %collective-permute-start = (f32[11,2,8,128]{3,2,1,0:T(8,128)S(1)}, f32[11,2,8,128]{3,2,1,0:T(8,128)S(1)}, u32[]{:S(2)}, u32[]{:S(2)}) collective-permute-start(f32[11,2,8,128]{3,2,1,0:T(8,128)S(1)} %get-tuple-element.28), channel_id=1, source_target_pairs={{16,32},{32,16},{48,64},{64,48},{80,96},{96,80},{112,128},{128,112... | collective-permute-start | bytes 270344 | tf_op jit(solution)/shard_map/ppermute | solution.py:467
  7.7 0.7 collective-permute-start.1
  8.3 0.4 pack_strips.1
  8.8 0.8 collective-permute-done.by_odd_ref
  9.6 0.0 collective-permute-done.1.by_even_ref
  9.6 0.2 pack_columns.1
  9.8 3.3 %collective-permute-start.2 = (f32[2,24,128]{2,1,0:T(8,128)S(1)}, f32[2,24,128]{2,1,0:T(8,128)S(1)}, u32[]{:S(2)}, u32[]{:S(2)}) collective-permute-start(f32[2,24,128]{2,1,0:T(8,128)S(1)} %get-tuple-element.31), channel_id=1, source_target_pairs={{2,4},{4,2},{6,8},{8,6},{10,12},{12,10},{1,3},{3,1},{5,7},{7,5},{9... | collective-permute-start | bytes 73736 | tf_op jit(solution)/shard_map/ppermute | solution.py:467
  13.1 0.7 collective-permute-start.3
  13.8 2.4 %main_part.1 = (f32[4,10,16,128]{3,2,1,0:T(8,128)S(1)}, f32[4,10,16,128]{3,2,1,0:T(8,128)S(1)}, f32[2,10,16,128]{3,2,1,0:T(8,128)S(1)}, f32[8,128]{1,0:T(8,128)S(1)}) custom-call(s32[1]{0:T(128)} %bitcast.refs_0_, f32[2,2,10,16,128]{4,3,2,1,0:T(8,128)S(1)} %get-tuple-element.23.u_ref.refs_1_, f32[4,16,128]{2,1,0:T(8,128)S(1)} %get-tuple-element.24.geo_ref.refs_2_, ...), custom_call_target="tpu_custom_call" | custom-call | tf_op jit(solution)/shard_map/main_part/pallas_call | solution.py:447
  16.1 0.0 collective-permute-done.2.refs_3_
  16.2 0.0 collective-permute-done.3.refs_4_
  16.2 1.0 %strip_part.1 = (f32[10,16,128]{2,1,0:T(8,128)S(1)}, f32[10,16,128]{2,1,0:T(8,128)S(1)}, f32[128,128]{1,0:T(8,128)S(1)}) custom-call(s32[1]{0:T(128)} %bitcast.refs_0_, s32[1]{0:T(128)} %bitcast.1.column_turn_ref.refs_1_, f32[11,24,128]{2,1,0:T(8,128)S(1)} %get-tuple-element.30.refs_2_, f32[2,24,128]{2,1,0:T(8,128)S(1)} %collective-permute-done.2.refs_3_, ...), custom_call_target="tpu_custom_call" | custom-call | tf_op jit(solution)/shard_map/strip_part/pallas_call | solution.py:447
  17.1 69.9 %all_to_all.11 = f32[128,1,128]{2,1,0:T(1,128)S(1)} all-to-all(f32[128,1,128]{2,1,0:T(1,128)S(1)} %bitcast.9), channel_id=1, replica_groups=mesh['group'=2,'plane'=16,'planey'=8,'ens'=2] {'plane','planey'}, dimensions={0} | all-to-all | bytes 131072 | tf_op jit(solution)/shard_map/all_to_all | solution.py:545
  87.0 0.4 combine.1
  87.4 3.5 %all-gather = f32[4,10,16,128]{3,2,1,0:T(8,128)S(1)} all-gather(f32[2,10,16,128]{3,2,1,0:T(8,128)S(1)} %combine.1), channel_id=2, replica_groups=mesh['group'=2,'plane'=16,'planey'=8,'ens'=2] {'ens'}, dimensions={0}, use_global_device_ids=true | all-gather | bytes 491520 | tf_op jit(solution)/shard_map/all_gather | solution.py:551
  90.9 0.7 broadcast_multiply_fusion
  (1 shorter events, 0.0 us)
Async XLA Ops:
  1.1 8.5 %collective-permute-start = (f32[11,2,8,128]{3,2,1,0:T(8,128)S(1)}, f32[11,2,8,128]{3,2,1,0:T(8,128)S(1)}, u32[]{:S(2)}, u32[]{:S(2)}) collective-permute-start(f32[11,2,8,128]{3,2,1,0:T(8,128)S(1)} %get-tuple-element.28), channel_id=1, source_target_pairs={{16,32},{32,16},{48,64},{64,48},{80,96},{96,80},{112,128},{128,112... | collective-permute-start | bytes 270344 | tf_op jit(solution)/shard_map/ppermute | solution.py:467
  7.7 1.9 %collective-permute-start.1 = (f32[11,2,8,128]{3,2,1,0:T(8,128)S(1)}, f32[11,2,8,128]{3,2,1,0:T(8,128)S(1)}, u32[]{:S(2)}, u32[]{:S(2)}) collective-permute-start(f32[11,2,8,128]{3,2,1,0:T(8,128)S(1)} %get-tuple-element.29), channel_id=1, source_target_pairs={{0,16},{16,0},{32,48},{48,32},{64,80},{80,64},{96,112},{112,96},{1... | collective-permute-start | bytes 270344 | tf_op jit(solution)/shard_map/ppermute | solution.py:467
  9.8 6.3 %collective-permute-start.2 = (f32[2,24,128]{2,1,0:T(8,128)S(1)}, f32[2,24,128]{2,1,0:T(8,128)S(1)}, u32[]{:S(2)}, u32[]{:S(2)}) collective-permute-start(f32[2,24,128]{2,1,0:T(8,128)S(1)} %get-tuple-element.31), channel_id=1, source_target_pairs={{2,4},{4,2},{6,8},{8,6},{10,12},{12,10},{1,3},{3,1},{5,7},{7,5},{9... | collective-permute-start | bytes 73736 | tf_op jit(solution)/shard_map/ppermute | solution.py:467
  13.1 3.1 %collective-permute-start.3 = (f32[2,24,128]{2,1,0:T(8,128)S(1)}, f32[2,24,128]{2,1,0:T(8,128)S(1)}, u32[]{:S(2)}, u32[]{:S(2)}) collective-permute-start(f32[2,24,128]{2,1,0:T(8,128)S(1)} %get-tuple-element.32), channel_id=1, source_target_pairs={{0,2},{2,0},{4,6},{6,4},{8,10},{10,8},{12,14},{14,12},{3,5},{5,3},... | collective-permute-start | bytes 73736 | tf_op jit(solution)/shard_map/ppermute | solution.py:467
